TPU v7x, 768 devices: a whole 4x8x12 slice. The times are simulated.
768 devices in a mesh: gx: 4 (over y_lo, core), gy: 16 (over x, y_hi), gz: 12 (over z).
Axes of the slice: x: 4, y: 8 (y_hi: 4, y_lo: 2; y = y_hi * 2 + y_lo), z: 12, core: 2. Of those that a mesh axis runs over, the one named last changes fastest.
Arguments:
- velocity: float32 [3, 32, 256, 1536], P(None, 'gx', 'gy', 'gz'), may hold values from -6 to 6
- diffusion: float32 [3], replicated, may hold values from 0.5 to 4
Outputs:
- viscous_velocity: float32 [3, 32, 256, 1536], P(None, 'gx', 'gy', 'gz')
- residual: float32 [3, 32, 256, 1536], P(None, 'gx', 'gy', 'gz')
All inputs are finite; a program needn't handle non-finite values.
Results may differ from a plain program's by a relative error of at most 0.0003.
Values sent between devices are 32-bit elements; how exact they have to be, the bound alone decides.
No kernel may reach another device: no remote copies, remote signals or barrier semaphores. Data moves between devices by JAX's collectives and lax.ppermute only.
A program may use at most 32 MiB of HBM per device.

v0:
```python
import jax
import jax.numpy as jnp
from jax import lax
from jax.sharding import Mesh
from jax.sharding import PartitionSpec as P

ITERS = 3
GX_GY_GZ = ("gx_0", "gx_1", "gy_0", "gy_1", "gz")
GX = ("gx_0", "gx_1")
GY = ("gy_0", "gy_1")


time_step = 0.25


def extended(value, sides, width):
    edges = {}
    for axis, dim in sides:
        size, length = (lax.axis_size(axis), value.shape[dim])
        up = [(i, (i + 1) % size) for i in range(size - 1)]
        last = lax.slice_in_dim(value, length - width, length, axis=dim)
        first = lax.slice_in_dim(value, 0, width, axis=dim)
        edges[dim] = (
            lax.ppermute(last, axis, up),
            lax.ppermute(first, axis, [(b, a) for a, b in up]),
        )
    done = []
    for _, dim in sides:
        low, high = edges[dim]
        around = [(width, width) if d in done else (0, 0) for d in range(value.ndim)]
        value = jnp.concatenate([jnp.pad(low, around), value, jnp.pad(high, around)], axis=dim)
        done.append(dim)
    return value


def over_axes(value, axes):
    for axis in axes:
        value = lax.psum(value, axis)
    return value


def with_halo(value, sides, width):
    for axis, dim in sides:
        size, length = (lax.axis_size(axis), value.shape[dim])
        up = [(i, (i + 1) % size) for i in range(size - 1)]
        down = [(j, i) for i, j in up]
        last = lax.slice_in_dim(value, length - width, length, axis=dim)
        first = lax.slice_in_dim(value, 0, width, axis=dim)
        before = lax.ppermute(last, axis, up)
        after = lax.ppermute(first, axis, down)
        value = jnp.concatenate([before, value, after], axis=dim)
    return value


def trimmed(array, axis, offset):
    index = [slice(None)] + [slice(1, -1)] * 3
    index[axis + 1] = slice(1 + offset, array.shape[axis + 1] - 1 + offset)
    return array[tuple(index)]


def advection(padded):
    total = None
    for axis in range(3):
        flux = padded[axis : axis + 1] * padded
        term = (trimmed(flux, axis, 1) - trimmed(flux, axis, -1)) * 0.5
        total = term if total is None else total + term
    return total


def apply_padded(padded, field, coefficient):
    beside = padded[:, 2:, 1:-1, 1:-1] + padded[:, :-2, 1:-1, 1:-1]
    beside = beside + padded[:, 1:-1, 2:, 1:-1] + padded[:, 1:-1, :-2, 1:-1]
    beside = beside + padded[:, 1:-1, 1:-1, 2:] + padded[:, 1:-1, 1:-1, :-2]
    return (1.0 + 6.0 * coefficient) * field - coefficient * beside


def operate(field, coefficient):
    padded = extended(field, ((GX, 1), (GY, 2), ("gz", 3)), 1)
    return apply_padded(padded, field, coefficient)


def products(residual, image):
    sums = (
        over_axes(jnp.sum(residual * residual, axis=(1, 2, 3)), GX_GY_GZ),
        over_axes(jnp.sum(residual * image, axis=(1, 2, 3)), GX_GY_GZ),
    )
    return (sums[0][:, None, None, None], sums[1][:, None, None, None])


def valid_cells(block_index, block_total, count, margin):
    position = block_index * count - margin + jnp.arange(count + 2 * margin)
    return ((position >= 0) & (position < count * block_total)).astype(jnp.float32)


def inside_mask(velocity, margin):
    mask_x = valid_cells(lax.axis_index(GX), lax.axis_size(GX), velocity.shape[1], margin)
    mask_y = valid_cells(lax.axis_index(GY), lax.axis_size(GY), velocity.shape[2], margin)
    mask_z = valid_cells(lax.axis_index("gz"), lax.axis_size("gz"), velocity.shape[3], margin)
    return (mask_x[:, None, None] * mask_y[None, :, None] * mask_z[None, None, :])[None]


def identity_cut(field):
    return field


def body(velocity, diffusion):
    coefficient = diffusion[:, None, None, None]

    def apply_next(field):
        return operate(field, coefficient)

    cut = identity_cut
    margin = ITERS
    deep = with_halo(velocity, ((GX, 1), (GY, 2), ("gz", 3)), margin + 1)
    inside = inside_mask(velocity, margin)
    section = (deep[:, 1:-1, 1:-1, 1:-1] - time_step * advection(deep)) * inside

    def apply_next(field):
        padded = jnp.pad(field, ((0, 0), (1, 1), (1, 1), (1, 1)))
        return apply_padded(padded, field, coefficient) * inside

    def cut(field):
        return field[:, margin:-margin, margin:-margin, margin:-margin]

    first_image = apply_next(section)
    solution = jnp.zeros_like(section)
    residual = section
    image = first_image
    norm_now, curvature = products(cut(residual), cut(image))
    step_size = norm_now / curvature
    direction = residual
    along = image
    for iteration in range(ITERS):
        solution = solution + step_size * direction
        residual = residual - step_size * along
        if iteration + 1 < ITERS:
            image = apply_next(residual)
            norm_next, curvature = products(cut(residual), cut(image))
            dir_ratio = norm_next / norm_now
            step_size = norm_next / (curvature - dir_ratio * norm_next / step_size)
            direction = residual + dir_ratio * direction
            along = image + dir_ratio * along
            norm_now = norm_next
    return (cut(solution), cut(residual))


def solution(mesh):
    finer = Mesh(
        mesh.devices.reshape(2, 2, 4, 4, mesh.shape["gz"]), ("gx_0", "gx_1", "gy_0", "gy_1", "gz")
    )
    return jax.shard_map(
        body,
        mesh=finer,
        in_specs=(P(None, GX, GY, "gz"), P()),
        out_specs=(P(None, GX, GY, "gz"), P(None, GX, GY, "gz")),
        check_vma=False,
    )
```

profile of v0, /device:TPU:8, one launch (start us, length us, event | category | flops | bytes accessed | tf_op | source)
XLA Modules:
  0.0 214.0 jit_solution(8170348838469068077)
XLA Ops:
  0.6 1.0 fusion.37
  1.6 1.9 collective-permute-start
  3.5 3.6 %collective-permute-start.1 = (f32[3,4,16,128]{3,2,1,0:T(8,128)S(1)}, f32[3,4,16,128]{3,2,1,0:T(8,128)S(1)}, u32[]{:S(2)}, u32[]{:S(2)}) collective-permute-start(f32[3,4,16,128]{3,2,1,0:T(8,128)S(1)} %get-tuple-element.59), channel_id=1, source_target_pairs={{192,0},{384,192},{576,384},{193,1},{385,193},{577,385},{194,2},{3... | collective-permute-start | bytes 294920 | tf_op jit(solution)/shard_map/ppermute | solution.py:50
  7.3 0.2 collective-permute-done
  7.5 0.9 constant_dynamic-update-slice_fusion.1
  8.5 0.9 collective-permute-done.1
  9.4 4.5 %collective-permute-start.2 = (f32[3,16,4,128]{3,1,2,0:T(8,128)S(1)}, f32[3,16,4,128]{3,1,2,0:T(8,128)S(1)}, u32[]{:S(2)}, u32[]{:S(2)}) collective-permute-start(f32[3,16,4,128]{3,1,2,0:T(8,128)S(1)} %copy.25), channel_id=1, source_target_pairs={{0,12},{12,24},{24,36},{36,48},{48,60},{60,72},{72,84},{84,96},{96... | collective-permute-start | bytes 294920 | tf_op jit(solution)/shard_map/ppermute | solution.py:49
  13.9 1.3 collective-permute-start.3
  15.4 2.3 %copy.20 = f32[3,16,16,128]{2,1,3,0:T(8,128)} copy(f32[3,16,16,128]{3,2,1,0:T(8,128)S(1)} %constant_dynamic-update-slice_fusion) | data formatting | bytes 786432 | tf_op jit(solution)/shard_map/concatenate | solution.py:51
  17.6 2.3 %copy.19 = f32[3,16,4,128]{2,1,3,0:T(8,128)} copy(f32[3,16,4,128]{3,1,2,0:T(8,128)S(1)} %collective-permute-done.2) | data formatting | bytes 196608 | tf_op jit(solution)/shard_map/ppermute | solution.py:49
  19.9 1.5 collective-permute-done.3
  21.4 2.2 %copy.21 = f32[3,16,4,128]{2,1,3,0:T(8,128)} copy(f32[3,16,4,128]{3,1,2,0:T(8,128)S(1)} %collective-permute-done.3) | data formatting | bytes 196608 | tf_op jit(solution)/shard_map/ppermute | solution.py:50
  23.6 5.4 %pad_maximum_fusion = f32[3,16,24,128]{2,1,3,0:T(8,128)S(1)} fusion(f32[3,16,4,128]{2,1,3,0:T(8,128)} %copy.21, f32[3,16,16,128]{2,1,3,0:T(8,128)} %copy.20, f32[3,16,4,128]{2,1,3,0:T(8,128)} %copy.19), kind=kLoop, calls=%fused_computation | loop fusion | flops 294912 | bytes 1179648 | tf_op jit(solution)/shard_map/concatenate | solution.py:51
  29.0 0.7 fusion.35
  29.7 5.0 %collective-permute-start.4 = (f32[3,16,24,4]{2,1,3,0:T(8,128)}, f32[3,16,24,4]{2,1,3,0:T(8,128)}, u32[]{:S(2)}, u32[]{:S(2)}) collective-permute-start(f32[3,16,24,4]{2,1,3,0:T(8,128)} %get-tuple-element.45), channel_id=1, source_target_pairs={{0,1},{1,2},{2,3},{3,4},{4,5},{5,6},{6,7},{7,8},{8,9},{9,10},{10,1... | collective-permute-start | bytes 55304 | tf_op jit(solution)/shard_map/ppermute | solution.py:49
  34.7 1.3 collective-permute-start.5
  36.0 1.8 copy.23
  37.9 1.3 copy.22
  39.2 2.4 %collective-permute-done.5 = f32[3,16,24,4]{2,1,3,0:T(8,128)} collective-permute-done((f32[3,16,24,4]{2,1,3,0:T(8,128)}, f32[3,16,24,4]{2,1,3,0:T(8,128)}, u32[]{:S(2)}, u32[]{:S(2)}) %collective-permute-start.5) | collective-permute-done | bytes 18464 | tf_op jit(solution)/shard_map/ppermute | solution.py:50
  41.5 1.2 copy.24
  42.8 0.5 pad_maximum_fusion.1
  43.4 0.3 broadcast_multiply_fusion.2
  43.7 1.7 fusion.27
  45.4 0.7 fusion.7
  46.1 0.3 fusion.33
  46.4 4.9 %all-reduce.17 = (f32[3]{0:T(128)S(1)}, f32[3]{0:T(128)S(1)}) all-reduce(f32[3]{0:T(128)S(1)} %get-tuple-element.9, f32[3]{0:T(128)S(1)} %get-tuple-element.8), channel_id=1, replica_groups=mesh['gx_0'=2,'gx_1'=2,'gy_0'=4,'gy_1'=4,'gz'=12] {'gx_0'}, use_global_device_ids=true, to_apply=%region_1.2 | all-reduce | flops 6 | bytes 48 | tf_op jit(solution)/shard_map/psum | solution.py:38
  51.3 2.5 %all-reduce.14 = (f32[3]{0:T(128)S(1)}, f32[3]{0:T(128)S(1)}) all-reduce(f32[3]{0:T(128)S(1)} %get-tuple-element.38, f32[3]{0:T(128)S(1)} %get-tuple-element.39), channel_id=1, replica_groups=mesh['gx_0'=2,'gx_1'=2,'gy_0'=4,'gy_1'=4,'gz'=12] {'gx_1'}, use_global_device_ids=true, to_apply=%region_2.3 | all-reduce | flops 6 | bytes 48 | tf_op jit(solution)/shard_map/psum | solution.py:38
  53.8 12.0 %all-reduce.11 = (f32[3]{0:T(128)S(1)}, f32[3]{0:T(128)S(1)}) all-reduce(f32[3]{0:T(128)S(1)} %get-tuple-element.32, f32[3]{0:T(128)S(1)} %get-tuple-element.33), channel_id=1, replica_groups=mesh['gx_0'=2,'gx_1'=2,'gy_0'=4,'gy_1'=4,'gz'=12] {'gy_0'}, use_global_device_ids=true, to_apply=%region_3.4 | all-reduce | flops 6 | bytes 48 | tf_op jit(solution)/shard_map/psum | solution.py:38
  65.7 11.2 %all-reduce.8 = (f32[3]{0:T(128)S(1)}, f32[3]{0:T(128)S(1)}) all-reduce(f32[3]{0:T(128)S(1)} %get-tuple-element.26, f32[3]{0:T(128)S(1)} %get-tuple-element.27), channel_id=1, replica_groups=mesh['gx_0'=2,'gx_1'=2,'gy_0'=4,'gy_1'=4,'gz'=12] {'gy_1'}, use_global_device_ids=true, to_apply=%region_4.5 | all-reduce | flops 6 | bytes 48 | tf_op jit(solution)/shard_map/psum | solution.py:38
  77.0 31.2 %all-reduce.5 = (f32[3]{0:T(128)S(1)}, f32[3]{0:T(128)S(1)}) all-reduce(f32[3]{0:T(128)S(1)} %get-tuple-element.20, f32[3]{0:T(128)S(1)} %get-tuple-element.21), channel_id=1, replica_groups=mesh['gx_0'=2,'gx_1'=2,'gy_0'=4,'gy_1'=4,'gz'=12] {'gz'}, use_global_device_ids=true, to_apply=%region_5.6 | all-reduce | flops 6 | bytes 48 | tf_op jit(solution)/shard_map/psum | solution.py:38
  108.1 0.8 multiply_subtract_fusion.1
  108.9 0.7 fusion.15
  109.6 0.3 fusion.32
  109.9 4.9 %all-reduce.16 = (f32[3]{0:T(128)S(1)}, f32[3]{0:T(128)S(1)}) all-reduce(f32[3]{0:T(128)S(1)} %get-tuple-element.7, f32[3]{0:T(128)S(1)} %get-tuple-element.6), channel_id=1, replica_groups=mesh['gx_0'=2,'gx_1'=2,'gy_0'=4,'gy_1'=4,'gz'=12] {'gx_0'}, use_global_device_ids=true, to_apply=%region_13.14 | all-reduce | flops 6 | bytes 48 | tf_op jit(solution)/shard_map/psum | solution.py:38
  114.8 2.5 %all-reduce.13 = (f32[3]{0:T(128)S(1)}, f32[3]{0:T(128)S(1)}) all-reduce(f32[3]{0:T(128)S(1)} %get-tuple-element.36, f32[3]{0:T(128)S(1)} %get-tuple-element.37), channel_id=1, replica_groups=mesh['gx_0'=2,'gx_1'=2,'gy_0'=4,'gy_1'=4,'gz'=12] {'gx_1'}, use_global_device_ids=true, to_apply=%region_14.15 | all-reduce | flops 6 | bytes 48 | tf_op jit(solution)/shard_map/psum | solution.py:38
  117.3 7.7 %all-reduce.10 = (f32[3]{0:T(128)S(1)}, f32[3]{0:T(128)S(1)}) all-reduce(f32[3]{0:T(128)S(1)} %get-tuple-element.30, f32[3]{0:T(128)S(1)} %get-tuple-element.31), channel_id=1, replica_groups=mesh['gx_0'=2,'gx_1'=2,'gy_0'=4,'gy_1'=4,'gz'=12] {'gy_0'}, use_global_device_ids=true, to_apply=%region_15.16 | all-reduce | flops 6 | bytes 48 | tf_op jit(solution)/shard_map/psum | solution.py:38
  125.0 10.6 %all-reduce.7 = (f32[3]{0:T(128)S(1)}, f32[3]{0:T(128)S(1)}) all-reduce(f32[3]{0:T(128)S(1)} %get-tuple-element.24, f32[3]{0:T(128)S(1)} %get-tuple-element.25), channel_id=1, replica_groups=mesh['gx_0'=2,'gx_1'=2,'gy_0'=4,'gy_1'=4,'gz'=12] {'gy_1'}, use_global_device_ids=true, to_apply=%region_16.17 | all-reduce | flops 6 | bytes 48 | tf_op jit(solution)/shard_map/psum | solution.py:38
  135.6 20.8 %all-reduce.4 = (f32[3]{0:T(128)S(1)}, f32[3]{0:T(128)S(1)}) all-reduce(f32[3]{0:T(128)S(1)} %get-tuple-element.18, f32[3]{0:T(128)S(1)} %get-tuple-element.19), channel_id=1, replica_groups=mesh['gx_0'=2,'gx_1'=2,'gy_0'=4,'gy_1'=4,'gz'=12] {'gz'}, use_global_device_ids=true, to_apply=%region_17.18 | all-reduce | flops 6 | bytes 48 | tf_op jit(solution)/shard_map/psum | solution.py:38
  156.4 2.8 %multiply_add_fusion = (f32[3,14,22,134]{3,2,1,0:T(8,128)}, f32[3,14,22,134]{3,2,1,0:T(8,128)S(1)}) fusion(f32[3]{0:T(128)S(1)} %get-tuple-element.44, f32[3,14,22,134]{3,2,1,0:T(8,128)S(1)} %multiply_subtract_fusion.1, f32[3]{0:T(128)S(1)} %get-tuple-element.42, f32[14,22,134]{2,1,0:T(8,128)S(1)} %broadcast_multiply_fusion.3, f32[3]{0:T(128)S(1)} %copy-done.2, ...), kind=kLoop, calls=%fused_computation.53 | loop fusion | flops 2723952 | bytes 2146192 | tf_op jit(solution)/shard_map/add | solution.py:142
  159.2 0.7 fusion.23
  160.0 1.0 copy-done.1
  161.0 0.3 multiply_reduce_fusion
  161.2 4.9 %all-reduce.15 = (f32[3]{0:T(128)S(1)}, f32[3]{0:T(128)S(1)}) all-reduce(f32[3]{0:T(128)S(1)} %get-tuple-element.5, f32[3]{0:T(128)S(1)} %get-tuple-element.4), channel_id=1, replica_groups=mesh['gx_0'=2,'gx_1'=2,'gy_0'=4,'gy_1'=4,'gz'=12] {'gx_0'}, use_global_device_ids=true, to_apply=%region_25.26 | all-reduce | flops 6 | bytes 48 | tf_op jit(solution)/shard_map/psum | solution.py:38
  166.2 2.5 %all-reduce.12 = (f32[3]{0:T(128)S(1)}, f32[3]{0:T(128)S(1)}) all-reduce(f32[3]{0:T(128)S(1)} %get-tuple-element.34, f32[3]{0:T(128)S(1)} %get-tuple-element.35), channel_id=1, replica_groups=mesh['gx_0'=2,'gx_1'=2,'gy_0'=4,'gy_1'=4,'gz'=12] {'gx_1'}, use_global_device_ids=true, to_apply=%region_26.27 | all-reduce | flops 6 | bytes 48 | tf_op jit(solution)/shard_map/psum | solution.py:38
  168.6 9.7 %all-reduce.9 = (f32[3]{0:T(128)S(1)}, f32[3]{0:T(128)S(1)}) all-reduce(f32[3]{0:T(128)S(1)} %get-tuple-element.28, f32[3]{0:T(128)S(1)} %get-tuple-element.29), channel_id=1, replica_groups=mesh['gx_0'=2,'gx_1'=2,'gy_0'=4,'gy_1'=4,'gz'=12] {'gy_0'}, use_global_device_ids=true, to_apply=%region_27.28 | all-reduce | flops 6 | bytes 48 | tf_op jit(solution)/shard_map/psum | solution.py:38
  178.3 10.7 %all-reduce.6 = (f32[3]{0:T(128)S(1)}, f32[3]{0:T(128)S(1)}) all-reduce(f32[3]{0:T(128)S(1)} %get-tuple-element.22, f32[3]{0:T(128)S(1)} %get-tuple-element.23), channel_id=1, replica_groups=mesh['gx_0'=2,'gx_1'=2,'gy_0'=4,'gy_1'=4,'gz'=12] {'gy_1'}, use_global_device_ids=true, to_apply=%region_28.29 | all-reduce | flops 6 | bytes 48 | tf_op jit(solution)/shard_map/psum | solution.py:38
  189.1 22.6 %all-reduce.3 = (f32[3]{0:T(128)S(1)}, f32[3]{0:T(128)S(1)}) all-reduce(f32[3]{0:T(128)S(1)} %get-tuple-element.16, f32[3]{0:T(128)S(1)} %get-tuple-element.17), channel_id=1, replica_groups=mesh['gx_0'=2,'gx_1'=2,'gy_0'=4,'gy_1'=4,'gz'=12] {'gz'}, use_global_device_ids=true, to_apply=%region_29.30 | all-reduce | flops 6 | bytes 48 | tf_op jit(solution)/shard_map/psum | solution.py:38
  211.7 2.3 %fusion.31 = (f32[3,8,16,128]{3,2,1,0:T(8,128)}, f32[3,8,16,128]{3,2,1,0:T(8,128)}) fusion(f32[3,14,22,134]{3,2,1,0:T(8,128)} %get-tuple-element.47, f32[3,14,22,134]{3,2,1,0:T(8,128)} %copy-done.1, f32[3,14,22,134]{3,2,1,0:T(8,128)S(1)} %get-tuple-element.48, f32[3]{0:T(128)S(1)} %get-tuple-element.40, f32[3]{0:T(128)S(1)} %get-tuple-element.41, ...), kind=kLoop, calls=%fused_computation.64 | loop fusion | flops 638976 | bytes 1376316 | tf_op jit(solution)/shard_map/sub | solution.py:135
  (22 shorter events, 0.4 us)
Async XLA Ops:
  1.6 5.9 %collective-permute-start = (f32[3,4,16,128]{3,2,1,0:T(8,128)S(1)}, f32[3,4,16,128]{3,2,1,0:T(8,128)S(1)}, u32[]{:S(2)}, u32[]{:S(2)}) collective-permute-start(f32[3,4,16,128]{3,2,1,0:T(8,128)S(1)} %get-tuple-element.60), channel_id=1, source_target_pairs={{0,192},{192,384},{384,576},{1,193},{193,385},{385,577},{2,194},{1... | collective-permute-start | bytes 294920 | tf_op jit(solution)/shard_map/ppermute | solution.py:49
  3.5 5.8 %collective-permute-start.1 = (f32[3,4,16,128]{3,2,1,0:T(8,128)S(1)}, f32[3,4,16,128]{3,2,1,0:T(8,128)S(1)}, u32[]{:S(2)}, u32[]{:S(2)}) collective-permute-start(f32[3,4,16,128]{3,2,1,0:T(8,128)S(1)} %get-tuple-element.59), channel_id=1, source_target_pairs={{192,0},{384,192},{576,384},{193,1},{385,193},{577,385},{194,2},{3... | collective-permute-start | bytes 294920 | tf_op jit(solution)/shard_map/ppermute | solution.py:50
  9.4 8.2 %collective-permute-start.2 = (f32[3,16,4,128]{3,1,2,0:T(8,128)S(1)}, f32[3,16,4,128]{3,1,2,0:T(8,128)S(1)}, u32[]{:S(2)}, u32[]{:S(2)}) collective-permute-start(f32[3,16,4,128]{3,1,2,0:T(8,128)S(1)} %copy.25), channel_id=1, source_target_pairs={{0,12},{12,24},{24,36},{36,48},{48,60},{60,72},{72,84},{84,96},{96... | collective-permute-start | bytes 294920 | tf_op jit(solution)/shard_map/ppermute | solution.py:49
  13.9 7.4 %collective-permute-start.3 = (f32[3,16,4,128]{3,1,2,0:T(8,128)S(1)}, f32[3,16,4,128]{3,1,2,0:T(8,128)S(1)}, u32[]{:S(2)}, u32[]{:S(2)}) collective-permute-start(f32[3,16,4,128]{3,1,2,0:T(8,128)S(1)} %copy.26), channel_id=1, source_target_pairs={{12,0},{24,12},{36,24},{48,36},{60,48},{72,60},{84,72},{96,84},{10... | collective-permute-start | bytes 294920 | tf_op jit(solution)/shard_map/ppermute | solution.py:50
  23.6 12.4 %copy-start.2 = (f32[3]{0:T(128)S(1)}, f32[3]{0:T(128)}, u32[]{:S(2)}) copy-start(f32[3]{0:T(128)} %param.3) | copy-start | bytes 40
  29.7 8.1 %collective-permute-start.4 = (f32[3,16,24,4]{2,1,3,0:T(8,128)}, f32[3,16,24,4]{2,1,3,0:T(8,128)}, u32[]{:S(2)}, u32[]{:S(2)}) collective-permute-start(f32[3,16,24,4]{2,1,3,0:T(8,128)} %get-tuple-element.45), channel_id=1, source_target_pairs={{0,1},{1,2},{2,3},{3,4},{4,5},{5,6},{6,7},{7,8},{8,9},{9,10},{10,1... | collective-permute-start | bytes 55304 | tf_op jit(solution)/shard_map/ppermute | solution.py:49
  34.7 6.8 %collective-permute-start.5 = (f32[3,16,24,4]{2,1,3,0:T(8,128)}, f32[3,16,24,4]{2,1,3,0:T(8,128)}, u32[]{:S(2)}, u32[]{:S(2)}) collective-permute-start(f32[3,16,24,4]{2,1,3,0:T(8,128)} %get-tuple-element.46), channel_id=1, source_target_pairs={{1,0},{2,1},{3,2},{4,3},{5,4},{6,5},{7,6},{8,7},{9,8},{10,9},{11,1... | collective-permute-start | bytes 55304 | tf_op jit(solution)/shard_map/ppermute | solution.py:50
  37.8 4.9 %copy-start = (f32[3,16,24,128]{3,2,1,0:T(8,128)S(1)}, f32[3,16,24,128]{3,2,1,0:T(8,128)}, u32[]{:S(2)}) copy-start(f32[3,16,24,128]{3,2,1,0:T(8,128)} %copy.23) | copy-start | bytes 1769476
  160.0 1.0 copy-start.1
where the time goes:
time: 215 us; the launch traced here: 214 us
  blocking collectives  159 us (74%)
  starting transfers between devices  17.6 us (8%)
  other arithmetic  17 us (8%)
  local copies, waits for them, and re-layouts  14.9 us (7%)
  waiting for transfers between devices  4.93 us (2%)
    psum x15, blocking collectives, over_axes(): value = lax.psum(value, axis)  159 us
    ppermute x3, starting transfers between devices, with_halo(): before = lax.ppermute(last, axis, up)  11.4 us
    ppermute x3, starting transfers between devices, with_halo(): after = lax.ppermute(first, axis, down)  6.21 us
    concatenate x2, other arithmetic, with_halo(): value = jnp.concatenate([before, value, after], axis=dim)  5.97 us
    ppermute x3, waiting for transfers between devices, with_halo(): after = lax.ppermute(first, axis, down)  4.7 us
  transfers between devices with their start and end apart: 6, of which 4 were waited for; matrix products, arithmetic and copies ran while one was open for 4% of the time, Pallas kernels for 0%

commit v1 on v0

--- a/solution.py
+++ b/solution.py
@@ -103,45 +103,68 @@
     return field
 
 
+def gathered_sum(value, axes):
+    count = lax.axis_size(axes)
+    spread = jnp.broadcast_to(value[None], (count,) + value.shape)
+    return jnp.sum(lax.all_to_all(spread, axes, 0, 0, tiled=True), axis=0)
+
+
+def weights_of(moments, coefficient):
+    scale = 6.0 * coefficient
+
+    def inner(first, second):
+        return sum(f * s * moments[i + j] for i, f in enumerate(first) for j, s in enumerate(second))
+
+    def plus(first, factor, second):
+        size = max(len(first), len(second))
+        padded = [list(v) + [0.0] * (size - len(v)) for v in (first, second)]
+        return [f + factor * s for f, s in zip(*padded)]
+
+    one = jnp.ones_like(coefficient)
+    total, residual, direction = [], [one], [one]
+    now = moments[0]
+    for iteration in range(ITERS):
+        image = plus(direction, scale, [0.0] + direction)
+        step = now / inner(direction, image)
+        total = plus(total, step, direction)
+        residual = plus(residual, -step, image)
+        if iteration + 1 < ITERS:
+            new = inner(residual, residual)
+            direction = plus(residual, new / now, direction)
+            now = new
+    return total, residual
+
+
+def laplace(field):
+    padded = jnp.pad(field, ((0, 0), (1, 1), (1, 1), (1, 1)))
+    beside = padded[:, 2:, 1:-1, 1:-1] + padded[:, :-2, 1:-1, 1:-1]
+    beside = beside + padded[:, 1:-1, 2:, 1:-1] + padded[:, 1:-1, :-2, 1:-1]
+    beside = beside + padded[:, 1:-1, 1:-1, 2:] + padded[:, 1:-1, 1:-1, :-2]
+    return field - beside * (1.0 / 6.0)
+
+
 def body(velocity, diffusion):
-    coefficient = diffusion[:, None, None, None]
-
-    def apply_next(field):
-        return operate(field, coefficient)
-
-    cut = identity_cut
     margin = ITERS
     deep = with_halo(velocity, ((GX, 1), (GY, 2), ("gz", 3)), margin + 1)
     inside = inside_mask(velocity, margin)
     section = (deep[:, 1:-1, 1:-1, 1:-1] - time_step * advection(deep)) * inside
 
-    def apply_next(field):
-        padded = jnp.pad(field, ((0, 0), (1, 1), (1, 1), (1, 1)))
-        return apply_padded(padded, field, coefficient) * inside
-
     def cut(field):
         return field[:, margin:-margin, margin:-margin, margin:-margin]
 
-    first_image = apply_next(section)
-    solution = jnp.zeros_like(section)
-    residual = section
-    image = first_image
-    norm_now, curvature = products(cut(residual), cut(image))
-    step_size = norm_now / curvature
-    direction = residual
-    along = image
-    for iteration in range(ITERS):
-        solution = solution + step_size * direction
-        residual = residual - step_size * along
-        if iteration + 1 < ITERS:
-            image = apply_next(residual)
-            norm_next, curvature = products(cut(residual), cut(image))
-            dir_ratio = norm_next / norm_now
-            step_size = norm_next / (curvature - dir_ratio * norm_next / step_size)
-            direction = residual + dir_ratio * direction
-            along = image + dir_ratio * along
-            norm_now = norm_next
-    return (cut(solution), cut(residual))
+    powers = [section]
+    for _ in range(ITERS):
+        powers.append(laplace(powers[-1]) * inside)
+    powers = [cut(p) for p in powers]
+    local = [jnp.sum(powers[k // 2] * powers[(k + 1) // 2], axis=(1, 2, 3)) for k in range(2 * ITERS)]
+    moments = gathered_sum(gathered_sum(jnp.concatenate(local), GX + GY), ("gz",))
+    moments = [moments[3 * k : 3 * k + 3] for k in range(2 * ITERS)]
+    total, rest = weights_of(moments, diffusion)
+    total, rest = ([w[:, None, None, None] for w in v] for v in (total, rest))
+    return (
+        sum(w * p for w, p in zip(total, powers)),
+        sum(w * p for w, p in zip(rest, powers)),
+    )
 
 
 def solution(mesh):

time: 215 us -> 93.7 us (0.44)
  the two profiles are of different devices: /device:TPU:8 before, /device:TPU:1 now
where the time goes in v1:
time: 93.7 us; the launch traced here: 93.3 us
  blocking collectives  41.9 us (45%)
  starting transfers between devices  21.1 us (23%)
  local copies, waits for them, and re-layouts  14.1 us (15%)
  other arithmetic  12.1 us (13%)
  waiting for transfers between devices  3.3 us (4%)
    all_to_all x2, blocking collectives, gathered_sum(): return jnp.sum(lax.all_to_all(spread, axes, 0, 0, tiled=True), axis=0)  41.9 us
    ppermute x3, starting transfers between devices, with_halo(): after = lax.ppermute(first, axis, down)  11.7 us
    ppermute x3, starting transfers between devices, with_halo(): before = lax.ppermute(last, axis, up)  9.38 us
    concatenate x2, other arithmetic, with_halo(): value = jnp.concatenate([before, value, after], axis=dim)  5.96 us
    concatenate x3, local copies, waits for them, and re-layouts, with_halo(): value = jnp.concatenate([before, value, after], axis=dim)  4.11 us
    ppermute x2, local copies, waits for them, and re-layouts, with_halo(): before = lax.ppermute(last, axis, up)  3.58 us
    ppermute x2, local copies, waits for them, and re-layouts, with_halo(): after = lax.ppermute(first, axis, down)  3.45 us
    ppermute x3, waiting for transfers between devices, with_halo(): after = lax.ppermute(first, axis, down)  3.29 us
  transfers between devices with their start and end apart: 6, of which 2 were waited for; matrix products, arithmetic and copies ran while one was open for 10% of the time, Pallas kernels for 0%

profile of v1, /device:TPU:1, one launch (start us, length us, event | category | flops | bytes accessed | tf_op | source)
XLA Modules:
  0.0 93.3 jit_solution(8407992645319982451)
XLA Ops:
  0.6 1.0 %fusion.33 = (f32[3,4,16,128]{3,2,1,0:T(8,128)S(1)}, f32[3,4,16,128]{3,2,1,0:T(8,128)S(1)}) fusion(f32[3,8,16,128]{3,2,1,0:T(8,128)} %param.2), kind=kLoop, calls=%fused_computation.105 | loop fusion | bytes 393216 | tf_op jit(solution)/shard_map/slice | solution.py:48
  1.6 4.6 %collective-permute-start = (f32[3,4,16,128]{3,2,1,0:T(8,128)S(1)}, f32[3,4,16,128]{3,2,1,0:T(8,128)S(1)}, u32[]{:S(2)}, u32[]{:S(2)}) collective-permute-start(f32[3,4,16,128]{3,2,1,0:T(8,128)S(1)} %get-tuple-element.42), channel_id=1, source_target_pairs={{0,192},{192,384},{384,576},{1,193},{193,385},{385,577},{2,194},{1... | collective-permute-start | bytes 294920 | tf_op jit(solution)/shard_map/ppermute | solution.py:49
  6.2 9.1 %collective-permute-start.1 = (f32[3,4,16,128]{3,2,1,0:T(8,128)S(1)}, f32[3,4,16,128]{3,2,1,0:T(8,128)S(1)}, u32[]{:S(2)}, u32[]{:S(2)}) collective-permute-start(f32[3,4,16,128]{3,2,1,0:T(8,128)S(1)} %get-tuple-element.41), channel_id=1, source_target_pairs={{192,0},{384,192},{576,384},{193,1},{385,193},{577,385},{194,2},{3... | collective-permute-start | bytes 294920 | tf_op jit(solution)/shard_map/ppermute | solution.py:50
  15.3 0.1 broadcast_multiply_fusion.4
  15.4 0.0 collective-permute-done
  15.4 0.9 %constant_dynamic-update-slice_fusion.1 = f32[3,16,16,128]{3,2,1,0:T(8,128)S(1)} fusion(f32[3,16,16,128]{3,2,1,0:T(8,128)S(1)} %constant_dynamic-update-slice_fusion.2, f32[3,8,16,128]{3,2,1,0:T(8,128)} %param.2), kind=kLoop, calls=%fused_computation.68 | loop fusion | bytes 393216
  16.4 0.0 collective-permute-done.1
  16.5 1.3 %collective-permute-start.2 = (f32[3,16,4,128]{3,1,2,0:T(8,128)S(1)}, f32[3,16,4,128]{3,1,2,0:T(8,128)S(1)}, u32[]{:S(2)}, u32[]{:S(2)}) collective-permute-start(f32[3,16,4,128]{3,1,2,0:T(8,128)S(1)} %copy.44), channel_id=1, source_target_pairs={{0,12},{12,24},{24,36},{36,48},{48,60},{60,72},{72,84},{84,96},{96... | collective-permute-start | bytes 294920 | tf_op jit(solution)/shard_map/ppermute | solution.py:49
  17.8 1.3 %collective-permute-start.3 = (f32[3,16,4,128]{3,1,2,0:T(8,128)S(1)}, f32[3,16,4,128]{3,1,2,0:T(8,128)S(1)}, u32[]{:S(2)}, u32[]{:S(2)}) collective-permute-start(f32[3,16,4,128]{3,1,2,0:T(8,128)S(1)} %copy.45), channel_id=1, source_target_pairs={{12,0},{24,12},{36,24},{48,36},{60,48},{72,60},{84,72},{96,84},{10... | collective-permute-start | bytes 294920 | tf_op jit(solution)/shard_map/ppermute | solution.py:50
  19.1 2.3 %copy.37 = f32[3,16,16,128]{2,1,3,0:T(8,128)} copy(f32[3,16,16,128]{3,2,1,0:T(8,128)S(1)} %constant_dynamic-update-slice_fusion) | data formatting | bytes 786432 | tf_op jit(solution)/shard_map/concatenate | solution.py:51
  21.4 0.0 collective-permute-done.2
  21.4 2.3 %copy.36 = f32[3,16,4,128]{2,1,3,0:T(8,128)} copy(f32[3,16,4,128]{3,1,2,0:T(8,128)S(1)} %collective-permute-done.2) | data formatting | bytes 196608 | tf_op jit(solution)/shard_map/ppermute | solution.py:49
  23.6 1.5 %collective-permute-done.3 = f32[3,16,4,128]{3,1,2,0:T(8,128)S(1)} collective-permute-done((f32[3,16,4,128]{3,1,2,0:T(8,128)S(1)}, f32[3,16,4,128]{3,1,2,0:T(8,128)S(1)}, u32[]{:S(2)}, u32[]{:S(2)}) %collective-permute-start.3) | collective-permute-done | bytes 98336 | tf_op jit(solution)/shard_map/ppermute | solution.py:50
  25.1 2.2 %copy.38 = f32[3,16,4,128]{2,1,3,0:T(8,128)} copy(f32[3,16,4,128]{3,1,2,0:T(8,128)S(1)} %collective-permute-done.3) | data formatting | bytes 196608 | tf_op jit(solution)/shard_map/ppermute | solution.py:50
  27.3 5.4 %pad_maximum_fusion = f32[3,16,24,128]{2,1,3,0:T(8,128)S(1)} fusion(f32[3,16,4,128]{2,1,3,0:T(8,128)} %copy.38, f32[3,16,16,128]{2,1,3,0:T(8,128)} %copy.37, f32[3,16,4,128]{2,1,3,0:T(8,128)} %copy.36), kind=kLoop, calls=%fused_computation | loop fusion | flops 294912 | bytes 1179648 | tf_op jit(solution)/shard_map/concatenate | solution.py:51
  32.8 0.7 fusion.31
  33.5 3.5 %collective-permute-start.4 = (f32[3,16,24,4]{2,1,3,0:T(8,128)}, f32[3,16,24,4]{2,1,3,0:T(8,128)}, u32[]{:S(2)}, u32[]{:S(2)}) collective-permute-start(f32[3,16,24,4]{2,1,3,0:T(8,128)} %get-tuple-element.25), channel_id=1, source_target_pairs={{0,1},{1,2},{2,3},{3,4},{4,5},{5,6},{6,7},{7,8},{8,9},{9,10},{10,1... | collective-permute-start | bytes 55304 | tf_op jit(solution)/shard_map/ppermute | solution.py:49
  37.0 1.3 %collective-permute-start.5 = (f32[3,16,24,4]{2,1,3,0:T(8,128)}, f32[3,16,24,4]{2,1,3,0:T(8,128)}, u32[]{:S(2)}, u32[]{:S(2)}) collective-permute-start(f32[3,16,24,4]{2,1,3,0:T(8,128)} %get-tuple-element.26), channel_id=1, source_target_pairs={{1,0},{2,1},{3,2},{4,3},{5,4},{6,5},{7,6},{8,7},{9,8},{10,9},{11,1... | collective-permute-start | bytes 55304 | tf_op jit(solution)/shard_map/ppermute | solution.py:50
  38.3 0.1 broadcast_multiply_fusion.3
  38.4 0.1 slice.198
  38.5 1.8 %copy.40 = f32[3,16,24,128]{3,2,1,0:T(8,128)} copy(f32[3,16,24,128]{2,1,3,0:T(8,128)S(1)} %pad_maximum_fusion) | data formatting | bytes 1179648 | tf_op jit(solution)/shard_map/concatenate | solution.py:51
  40.3 0.0 copy-start
  40.3 0.0 collective-permute-done.4
  40.3 1.3 %copy.39 = f32[3,16,24,4]{3,2,1,0:T(8,128)S(1)} copy(f32[3,16,24,4]{2,1,3,0:T(8,128)} %collective-permute-done.4) | data formatting | bytes 36864 | tf_op jit(solution)/shard_map/ppermute | solution.py:49
  41.6 1.8 %collective-permute-done.5 = f32[3,16,24,4]{2,1,3,0:T(8,128)} collective-permute-done((f32[3,16,24,4]{2,1,3,0:T(8,128)}, f32[3,16,24,4]{2,1,3,0:T(8,128)}, u32[]{:S(2)}, u32[]{:S(2)}) %collective-permute-start.5) | collective-permute-done | bytes 18464 | tf_op jit(solution)/shard_map/ppermute | solution.py:50
  43.4 1.2 %copy.41 = f32[3,16,24,4]{3,2,1,0:T(8,128)S(1)} copy(f32[3,16,24,4]{2,1,3,0:T(8,128)} %collective-permute-done.5) | data formatting | bytes 36864 | tf_op jit(solution)/shard_map/ppermute | solution.py:50
  44.6 0.0 copy-done
  44.6 0.5 pad_maximum_fusion.1
  45.2 0.1 slice_bitcast_fusion.2
  45.3 0.3 broadcast_multiply_fusion.2
  45.6 1.7 %fusion.21 = f32[3,14,22,134]{3,2,1,0:T(8,128)S(1)} fusion(f32[3,16,24,136]{3,2,1,0:T(8,128)S(1)} %get-tuple-element.30, f32[3,16,24,136]{3,2,1,0:T(8,128)S(1)} %get-tuple-element.31, f32[3,16,24,136]{3,2,1,0:T(8,128)S(1)} %get-tuple-element.29, f32[3,16,24,136]{3,2,1,0:T(8,128)S(1)} %pad_maximum_fusion.1, f32[14,22,134]{2,1,0:T(8,128)S(1)} %broadcast_multiply_fusion.3), kind=kLoop, calls=%fused_computation.42 | loop fusion | flops 990528 | bytes 4127200 | tf_op jit(solution)/shard_map/mul | solution.py:150
  47.3 0.6 fusion.7
  47.9 0.6 fusion.15
  48.5 0.8 fusion.17
  49.3 0.0 copy-start.1
  49.3 0.6 multiply_reduce_fusion
  49.9 0.1 concatenate.15
  50.0 18.6 %all_to_all.12 = f32[64,1,18]{2,1,0:T(1,128)S(1)} all-to-all(f32[64,1,18]{2,1,0:T(1,128)S(1)} %broadcast_in_dim.4), channel_id=1, replica_groups=mesh['gx_0'=2,'gx_1'=2,'gy_0'=4,'gy_1'=4,'gz'=12] {'gx_0','gx_1','gy_0',..., dimensions={0} | all-to-all | bytes 9216 | tf_op jit(solution)/shard_map/all_to_all | solution.py:109
  68.6 0.1 reduce_sum.78
  68.7 23.3 %all_to_all.13 = f32[12,1,18]{2,1,0:T(1,128)S(1)} all-to-all(f32[12,1,18]{2,1,0:T(1,128)S(1)} %broadcast_in_dim.5), channel_id=1, replica_groups=mesh['gx_0'=2,'gx_1'=2,'gy_0'=4,'gy_1'=4,'gz'=12] {'gz'}, dimensions={0} | all-to-all | bytes 1728 | tf_op jit(solution)/shard_map/all_to_all | solution.py:109
  92.1 0.0 copy-done.1
  92.1 0.1 multiply_add_fusion.12
  92.2 0.1 multiply_add_fusion.4
  92.3 1.0 %multiply_add_fusion = (f32[3,8,16,128]{3,2,1,0:T(8,128)}, f32[3,8,16,128]{3,2,1,0:T(8,128)}) fusion(f32[3,8,16,128]{3,2,1,0:T(8,128)S(1)} %get-tuple-element.24, f32[3,14,22,134]{3,2,1,0:T(8,128)S(1)} %fusion.21, f32[3,14,22,134]{3,2,1,0:T(8,128)S(1)} %fusion.7, f32[3,14,22,134]{3,2,1,0:T(8,128)S(1)} %fusion.15, f32[3]{0:T(128)S(1)} %get-tuple-element.48, ...), kind=kLoop, calls=%fused_computation.58 | loop fusion | flops 589824 | bytes 1179732 | tf_op jit(solution)/shard_map/add | solution.py:166
  (12 shorter events, 0.2 us)
Async XLA Ops:
  1.6 13.8 %collective-permute-start = (f32[3,4,16,128]{3,2,1,0:T(8,128)S(1)}, f32[3,4,16,128]{3,2,1,0:T(8,128)S(1)}, u32[]{:S(2)}, u32[]{:S(2)}) collective-permute-start(f32[3,4,16,128]{3,2,1,0:T(8,128)S(1)} %get-tuple-element.42), channel_id=1, source_target_pairs={{0,192},{192,384},{384,576},{1,193},{193,385},{385,577},{2,194},{1... | collective-permute-start | bytes 294920 | tf_op jit(solution)/shard_map/ppermute | solution.py:49
  6.2 10.2 %collective-permute-start.1 = (f32[3,4,16,128]{3,2,1,0:T(8,128)S(1)}, f32[3,4,16,128]{3,2,1,0:T(8,128)S(1)}, u32[]{:S(2)}, u32[]{:S(2)}) collective-permute-start(f32[3,4,16,128]{3,2,1,0:T(8,128)S(1)} %get-tuple-element.41), channel_id=1, source_target_pairs={{192,0},{384,192},{576,384},{193,1},{385,193},{577,385},{194,2},{3... | collective-permute-start | bytes 294920 | tf_op jit(solution)/shard_map/ppermute | solution.py:50
  16.5 4.9 %collective-permute-start.2 = (f32[3,16,4,128]{3,1,2,0:T(8,128)S(1)}, f32[3,16,4,128]{3,1,2,0:T(8,128)S(1)}, u32[]{:S(2)}, u32[]{:S(2)}) collective-permute-start(f32[3,16,4,128]{3,1,2,0:T(8,128)S(1)} %copy.44), channel_id=1, source_target_pairs={{0,12},{12,24},{24,36},{36,48},{48,60},{60,72},{72,84},{84,96},{96... | collective-permute-start | bytes 294920 | tf_op jit(solution)/shard_map/ppermute | solution.py:49
  17.8 7.3 %collective-permute-start.3 = (f32[3,16,4,128]{3,1,2,0:T(8,128)S(1)}, f32[3,16,4,128]{3,1,2,0:T(8,128)S(1)}, u32[]{:S(2)}, u32[]{:S(2)}) collective-permute-start(f32[3,16,4,128]{3,1,2,0:T(8,128)S(1)} %copy.45), channel_id=1, source_target_pairs={{12,0},{24,12},{36,24},{48,36},{60,48},{72,60},{84,72},{96,84},{10... | collective-permute-start | bytes 294920 | tf_op jit(solution)/shard_map/ppermute | solution.py:50
  33.5 6.8 %collective-permute-start.4 = (f32[3,16,24,4]{2,1,3,0:T(8,128)}, f32[3,16,24,4]{2,1,3,0:T(8,128)}, u32[]{:S(2)}, u32[]{:S(2)}) collective-permute-start(f32[3,16,24,4]{2,1,3,0:T(8,128)} %get-tuple-element.25), channel_id=1, source_target_pairs={{0,1},{1,2},{2,3},{3,4},{4,5},{5,6},{6,7},{7,8},{8,9},{9,10},{10,1... | collective-permute-start | bytes 55304 | tf_op jit(solution)/shard_map/ppermute | solution.py:49
  37.0 6.4 %collective-permute-start.5 = (f32[3,16,24,4]{2,1,3,0:T(8,128)}, f32[3,16,24,4]{2,1,3,0:T(8,128)}, u32[]{:S(2)}, u32[]{:S(2)}) collective-permute-start(f32[3,16,24,4]{2,1,3,0:T(8,128)} %get-tuple-element.26), channel_id=1, source_target_pairs={{1,0},{2,1},{3,2},{4,3},{5,4},{6,5},{7,6},{8,7},{9,8},{10,9},{11,1... | collective-permute-start | bytes 55304 | tf_op jit(solution)/shard_map/ppermute | solution.py:50
  40.3 4.4 %copy-start = (f32[3,16,24,128]{3,2,1,0:T(8,128)S(1)}, f32[3,16,24,128]{3,2,1,0:T(8,128)}, u32[]{:S(2)}) copy-start(f32[3,16,24,128]{3,2,1,0:T(8,128)} %copy.40) | copy-start | bytes 1769476
  49.3 42.8 %copy-start.1 = (f32[3]{0:T(128)S(1)}, f32[3]{0:T(128)}, u32[]{:S(2)}) copy-start(f32[3]{0:T(128)} %param.3) | copy-start | bytes 40

commit v2 on v1

v2 whole, which is shorter than its diff:
```python
import functools

import jax
import jax.numpy as jnp
from jax import lax
from jax.experimental import pallas as pl
from jax.experimental.pallas import tpu as pltpu
from jax.sharding import Mesh
from jax.sharding import PartitionSpec as P

ITERS = 3
GX = ("gx_0", "gx_1")
GY = ("gy_0", "gy_1")
GZ = ("gz",)
HALO = ITERS + 1

time_step = 0.25

NX, NY, NZ = 8, 16, 128
EX, EY = NX + 2 * HALO, NY + 2 * HALO
GROUPS = 4
STEP = NZ // GROUPS
MOMENTS = 2 * ITERS


def lanes(shape):
    return lax.broadcasted_iota(jnp.int32, shape, len(shape) - 1)


def rows(shape):
    return lax.broadcasted_iota(jnp.int32, shape, len(shape) - 2)


def back(value, axis):
    return pltpu.roll(value, value.shape[axis] - 1, axis)


def ahead(value, axis):
    return pltpu.roll(value, 1, axis)


def turned(value, shift):
    shift = shift % value.shape[-1]
    return pltpu.roll(value, shift, value.ndim - 1) if shift else value


def pack_y(own, below, above, up, down):
    def plane(c, i, part):
        if i < NX:
            return own[c, i, part, :]
        return above[c, i - NX, part, :] if i < NX + HALO else below[c, i - NX - HALO, part, :]

    for c in range(3):
        for p in range(8):
            up[c, p, 4:8, :] = plane(c, p, slice(NY - HALO, NY))
            up[c, p, 0:4, :] = plane(c, p + 8, slice(NY - HALO, NY))
            down[c, p, 0:4, :] = plane(c, p, slice(0, HALO))
            down[c, p, 4:8, :] = plane(c, p + 8, slice(0, HALO))


def pack_z(own, below, above, low, high, whole, up, down):
    sub = rows((8, NZ))
    lane = lanes((8, NZ))
    for c in range(3):
        for t in range(3):
            ups = jnp.zeros((8, NZ), jnp.float32)
            downs = jnp.zeros((8, NZ), jnp.float32)
            for i in range(EX):
                if t < 2:
                    part = slice(8 * t, 8 * t + 8)
                    if i < NX:
                        tile = own[c, i, part, :]
                    elif i < NX + HALO:
                        tile = above[c, i - NX, part, :]
                    else:
                        tile = below[c, i - NX - HALO, part, :]
                elif i < 8:
                    tile = jnp.where(sub < 4, high[c, i], low[c, i])
                else:
                    tile = pltpu.roll(jnp.where(sub < 4, low[c, i - 8], high[c, i - 8]), 4, 0)
                whole[c, i, 8 * t : 8 * t + 8, :] = tile
                place = STEP * (i // 4) + 4 * (i % 4)
                here = (lane >= place) & (lane < place + 4)
                ups = jnp.where(here, turned(tile, place - (NZ - HALO)), ups)
                downs = jnp.where(here, turned(tile, place), downs)
            up[c, 8 * t : 8 * t + 8, :] = ups
            down[c, 8 * t : 8 * t + 8, :] = downs


def section_of(at, here, before, after):
    result = []
    for c in range(3):
        slope = after[c] - before[c]
        flux = at[1] * at[c]
        slope = slope + (back(flux, 0) - ahead(flux, 0))
        flux = at[2] * at[c]
        slope = slope + (back(flux, 1) - ahead(flux, 1))
        result.append((at[c] - (0.5 * time_step) * slope) * here)
    return result


def laplace_of(at, before, after):
    beside = (before + after) + (back(at, 0) + ahead(at, 0))
    beside = beside + (back(at, 1) + ahead(at, 1))
    return at - beside * (1.0 / 6.0)


def pairs():
    return [(k // 2, (k + 1) // 2) for k in range(MOMENTS)]


def inner_lanes(place, whole, powers, sums, edge, *work):
    at_x, last_x, at_y, last_y = (place[k] for k in range(4))
    row = rows((EY, NZ))
    keep = jnp.float32(1.0)
    below_y = jnp.where(at_y == 0, 0.0, keep)
    above_y = jnp.where(at_y == last_y, 0.0, keep)
    in_y = jnp.where(row < NY, 1.0, jnp.where(row < NY + HALO, above_y, below_y))
    below_x = in_y * jnp.where(at_x == 0, 0.0, keep)
    above_x = in_y * jnp.where(at_x == last_x, 0.0, keep)

    def inside(x):
        return below_x if x < 0 else (above_x if x >= NX else in_y)

    def plane(x):
        return [whole[c, x % EX] for c in range(3)]

    def products(value):
        return [value[0] * value[c] for c in range(3)]

    lane = lanes((8, NZ))
    for c in range(3):
        for p in range(GROUPS):
            for t in range(3):
                part = slice(8 * t, 8 * t + 8)
                tile = jnp.zeros((8, NZ), jnp.float32)
                for g in range(GROUPS):
                    source = whole[c, GROUPS * g + p, part, :]
                    first = STEP * g + 4
                    tile = jnp.where((lane >= first) & (lane < first + 8), turned(source, first), tile)
                    first = STEP * g + 16
                    tile = jnp.where((lane >= first) & (lane < first + 8), turned(source, first - 120), tile)
                edge[c, p, part, :] = tile

    for x in range(-ITERS, NX + ITERS):
        new = section_of(plane(x), inside(x), products(plane(x - 1)), products(plane(x + 1)))
        for c in range(3):
            work[0][c, x % EX] = new[c]
            if 0 <= x < NX:
                powers[0, c, x] = new[c][:NY]
    for k in range(1, ITERS + 1):
        reach = ITERS - k
        for x in range(-reach, NX + reach):
            for c in range(3):
                source = work[k - 1]
                new = laplace_of(source[c, x % EX], source[c, (x - 1) % EX], source[c, (x + 1) % EX])
                if k < ITERS:
                    new = new * inside(x)
                    work[k][c, x % EX] = new
                if 0 <= x < NX:
                    powers[k, c, x] = new[:NY]
    valid = (lane >= HALO) & (lane < NZ - HALO)
    for c in range(3):
        total = [jnp.zeros((8, NZ), jnp.float32) for _ in range(MOMENTS)]
        for x in range(NX):
            for t in range(2):
                v = [powers[k, c, x, 8 * t : 8 * t + 8, :] for k in range(ITERS + 1)]
                total = [s + v[a] * v[b] for s, (a, b) in zip(total, pairs())]
        for k in range(MOMENTS):
            sums[c, k] = jnp.where(valid, total[k], 0.0)


def edge_lanes(place, edge, low, high, sums, powers, moments, whole, *work):
    at_x, last_x, at_y, last_y, at_z, last_z = (place[k] for k in range(6))
    row = rows((EY, NZ))
    lane = lanes((EY, NZ))
    group, offset = lane // STEP, lane % STEP
    outside = (row >= NY + HALO) & (at_y == 0)
    outside |= (row >= NY) & (row < NY + HALO) & (at_y == last_y)
    outside |= (group == 3) & (at_x == 0)
    outside |= (group == 2) & (at_x == last_x)
    outside |= (offset < 4) & (at_z == 0)
    outside |= (offset >= 24) & (at_z == last_z)
    inside = jnp.where(outside, 0.0, 1.0)
    for c in range(3):
        for p in range(GROUPS):
            value = jnp.where(offset < 4, turned(low[c], -4 * p), edge[c, p])
            whole[c, p] = jnp.where((offset >= 24) & (offset < 28), turned(high[c], 24 - 4 * p), value)

    def beyond(read, p):
        return turned(read(0), -STEP) if p == GROUPS - 1 else read(p + 1)

    def behind(read, p):
        return turned(read(GROUPS - 1), STEP) if p == 0 else read(p - 1)

    for p in range(GROUPS):
        at = [whole[c, p] for c in range(3)]
        before, after = (
            [side(lambda q, c=c: whole[0, q] * whole[c, q], p) for c in range(3)] for side in (behind, beyond)
        )
        new = section_of(at, inside, before, after)
        for c in range(3):
            work[0][c, p] = new[c]
            powers[0, c, p] = new[c][:NY]
    for k in range(1, ITERS + 1):
        for p in range(GROUPS):
            for c in range(3):
                read = functools.partial(lambda c, q: work[k - 1][c, q], c)
                new = laplace_of(read(p), behind(read, p), beyond(read, p))
                if k < ITERS:
                    new = new * inside
                    work[k][c, p] = new
                powers[k, c, p] = new[:NY]
    lane = lanes((8, NZ))
    group, offset = lane // STEP, lane % STEP
    valid = (group < 2) & (((offset >= 4) & (offset < 8)) | ((offset >= 20) & (offset < 24)))
    for c in range(3):
        total = [jnp.zeros((8, NZ), jnp.float32) for _ in range(MOMENTS)]
        for p in range(GROUPS):
            for t in range(2):
                v = [powers[k, c, p, 8 * t : 8 * t + 8, :] for k in range(ITERS + 1)]
                total = [s + v[a] * v[b] for s, (a, b) in zip(total, pairs())]
        for k in range(MOMENTS):
            value = jnp.where(valid, total[k], 0.0) + sums[c, k]
            value = jnp.sum(jnp.sum(value, axis=0, keepdims=True), axis=1, keepdims=True)
            moments[3 * k + c : 3 * k + c + 1, :] = jnp.broadcast_to(value, (1, NZ))


def combine(weights, powers, edges, total, rest):
    lane = lanes((8, NZ))

    def mix(out, first, count, c, read):
        value = weights[first + c : first + c + 1, :] * read(0)
        for k in range(1, count):
            value = value + weights[first + 3 * k + c : first + 3 * k + c + 1, :] * read(k)
        return value

    for out, first, count in ((total, 0, ITERS), (rest, 3 * ITERS, ITERS + 1)):
        for c in range(3):
            for p in range(GROUPS):
                for t in range(2):
                    part = slice(8 * t, 8 * t + 8)
                    side = mix(out, first, count, c, lambda k: edges[k, c, p, part, :])
                    for g in range(2):
                        x = GROUPS * g + p
                        value = mix(out, first, count, c, lambda k: powers[k, c, x, part, :])
                        value = jnp.where(lane < HALO, turned(side, -(STEP * g + 4)), value)
                        value = jnp.where(lane >= NZ - HALO, turned(side, 104 - STEP * g), value)
                        out[c, x, part, :] = value


def kernel(body, outs, scratch=(), scalars=0):
    vmem = pl.BlockSpec(memory_space=pltpu.VMEM)
    smem = pl.BlockSpec(memory_space=pltpu.SMEM)

    def call(*args):
        return pl.pallas_call(
            body,
            in_specs=[smem] * scalars + [vmem] * (len(args) - scalars),
            out_specs=[vmem] * len(outs),
            out_shape=[jax.ShapeDtypeStruct(s, jnp.float32) for s in outs],
            scratch_shapes=[pltpu.VMEM(s, jnp.float32) for s in scratch],
            name=body.__name__,
        )(*args)

    return call


def exchanged(up, down, axis):
    size = lax.axis_size(axis)
    steps = [(i, i + 1) for i in range(size - 1)]
    return lax.ppermute(up, axis, steps), lax.ppermute(down, axis, [(b, a) for a, b in steps])


def gathered_sum(value, axes):
    count = lax.axis_size(axes)
    spread = jnp.broadcast_to(value[None], (count,) + value.shape)
    return jnp.sum(lax.all_to_all(spread, axes, 0, 0, tiled=True), axis=0)


def weights_of(moments, coefficient):
    scale = 6.0 * coefficient

    def inner(first, second):
        return sum(f * s * moments[i + j] for i, f in enumerate(first) for j, s in enumerate(second))

    def plus(first, factor, second):
        size = max(len(first), len(second))
        padded = [list(v) + [0.0] * (size - len(v)) for v in (first, second)]
        return [f + factor * s for f, s in zip(*padded)]

    one = jnp.ones_like(coefficient)
    total, residual, direction = [], [one], [one]
    now = moments[0]
    for iteration in range(ITERS):
        image = plus(direction, scale, [0.0] + direction)
        step = now / inner(direction, image)
        total = plus(total, step, direction)
        residual = plus(residual, -step, image)
        if iteration + 1 < ITERS:
            new = inner(residual, residual)
            direction = plus(residual, new / now, direction)
            now = new
    return total, residual


def body(velocity, diffusion):
    place = jnp.stack([f(a) - k for a in (GX, GY, GZ) for f, k in ((lax.axis_index, 0), (lax.axis_size, 1))])
    block = (3, NX, NY, NZ)
    below, above = exchanged(velocity[:, NX - HALO :], velocity[:, :HALO], GX)
    up, down = kernel(pack_y, [(3, 8, 8, NZ)] * 2)(velocity, below, above)
    low, high = exchanged(up, down, GY)
    wide = (3, EX, EY, NZ)
    tiles = (3, GROUPS, EY, NZ)
    whole, up, down = kernel(pack_z, [wide, (3, EY, NZ), (3, EY, NZ)])(velocity, below, above, low, high)
    low, high = exchanged(up, down, GZ)
    powers, sums, edge = kernel(
        inner_lanes, [(ITERS + 1,) + block, (3, MOMENTS, 8, NZ), tiles], [wide] * ITERS, 1
    )(place, whole)
    edges, moments = kernel(
        edge_lanes, [(ITERS + 1, 3, GROUPS, NY, NZ), (3 * MOMENTS, NZ)], [tiles] * (ITERS + 1), 1
    )(place, edge, low, high, sums)
    moments = gathered_sum(gathered_sum(moments[:, 0], GX + GY), GZ)
    moments = [moments[3 * k : 3 * k + 3] for k in range(MOMENTS)]
    total, rest = weights_of(moments, diffusion)
    weights = jnp.broadcast_to(jnp.concatenate(total + rest)[:, None], (3 * (2 * ITERS + 1), NZ))
    total, rest = kernel(combine, [block] * 2)(weights, powers, edges)
    return total, rest


def solution(mesh):
    finer = Mesh(
        mesh.devices.reshape(2, 2, 4, 4, mesh.shape["gz"]), ("gx_0", "gx_1", "gy_0", "gy_1", "gz")
    )
    return jax.shard_map(
        body,
        mesh=finer,
        in_specs=(P(None, GX, GY, "gz"), P()),
        out_specs=(P(None, GX, GY, "gz"), P(None, GX, GY, "gz")),
        check_vma=False,
    )
```

time: 93.7 us -> 90.3 us (0.964)
  Pallas kernels: 0 us -> 11.8 us
  other arithmetic: 12.1 us -> 0.34 us
  local copies, waits for them, and re-layouts: 14.1 us -> 5.77 us
  waiting for transfers between devices: 3.3 us -> 7.86 us
  blocking collectives: 41.9 us -> 43.8 us
  starting transfers between devices: 21.1 us -> 19.5 us
    pallas_call x0 -> x5, Pallas kernels: none -> 11.8 us  [call(): pl.pallas_call(body, in_specs=[smem] * scalars + [vmem] * (len(args) - sc...]
    ppermute x4 -> x0, local copies, waits for them, and re-layouts: 7.03 us -> none  [the longest x2 3.58 us: with_halo(): before = lax.ppermute(last, axis, up)]
    concatenate x2 -> x0, other arithmetic: 5.96 us -> none  [with_halo(): value = jnp.concatenate([before, value, after], axis=dim)]
    ppermute x6, waiting for transfers between devices: 3.3 us -> 7.86 us  [the longest x3 4.32 us: exchanged(): lax.ppermute(down, axis, [(b, a) for a, b in steps])]
    concatenate x4 -> x1, local copies, waits for them, and re-layouts: 4.19 us -> 0.08 us  [body(): jnp.concatenate(total + rest)[:, None]]
    mul x6 -> x1, other arithmetic: 3.4 us -> 0.09 us  [plus(): return [f + factor * s for f, s in zip(*padded)]]
    all_to_all x2, blocking collectives: 41.9 us -> 43.8 us  [gathered_sum(): return jnp.sum(lax.all_to_all(spread, axes, 0, 0, tiled=True), axis=0)]
    add x2 -> x0, other arithmetic: 1.78 us -> none  [the longest x1 0.99 us: body(): sum((w * p for w, p in zip(rest, powers)))]
  transfers between devices with their start and end apart: 6 -> 6, of which waited for: 2 -> 3; matrix products, arithmetic and copies ran while one was open for 10% -> 1% of each run, Pallas kernels for 0% -> 4%
where the time goes in v2:
time: 90.3 us; the launch traced here: 89.8 us
  blocking collectives  43.8 us (49%)
  starting transfers between devices  19.5 us (22%)
  Pallas kernels  11.8 us (13%)
  waiting for transfers between devices  7.86 us (9%)
  local copies, waits for them, and re-layouts  5.77 us (6%)
    all_to_all x2, blocking collectives, gathered_sum(): return jnp.sum(lax.all_to_all(spread, axes, 0, 0, tiled=True), axis=0)  43.8 us
    ppermute x3, starting transfers between devices, exchanged(): lax.ppermute(down, axis, [(b, a) for a, b in steps])  15 us
    pallas_call x5, Pallas kernels, call(): pl.pallas_call(body, in_specs=[smem] * scalars + [vmem] * (len(args) - sc...  11.8 us
    ppermute x3, starting transfers between devices, exchanged(): lax.ppermute(up, axis, steps)  4.48 us
    ppermute x3, waiting for transfers between devices, exchanged(): lax.ppermute(down, axis, [(b, a) for a, b in steps])  4.32 us
    ppermute x3, waiting for transfers between devices, exchanged(): lax.ppermute(up, axis, steps)  3.53 us
    unnamed x14, local copies, waits for them, and re-layouts  2.55 us
  transfers between devices with their start and end apart: 6, of which 3 were waited for; matrix products, arithmetic and copies ran while one was open for 1% of the time, Pallas kernels for 4%

profile of v2, /device:TPU:1, one launch (start us, length us, event | category | flops | bytes accessed | tf_op | source)
XLA Modules:
  0.0 89.8 jit_solution(10892436151369546522)
XLA Ops:
  0.6 1.0 %fusion.4 = (f32[3,4,16,128]{3,2,1,0:T(8,128)S(1)}, f32[3,4,16,128]{3,2,1,0:T(8,128)S(1)}) fusion(f32[3,8,16,128]{3,2,1,0:T(8,128)} %own.3), kind=kLoop, calls=%fused_computation.30 | loop fusion | bytes 393216 | tf_op jit(solution)/shard_map/slice | solution.py:310
  1.6 12.4 %collective-permute-start.1 = (f32[3,4,16,128]{3,2,1,0:T(8,128)S(1)}, f32[3,4,16,128]{3,2,1,0:T(8,128)S(1)}, u32[]{:S(2)}, u32[]{:S(2)}) collective-permute-start(f32[3,4,16,128]{3,2,1,0:T(8,128)S(1)} %get-tuple-element.36), channel_id=1, source_target_pairs={{192,0},{384,192},{576,384},{193,1},{385,193},{577,385},{194,2},{3... | collective-permute-start | bytes 294920 | tf_op jit(solution)/shard_map/ppermute | solution.py:272
  14.0 1.9 %collective-permute-start = (f32[3,4,16,128]{3,2,1,0:T(8,128)S(1)}, f32[3,4,16,128]{3,2,1,0:T(8,128)S(1)}, u32[]{:S(2)}, u32[]{:S(2)}) collective-permute-start(f32[3,4,16,128]{3,2,1,0:T(8,128)S(1)} %get-tuple-element.37), channel_id=1, source_target_pairs={{0,192},{192,384},{384,576},{1,193},{193,385},{385,577},{2,194},{1... | collective-permute-start | bytes 294920 | tf_op jit(solution)/shard_map/ppermute | solution.py:272
  15.9 0.0 collective-permute-done.1.above
  15.9 0.0 copy-start
  15.9 1.6 %collective-permute-done.below = f32[3,4,16,128]{3,2,1,0:T(8,128)S(1)} collective-permute-done((f32[3,4,16,128]{3,2,1,0:T(8,128)S(1)}, f32[3,4,16,128]{3,2,1,0:T(8,128)S(1)}, u32[]{:S(2)}, u32[]{:S(2)}) %collective-permute-start) | collective-permute-done | bytes 98336 | tf_op jit(solution)/shard_map/ppermute | solution.py:272
  17.5 0.0 copy-done
  17.5 0.0 copy-start.1
  17.5 0.6 copy-done.1
  18.2 1.7 %pack_y.1 = (f32[3,8,8,128]{3,2,1,0:T(8,128)}, f32[3,8,8,128]{3,2,1,0:T(8,128)}) custom-call(f32[3,8,16,128]{3,2,1,0:T(8,128)} %own.3, f32[3,4,16,128]{3,2,1,0:T(8,128)} %copy-done.1, f32[3,4,16,128]{3,2,1,0:T(8,128)} %copy-done), custom_call_target="tpu_custom_call" | custom-call | tf_op jit(solution)/shard_map/pack_y/pallas_call | solution.py:257
  19.9 1.3 %collective-permute-start.2 = (f32[3,8,8,128]{3,2,1,0:T(8,128)}, f32[3,8,8,128]{3,2,1,0:T(8,128)S(1)}, u32[]{:S(2)}, u32[]{:S(2)}) collective-permute-start(f32[3,8,8,128]{3,2,1,0:T(8,128)} %get-tuple-element.12), channel_id=1, source_target_pairs={{0,12},{12,24},{24,36},{36,48},{48,60},{60,72},{72,84},{84,96},{96... | collective-permute-start | bytes 294920 | tf_op jit(solution)/shard_map/ppermute | solution.py:272
  21.2 1.3 %collective-permute-start.3 = (f32[3,8,8,128]{3,2,1,0:T(8,128)}, f32[3,8,8,128]{3,2,1,0:T(8,128)S(1)}, u32[]{:S(2)}, u32[]{:S(2)}) collective-permute-start(f32[3,8,8,128]{3,2,1,0:T(8,128)} %get-tuple-element.13), channel_id=1, source_target_pairs={{12,0},{24,12},{36,24},{48,36},{60,48},{72,60},{84,72},{96,84},{10... | collective-permute-start | bytes 294920 | tf_op jit(solution)/shard_map/ppermute | solution.py:272
  22.5 1.9 %collective-permute-done.2.low = f32[3,8,8,128]{3,2,1,0:T(8,128)S(1)} collective-permute-done((f32[3,8,8,128]{3,2,1,0:T(8,128)}, f32[3,8,8,128]{3,2,1,0:T(8,128)S(1)}, u32[]{:S(2)}, u32[]{:S(2)}) %collective-permute-start.2) | collective-permute-done | bytes 98336 | tf_op jit(solution)/shard_map/ppermute | solution.py:272
  24.4 0.0 copy-start.2
  24.4 4.3 %collective-permute-done.3.high = f32[3,8,8,128]{3,2,1,0:T(8,128)S(1)} collective-permute-done((f32[3,8,8,128]{3,2,1,0:T(8,128)}, f32[3,8,8,128]{3,2,1,0:T(8,128)S(1)}, u32[]{:S(2)}, u32[]{:S(2)}) %collective-permute-start.3) | collective-permute-done | bytes 98336 | tf_op jit(solution)/shard_map/ppermute | solution.py:272
  28.8 0.0 copy-done.2
  28.8 0.0 copy-start.3
  28.8 0.6 copy-done.3
  29.4 2.2 %pack_z.1 = (f32[3,16,24,128]{3,2,1,0:T(8,128)}, f32[3,24,128]{2,1,0:T(8,128)}, f32[3,24,128]{2,1,0:T(8,128)}) custom-call(f32[3,8,16,128]{3,2,1,0:T(8,128)} %own.3, f32[3,4,16,128]{3,2,1,0:T(8,128)} %copy-done.1, f32[3,4,16,128]{3,2,1,0:T(8,128)} %copy-done, f32[3,8,8,128]{3,2,1,0:T(8,128)} %copy-done.2, f32[3,8,8,128]{3,2,1,0:T(8,128)} %copy-done.3), custom_call_target="tpu_custom_call" | custom-call | tf_op jit(solution)/shard_map/pack_z/pallas_call | solution.py:257
  31.6 1.3 %collective-permute-start.4 = (f32[3,24,128]{2,1,0:T(8,128)}, f32[3,24,128]{2,1,0:T(8,128)S(1)}, u32[]{:S(2)}, u32[]{:S(2)}) collective-permute-start(f32[3,24,128]{2,1,0:T(8,128)} %get-tuple-element.16), channel_id=1, source_target_pairs={{0,1},{1,2},{2,3},{3,4},{4,5},{5,6},{6,7},{7,8},{8,9},{9,10},{10,1... | collective-permute-start | bytes 110600 | tf_op jit(solution)/shard_map/ppermute | solution.py:272
  32.9 1.3 %collective-permute-start.5 = (f32[3,24,128]{2,1,0:T(8,128)}, f32[3,24,128]{2,1,0:T(8,128)S(1)}, u32[]{:S(2)}, u32[]{:S(2)}) collective-permute-start(f32[3,24,128]{2,1,0:T(8,128)} %get-tuple-element.17), channel_id=1, source_target_pairs={{1,0},{2,1},{3,2},{4,3},{5,4},{6,5},{7,6},{8,7},{9,8},{10,9},{11,1... | collective-permute-start | bytes 110600 | tf_op jit(solution)/shard_map/ppermute | solution.py:272
  34.2 0.7 stack.15.place
  34.9 3.2 %inner_lanes.1 = (f32[4,3,8,16,128]{4,3,2,1,0:T(8,128)}, f32[3,6,8,128]{3,2,1,0:T(8,128)}, f32[3,4,24,128]{3,2,1,0:T(8,128)}) custom-call(s32[6]{0:T(128)} %stack.15.place, f32[3,16,24,128]{3,2,1,0:T(8,128)} %get-tuple-element.14.whole), custom_call_target="tpu_custom_call" | custom-call | tf_op jit(solution)/shard_map/inner_lanes/pallas_call | solution.py:257
  38.1 0.0 collective-permute-done.4.low
  38.1 0.0 copy-start.4
  38.1 0.0 collective-permute-done.5.high
  38.1 0.0 copy-start.5
  38.1 0.6 copy-done.4
  38.7 0.0 copy-done.5
  38.7 2.5 %edge_lanes.1 = (f32[4,3,4,16,128]{4,3,2,1,0:T(8,128)}, f32[18,128]{1,0:T(8,128)}) custom-call(s32[6]{0:T(128)} %stack.15.place, f32[3,4,24,128]{3,2,1,0:T(8,128)} %get-tuple-element.15.edge, f32[3,24,128]{2,1,0:T(8,128)} %copy-done.4, f32[3,24,128]{2,1,0:T(8,128)} %copy-done.5, f32[3,6,8,128]{3,2,1,0:T(8,128)} %get-tuple-element.18.sums), custom_call_target="tpu_custom_call" | custom-call | tf_op jit(solution)/shard_map/edge_lanes/pallas_call | solution.py:257
  41.2 0.8 slice_reduce_fusion
  42.0 20.3 %all_to_all.12 = f32[64,1,18]{2,1,0:T(1,128)S(1)} all-to-all(f32[64,1,18]{2,1,0:T(1,128)S(1)} %broadcast_in_dim.9), channel_id=1, replica_groups=mesh['gx_0'=2,'gx_1'=2,'gy_0'=4,'gy_1'=4,'gz'=12] {'gx_0','gx_1','gy_0',..., dimensions={0} | all-to-all | bytes 9216 | tf_op jit(solution)/shard_map/all_to_all | solution.py:278
  62.3 0.1 reduce_sum.18
  62.4 23.6 %all_to_all.13 = f32[12,1,18]{2,1,0:T(1,128)S(1)} all-to-all(f32[12,1,18]{2,1,0:T(1,128)S(1)} %broadcast_in_dim.10), channel_id=1, replica_groups=mesh['gx_0'=2,'gx_1'=2,'gy_0'=4,'gy_1'=4,'gz'=12] {'gz'}, dimensions={0} | all-to-all | bytes 1728 | tf_op jit(solution)/shard_map/all_to_all | solution.py:278
  86.0 0.0 copy-start.6
  86.0 0.6 copy-done.6
  86.6 0.1 multiply_add_fusion.10
  86.7 0.1 multiply_multiply_fusion
  86.8 0.1 concatenate.3
  86.9 0.7 broadcast_in_dim.22.weights
  87.6 2.2 %combine.1 = (f32[3,8,16,128]{3,2,1,0:T(8,128)}, f32[3,8,16,128]{3,2,1,0:T(8,128)}) custom-call(f32[21,128]{1,0:T(8,128)} %broadcast_in_dim.22.weights, f32[4,3,8,16,128]{4,3,2,1,0:T(8,128)} %get-tuple-element.20.powers, f32[4,3,4,16,128]{4,3,2,1,0:T(8,128)} %get-tuple-element.21.edges), custom_call_target="tpu_custom_call" | custom-call | tf_op jit(solution)/shard_map/combine/pallas_call | solution.py:257
  (4 shorter events, 0.1 us)
Async XLA Ops:
  1.6 14.3 %collective-permute-start.1 = (f32[3,4,16,128]{3,2,1,0:T(8,128)S(1)}, f32[3,4,16,128]{3,2,1,0:T(8,128)S(1)}, u32[]{:S(2)}, u32[]{:S(2)}) collective-permute-start(f32[3,4,16,128]{3,2,1,0:T(8,128)S(1)} %get-tuple-element.36), channel_id=1, source_target_pairs={{192,0},{384,192},{576,384},{193,1},{385,193},{577,385},{194,2},{3... | collective-permute-start | bytes 294920 | tf_op jit(solution)/shard_map/ppermute | solution.py:272
  14.0 3.5 %collective-permute-start = (f32[3,4,16,128]{3,2,1,0:T(8,128)S(1)}, f32[3,4,16,128]{3,2,1,0:T(8,128)S(1)}, u32[]{:S(2)}, u32[]{:S(2)}) collective-permute-start(f32[3,4,16,128]{3,2,1,0:T(8,128)S(1)} %get-tuple-element.37), channel_id=1, source_target_pairs={{0,192},{192,384},{384,576},{1,193},{193,385},{385,577},{2,194},{1... | collective-permute-start | bytes 294920 | tf_op jit(solution)/shard_map/ppermute | solution.py:272
  15.9 1.6 %copy-start = (f32[3,4,16,128]{3,2,1,0:T(8,128)}, f32[3,4,16,128]{3,2,1,0:T(8,128)S(1)}, u32[]{:S(2)}) copy-start(f32[3,4,16,128]{3,2,1,0:T(8,128)S(1)} %collective-permute-done.1.above) | copy-start | bytes 294916
  17.5 0.6 copy-start.1
  19.9 4.5 %collective-permute-start.2 = (f32[3,8,8,128]{3,2,1,0:T(8,128)}, f32[3,8,8,128]{3,2,1,0:T(8,128)S(1)}, u32[]{:S(2)}, u32[]{:S(2)}) collective-permute-start(f32[3,8,8,128]{3,2,1,0:T(8,128)} %get-tuple-element.12), channel_id=1, source_target_pairs={{0,12},{12,24},{24,36},{36,48},{48,60},{60,72},{72,84},{84,96},{96... | collective-permute-start | bytes 294920 | tf_op jit(solution)/shard_map/ppermute | solution.py:272
  21.2 7.6 %collective-permute-start.3 = (f32[3,8,8,128]{3,2,1,0:T(8,128)}, f32[3,8,8,128]{3,2,1,0:T(8,128)S(1)}, u32[]{:S(2)}, u32[]{:S(2)}) collective-permute-start(f32[3,8,8,128]{3,2,1,0:T(8,128)} %get-tuple-element.13), channel_id=1, source_target_pairs={{12,0},{24,12},{36,24},{48,36},{60,48},{72,60},{84,72},{96,84},{10... | collective-permute-start | bytes 294920 | tf_op jit(solution)/shard_map/ppermute | solution.py:272
  24.4 4.3 %copy-start.2 = (f32[3,8,8,128]{3,2,1,0:T(8,128)}, f32[3,8,8,128]{3,2,1,0:T(8,128)S(1)}, u32[]{:S(2)}) copy-start(f32[3,8,8,128]{3,2,1,0:T(8,128)S(1)} %collective-permute-done.2.low) | copy-start | bytes 294916
  28.8 0.6 copy-start.3
  31.6 6.5 %collective-permute-start.4 = (f32[3,24,128]{2,1,0:T(8,128)}, f32[3,24,128]{2,1,0:T(8,128)S(1)}, u32[]{:S(2)}, u32[]{:S(2)}) collective-permute-start(f32[3,24,128]{2,1,0:T(8,128)} %get-tuple-element.16), channel_id=1, source_target_pairs={{0,1},{1,2},{2,3},{3,4},{4,5},{5,6},{6,7},{7,8},{8,9},{9,10},{10,1... | collective-permute-start | bytes 110600 | tf_op jit(solution)/shard_map/ppermute | solution.py:272
  32.9 5.2 %collective-permute-start.5 = (f32[3,24,128]{2,1,0:T(8,128)}, f32[3,24,128]{2,1,0:T(8,128)S(1)}, u32[]{:S(2)}, u32[]{:S(2)}) collective-permute-start(f32[3,24,128]{2,1,0:T(8,128)} %get-tuple-element.17), channel_id=1, source_target_pairs={{1,0},{2,1},{3,2},{4,3},{5,4},{6,5},{7,6},{8,7},{9,8},{10,9},{11,1... | collective-permute-start | bytes 110600 | tf_op jit(solution)/shard_map/ppermute | solution.py:272
  38.1 0.6 copy-start.4
  38.1 0.6 copy-start.5
  86.0 0.7 copy-start.6

commit v3 on v2

v3 whole, which is shorter than its diff:
```python
import functools

import jax
import jax.numpy as jnp
from jax import lax
from jax.experimental import pallas as pl
from jax.experimental.pallas import tpu as pltpu
from jax.sharding import Mesh
from jax.sharding import PartitionSpec as P

ITERS = 3
GX = ("gx_0", "gx_1")
GY = ("gy_0", "gy_1")
GZ = ("gz",)
HALO = ITERS + 1

time_step = 0.25

NX, NY, NZ = 8, 16, 128
EX, EY = NX + 2 * HALO, NY + 2 * HALO
GROUPS = 4
STEP = NZ // GROUPS
MOMENTS = 2 * ITERS


def lanes(shape):
    return lax.broadcasted_iota(jnp.int32, shape, len(shape) - 1)


def rows(shape):
    return lax.broadcasted_iota(jnp.int32, shape, len(shape) - 2)


def back(value, axis):
    return pltpu.roll(value, value.shape[axis] - 1, axis)


def ahead(value, axis):
    return pltpu.roll(value, 1, axis)


def turned(value, shift):
    shift = shift % value.shape[-1]
    return pltpu.roll(value, shift, value.ndim - 1) if shift else value


def pack_y(block, own, up, down):
    own[...] = block[...]
    for c in range(3):
        for q in range(4):
            up[c, q, 4:8, :] = block[c, q, NY - HALO : NY, :]
            up[c, q, 0:4, :] = block[c, q + 4, NY - HALO : NY, :]
            down[c, q, 0:4, :] = block[c, q, 0:HALO, :]
            down[c, q, 4:8, :] = block[c, q + 4, 0:HALO, :]


def beside_y(low, high, c, x):
    sub = rows((8, NZ))
    if x < 4:
        return jnp.where(sub < 4, high[c, x], low[c, x])
    return pltpu.roll(jnp.where(sub < 4, low[c, x - 4], high[c, x - 4]), 4, 0)


def pack_x(own, low, high, up, down):
    for c in range(3):
        for n in range(HALO):
            for t in range(2):
                up[c, 2 * n + t] = own[c, NX - HALO + n, 8 * t : 8 * t + 8, :]
                down[c, 2 * n + t] = own[c, n, 8 * t : 8 * t + 8, :]
        for n in range(HALO - 1):
            up[c, 8 + n] = beside_y(low, high, c, NX - HALO + 1 + n)
            down[c, 8 + n] = beside_y(low, high, c, n)


def pack_z(own, low, high, below, above, whole, up, down):
    lane = lanes((8, NZ))
    zero = jnp.zeros((8, NZ), jnp.float32)

    def tile_of(c, i, t):
        if i < NX:
            return own[c, i, 8 * t : 8 * t + 8, :] if t < 2 else beside_y(low, high, c, i)
        n = i - NX
        if n < HALO:
            return above[c, 2 * n + t] if t < 2 else (above[c, 8 + n] if n < HALO - 1 else zero)
        n -= HALO
        return below[c, 2 * n + t] if t < 2 else (below[c, 7 + n] if n > 0 else zero)

    for c in range(3):
        for t in range(3):
            ups, downs = zero, zero
            for i in range(EX):
                tile = tile_of(c, i, t)
                whole[c, i, 8 * t : 8 * t + 8, :] = tile
                place = STEP * (i // 4) + 4 * (i % 4)
                here = (lane >= place) & (lane < place + 4)
                ups = jnp.where(here, turned(tile, place - (NZ - HALO)), ups)
                downs = jnp.where(here, turned(tile, place), downs)
            up[c, 8 * t : 8 * t + 8, :] = ups
            down[c, 8 * t : 8 * t + 8, :] = downs


def two_sum(a, b):
    total = a + b
    part = total - a
    return total, (a - (total - part)) + (b - part)


def split(a):
    large = a * 4097.0
    high = large - (large - a)
    return high, a - high


def two_product(a, b):
    total = a * b
    (ah, al), (bh, bl) = split(a), split(b)
    return total, ((ah * bh - total) + ah * bl + al * bh) + al * bl


def added(first, second):
    total, rest = two_sum(first[0], second[0])
    return total, (first[1] + second[1]) + rest


def rolled(value, shift, axis):
    return tuple(pltpu.roll(v, shift, axis) for v in value)


def chosen(where, first, second):
    return tuple(jnp.where(where, f, s) for f, s in zip(first, second))


def lane_totals(values):
    row, lane = rows((8, NZ)), lanes((8, NZ))
    reverse = (row % 2) * 4 + (row // 2 % 2) * 2 + row // 4
    zero = jnp.zeros((8, NZ), jnp.float32)
    found = zero
    for g in range(0, len(values), 8):
        group = values[g : g + 8]
        group = group + [(zero, zero)] * (8 - len(group))
        for half in (4, 2, 1):
            early = row % (2 * half) < half
            group = [
                added(
                    chosen(early, first, rolled(second, half, 0)),
                    chosen(early, rolled(first, 8 - half, 0), second),
                )
                for first, second in zip(group[::2], group[1::2])
            ]
        total = group[0]
        for half in (64, 32, 16, 8, 4, 2, 1):
            total = added(total, rolled(total, half, 1))
        total = two_sum(*total)
        found = jnp.where(lane == g + reverse, total[0], found)
        found = jnp.where(lane == 64 + g + reverse, total[1], found)
    return jnp.sum(found, axis=0, keepdims=True)


def folded(read, count):
    tiles = []
    for first in range(0, count, 8):
        size = min(8, count - first)
        tile = read(first, size)
        if size < 8:
            tile = jnp.concatenate([tile, jnp.zeros((8 - size, NZ), jnp.float32)], axis=0)
        tiles.append((tile, turned(tile, 64)))
    while len(tiles) > 1:
        tiles = [added(f, s) for f, s in zip(tiles[::2], tiles[1::2])] + tiles[len(tiles) // 2 * 2 :]
    total = tiles[0]
    for half in (4, 2, 1):
        total = added(total, rolled(total, half, 0))
    return two_sum(*total)


def fold(parts, out):
    high, rest = folded(lambda first, size: parts[first : first + size, :], parts.shape[0])
    row = jnp.where(lanes((8, NZ)) < 64, high, turned(rest, 64))[0:1]
    out[...] = jnp.broadcast_to(row, out.shape)


def section_of(at, here, before, after):
    result = []
    for c in range(3):
        slope = after[c] - before[c]
        flux = at[1] * at[c]
        slope = slope + (back(flux, 0) - ahead(flux, 0))
        flux = at[2] * at[c]
        slope = slope + (back(flux, 1) - ahead(flux, 1))
        result.append((at[c] - (0.5 * time_step) * slope) * here)
    return result


def laplace_of(at, before, after):
    beside = (before + after) + (back(at, 0) + ahead(at, 0))
    beside = beside + (back(at, 1) + ahead(at, 1))
    return at - beside * (1.0 / 6.0)


def pairs():
    return [(k // 2, (k + 1) // 2) for k in range(MOMENTS)]


def inner_lanes(flags, whole, powers, sums, edge, *work):
    row = rows((EY, NZ))
    in_y = jnp.where(row < NY, 1.0, jnp.where(row < NY + HALO, flags[3:4, :], flags[2:3, :]))
    below_x, above_x = in_y * flags[0:1, :], in_y * flags[1:2, :]

    def inside(x):
        return below_x if x < 0 else (above_x if x >= NX else in_y)

    def plane(x):
        return [whole[c, x % EX] for c in range(3)]

    def products(value):
        return [value[0] * value[c] for c in range(3)]

    lane = lanes((8, NZ))
    for c in range(3):
        for p in range(GROUPS):
            for t in range(3):
                part = slice(8 * t, 8 * t + 8)
                tile = jnp.zeros((8, NZ), jnp.float32)
                for g in range(GROUPS):
                    source = whole[c, GROUPS * g + p, part, :]
                    first = STEP * g + 4
                    tile = jnp.where((lane >= first) & (lane < first + 8), turned(source, first), tile)
                    first = STEP * g + 16
                    tile = jnp.where((lane >= first) & (lane < first + 8), turned(source, first - 120), tile)
                edge[c, p, part, :] = tile

    for x in range(-ITERS, NX + ITERS):
        new = section_of(plane(x), inside(x), products(plane(x - 1)), products(plane(x + 1)))
        for c in range(3):
            work[0][c, x % EX] = new[c]
            if 0 <= x < NX:
                powers[0, c, x] = new[c][:NY]
    for k in range(1, ITERS + 1):
        reach = ITERS - k
        for x in range(-reach, NX + reach):
            for c in range(3):
                source = work[k - 1]
                new = laplace_of(source[c, x % EX], source[c, (x - 1) % EX], source[c, (x + 1) % EX])
                if k < ITERS:
                    new = new * inside(x)
                    work[k][c, x % EX] = new
                if 0 <= x < NX:
                    powers[k, c, x] = new[:NY]
    valid = (lane >= HALO) & (lane < NZ - HALO)
    zero = jnp.zeros((8, NZ), jnp.float32)
    for c in range(3):
        total = [(zero, zero)] * MOMENTS
        for x in range(NX):
            for t in range(2):
                v = [powers[k, c, x, 8 * t : 8 * t + 8, :] for k in range(ITERS + 1)]
                total = [added(s, (v[a] * v[b], zero)) for s, (a, b) in zip(total, pairs())]
        for k in range(MOMENTS):
            for part in range(2):
                sums[c, k, part] = jnp.where(valid, total[k][part], 0.0)


def edge_lanes(flags, edge, low, high, sums, powers, moments, whole, *work):
    row = rows((EY, NZ))
    lane = lanes((EY, NZ))
    group, offset = lane // STEP, lane % STEP
    inside = jnp.where(row >= NY + HALO, flags[2:3, :], jnp.where(row >= NY, flags[3:4, :], 1.0))
    inside *= jnp.where(group == 3, flags[0:1, :], jnp.where(group == 2, flags[1:2, :], 1.0))
    inside *= jnp.where(offset < 4, flags[4:5, :], jnp.where(offset >= 24, flags[5:6, :], 1.0))
    for c in range(3):
        for p in range(GROUPS):
            value = jnp.where(offset < 4, turned(low[c], -4 * p), edge[c, p])
            whole[c, p] = jnp.where((offset >= 24) & (offset < 28), turned(high[c], 24 - 4 * p), value)

    def beyond(read, p):
        return turned(read(0), -STEP) if p == GROUPS - 1 else read(p + 1)

    def behind(read, p):
        return turned(read(GROUPS - 1), STEP) if p == 0 else read(p - 1)

    for p in range(GROUPS):
        at = [whole[c, p] for c in range(3)]
        before, after = (
            [side(lambda q, c=c: whole[0, q] * whole[c, q], p) for c in range(3)] for side in (behind, beyond)
        )
        new = section_of(at, inside, before, after)
        for c in range(3):
            work[0][c, p] = new[c]
            powers[0, c, p] = new[c][:NY]
    for k in range(1, ITERS + 1):
        for p in range(GROUPS):
            for c in range(3):
                read = functools.partial(lambda c, q: work[k - 1][c, q], c)
                new = laplace_of(read(p), behind(read, p), beyond(read, p))
                if k < ITERS:
                    new = new * inside
                    work[k][c, p] = new
                powers[k, c, p] = new[:NY]
    lane = lanes((8, NZ))
    group, offset = lane // STEP, lane % STEP
    valid = (group < 2) & (((offset >= 4) & (offset < 8)) | ((offset >= 20) & (offset < 24)))
    zero = jnp.zeros((8, NZ), jnp.float32)
    totals = []
    for k in range(MOMENTS):
        a, b = pairs()[k]
        for c in range(3):
            total = (sums[c, k, 0], sums[c, k, 1])
            for p in range(GROUPS):
                for t in range(2):
                    part = slice(8 * t, 8 * t + 8)
                    value = powers[a, c, p, part, :] * powers[b, c, p, part, :]
                    total = added(total, (jnp.where(valid, value, 0.0), zero))
            totals.append(total)
    moments[...] = jnp.broadcast_to(lane_totals(totals), moments.shape)


def weights_of(moments, scale):
    middle = moments[1][0] / moments[0][0]
    moments = list(moments)
    for r in range(1, MOMENTS):
        for k in range(MOMENTS - 1, r - 1, -1):
            total, rest = two_product(middle, moments[k - 1][0])
            rest = rest + middle * moments[k - 1][1]
            moments[k] = two_sum(*added(moments[k], (-total, -rest)))
    moments = [m[0] for m in moments]
    diagonal = 1.0 + scale * middle

    def inner(first, second):
        return sum(f * s * moments[i + j] for i, f in enumerate(first) for j, s in enumerate(second))

    def plus(first, factor, second):
        size = max(len(first), len(second))
        padded = [list(v) + [0.0] * (size - len(v)) for v in (first, second)]
        return [f + factor * s for f, s in zip(*padded)]

    def in_powers_of_l(weights):
        weights = list(weights)
        for r in range(len(weights) - 1):
            for k in range(len(weights) - 2, r - 1, -1):
                weights[k] = weights[k] - middle * weights[k + 1]
        return weights

    one = jnp.ones_like(scale)
    total, residual, direction = [], [one], [one]
    now = moments[0]
    for iteration in range(ITERS):
        image = plus([diagonal * d for d in direction], scale, [0.0] + direction)
        step = now / inner(direction, image)
        total = plus(total, step, direction)
        residual = plus(residual, -step, image)
        if iteration + 1 < ITERS:
            new = inner(residual, residual)
            direction = plus(residual, new / now, direction)
            now = new
    return in_powers_of_l(total), in_powers_of_l(residual)


def combine(parts, scale, powers, edges, total, rest):
    lane = lanes((8, NZ))
    high, low = folded(lambda first, size: parts[first : first + size, :], parts.shape[0])
    moments = [(turned(high, -3 * k), turned(low, -3 * k)) for k in range(MOMENTS)]

    def spread(value, c):
        return jnp.broadcast_to(jnp.sum(jnp.where(lane == c, value, 0.0), axis=1, keepdims=True), (8, NZ))

    for out, weights in zip((total, rest), weights_of(moments, jnp.broadcast_to(scale[0:1, :], (8, NZ)))):
        for c in range(3):
            factors = [spread(w, c) for w in weights]

            def mix(read):
                return sum(f * read(k) for k, f in enumerate(factors))

            for p in range(GROUPS):
                for t in range(2):
                    part = slice(8 * t, 8 * t + 8)
                    side = mix(lambda k: edges[k, c, p, part, :])
                    for g in range(2):
                        x = GROUPS * g + p
                        value = mix(lambda k: powers[k, c, x, part, :])
                        value = jnp.where(lane < HALO, turned(side, -(STEP * g + 4)), value)
                        value = jnp.where(lane >= NZ - HALO, turned(side, 104 - STEP * g), value)
                        out[c, x, part, :] = value


def kernel(body, outs, scratch=(), whole_array=False):
    vmem = pl.BlockSpec(memory_space=pltpu.VMEM)
    shape = jax.ShapeDtypeStruct if whole_array else pltpu.VMEM

    def call(*args):
        return pl.pallas_call(
            body,
            in_specs=[vmem] * len(args),
            out_specs=[vmem] * len(outs),
            out_shape=[shape(s, jnp.float32) for s in outs],
            scratch_shapes=[pltpu.VMEM(s, jnp.float32) for s in scratch],
            name=body.__name__,
        )(*args)

    return call


def held(value):
    return pltpu.with_memory_space_constraint(value, pltpu.VMEM)


def exchanged(up, down, axis):
    size = lax.axis_size(axis)
    steps = [(i, i + 1) for i in range(size - 1)]
    return lax.ppermute(up, axis, steps), lax.ppermute(down, axis, [(b, a) for a, b in steps])


def gathered(row, axes):
    return lax.all_to_all(row, axes, 0, 0, tiled=True)


def body(velocity, diffusion):
    ends = [f for a in (GX, GY, GZ) for f in (lax.axis_index(a) > 0, lax.axis_index(a) + 1 < lax.axis_size(a))]
    flags = jnp.broadcast_to(jnp.stack(ends + ends[:2]).astype(jnp.float32)[:, None], (8, NZ))
    scale = jnp.broadcast_to(jnp.pad(6.0 * diffusion, (0, NZ - 3))[None], (8, NZ))
    block, wide, tiles = (3, NX, NY, NZ), (3, EX, EY, NZ), (3, GROUPS, EY, NZ)
    flags, scale = held(flags), held(scale)
    own, up, down = kernel(pack_y, [block] + [(3, 4, 8, NZ)] * 2)(velocity)
    low, high = map(held, exchanged(up, down, GY))
    up, down = kernel(pack_x, [(3, 11, 8, NZ)] * 2)(own, low, high)
    below, above = map(held, exchanged(up, down, GX))
    whole, up, down = kernel(pack_z, [wide, (3, EY, NZ), (3, EY, NZ)])(own, low, high, below, above)
    low, high = map(held, exchanged(up, down, GZ))
    powers, sums, edge = kernel(
        inner_lanes, [(ITERS + 1,) + block, (3, MOMENTS, 2, 8, NZ), tiles], [wide] * ITERS
    )(flags, whole)
    planes, stack = lax.axis_size(GX + GY), lax.axis_size(GZ)
    edges, row = kernel(
        edge_lanes, [(ITERS + 1, 3, GROUPS, NY, NZ), (planes, NZ)], [tiles] * (ITERS + 1)
    )(flags, edge, low, high, sums)
    (row,) = kernel(fold, [(stack, NZ)])(held(gathered(row, GX + GY)))
    return kernel(combine, [block] * 2, whole_array=True)(held(gathered(row, GZ)), scale, powers, edges)


def solution(mesh):
    finer = Mesh(
        mesh.devices.reshape(2, 2, 4, 4, mesh.shape["gz"]), ("gx_0", "gx_1", "gy_0", "gy_1", "gz")
    )
    return jax.shard_map(
        body,
        mesh=finer,
        in_specs=(P(None, GX, GY, "gz"), P()),
        out_specs=(P(None, GX, GY, "gz"), P(None, GX, GY, "gz")),
        check_vma=False,
    )
```

time: 90.3 us -> 86.2 us (0.955)
  blocking collectives: 43.8 us -> 17.8 us
  starting transfers between devices: 19.5 us -> 35.6 us
  waiting for transfers between devices: 7.86 us -> 15.9 us
  Pallas kernels: 11.8 us -> 10.4 us
    all_to_all x2 -> x1, blocking collectives: 43.8 us -> 17.8 us  [gathered(): return lax.all_to_all(row, axes, 0, 0, tiled=True)]
    all_to_all x0 -> x1, starting transfers between devices: none -> 15 us  [gathered(): return lax.all_to_all(row, axes, 0, 0, tiled=True)]
    all_to_all x0 -> x1, waiting for transfers between devices: none -> 8.84 us  [gathered(): return lax.all_to_all(row, axes, 0, 0, tiled=True)]
    ppermute x3, starting transfers between devices: 4.48 us -> 12.1 us  [exchanged(): lax.ppermute(up, axis, steps)]
    ppermute x3, starting transfers between devices: 15 us -> 8.48 us  [exchanged(): lax.ppermute(down, axis, [(b, a) for a, b in steps])]
    ppermute x3, waiting for transfers between devices: 3.53 us -> 0.01 us  [exchanged(): lax.ppermute(up, axis, steps)]
    ppermute x3, waiting for transfers between devices: 4.32 us -> 7.08 us  [exchanged(): lax.ppermute(down, axis, [(b, a) for a, b in steps])]
    unnamed x14 -> x15, local copies, waits for them, and re-layouts: 2.55 us -> 4.45 us
  transfers between devices with their start and end apart: 6 -> 7, of which waited for: 3 -> 3; matrix products, arithmetic and copies ran while one was open for 1% -> 0% of each run, Pallas kernels for 4% -> 3%
where the time goes in v3:
time: 86.2 us; the launch traced here: 85.8 us
  starting transfers between devices  35.6 us (41%)
  blocking collectives  17.8 us (21%)
  waiting for transfers between devices  15.9 us (18%)
  Pallas kernels  10.4 us (12%)
  local copies, waits for them, and re-layouts  5.24 us (6%)
    all_to_all x1, blocking collectives, gathered(): return lax.all_to_all(row, axes, 0, 0, tiled=True)  17.8 us
    all_to_all x1, starting transfers between devices, gathered(): return lax.all_to_all(row, axes, 0, 0, tiled=True)  15 us
    ppermute x3, starting transfers between devices, exchanged(): lax.ppermute(up, axis, steps)  12.1 us
    pallas_call x7, Pallas kernels, call(): pl.pallas_call(body, in_specs=[vmem] * len(args), out_specs=[vmem] * len(...  10.4 us
    all_to_all x1, waiting for transfers between devices, gathered(): return lax.all_to_all(row, axes, 0, 0, tiled=True)  8.84 us
    ppermute x3, starting transfers between devices, exchanged(): lax.ppermute(down, axis, [(b, a) for a, b in steps])  8.48 us
    ppermute x3, waiting for transfers between devices, exchanged(): lax.ppermute(down, axis, [(b, a) for a, b in steps])  7.08 us
    unnamed x15, local copies, waits for them, and re-layouts  4.45 us
  transfers between devices with their start and end apart: 7, of which 3 were waited for; matrix products, arithmetic and copies ran while one was open for 0% of the time, Pallas kernels for 3%

profile of v3, /device:TPU:1, one launch (start us, length us, event | category | flops | bytes accessed | tf_op | source)
XLA Modules:
  0.0 85.8 jit_solution(12026379281538576726)
XLA Ops:
  0.6 1.0 %pack_y.1 = (f32[3,8,16,128]{3,2,1,0:T(8,128)S(1)}, f32[3,4,8,128]{3,2,1,0:T(8,128)S(1)}, f32[3,4,8,128]{3,2,1,0:T(8,128)S(1)}) custom-call(f32[3,8,16,128]{3,2,1,0:T(8,128)} %block.1), custom_call_target="tpu_custom_call" | custom-call | tf_op jit(solution)/shard_map/pack_y/pallas_call | solution.py:388
  1.6 0.0 copy-start.1
  1.6 0.7 copy-done.1
  2.3 5.0 %collective-permute-start = (f32[3,4,8,128]{3,2,1,0:T(8,128)S(1)}, f32[3,4,8,128]{3,2,1,0:T(8,128)S(1)}, u32[]{:S(2)}, u32[]{:S(2)}) collective-permute-start(f32[3,4,8,128]{3,2,1,0:T(8,128)S(1)} %get-tuple-element.16), channel_id=1, source_target_pairs={{0,12},{12,24},{24,36},{36,48},{48,60},{60,72},{72,84},{84,96},{96... | collective-permute-start | bytes 147464 | tf_op jit(solution)/shard_map/ppermute | solution.py:407
  7.3 1.3 %collective-permute-start.1 = (f32[3,4,8,128]{3,2,1,0:T(8,128)S(1)}, f32[3,4,8,128]{3,2,1,0:T(8,128)S(1)}, u32[]{:S(2)}, u32[]{:S(2)}) collective-permute-start(f32[3,4,8,128]{3,2,1,0:T(8,128)S(1)} %get-tuple-element.17), channel_id=1, source_target_pairs={{12,0},{24,12},{36,24},{48,36},{60,48},{72,60},{84,72},{96,84},{10... | collective-permute-start | bytes 147464 | tf_op jit(solution)/shard_map/ppermute | solution.py:407
  8.6 0.0 collective-permute-done.low
  8.6 6.1 %collective-permute-done.1.high = f32[3,4,8,128]{3,2,1,0:T(8,128)S(1)} collective-permute-done((f32[3,4,8,128]{3,2,1,0:T(8,128)S(1)}, f32[3,4,8,128]{3,2,1,0:T(8,128)S(1)}, u32[]{:S(2)}, u32[]{:S(2)}) %collective-permute-start.1) | collective-permute-done | bytes 49184 | tf_op jit(solution)/shard_map/ppermute | solution.py:407
  14.7 0.9 %pack_x.1 = (f32[3,11,8,128]{3,2,1,0:T(8,128)S(1)}, f32[3,11,8,128]{3,2,1,0:T(8,128)S(1)}) custom-call(f32[3,8,16,128]{3,2,1,0:T(8,128)} %copy-done.1, f32[3,4,8,128]{3,2,1,0:T(8,128)S(1)} %collective-permute-done.low, f32[3,4,8,128]{3,2,1,0:T(8,128)S(1)} %collective-permute-done.1.high), custom_call_target="tpu_custom_call" | custom-call | tf_op jit(solution)/shard_map/pack_x/pallas_call | solution.py:388
  15.7 3.5 %collective-permute-start.2 = (f32[3,11,8,128]{3,2,1,0:T(8,128)S(1)}, f32[3,11,8,128]{3,2,1,0:T(8,128)S(1)}, u32[]{:S(2)}, u32[]{:S(2)}) collective-permute-start(f32[3,11,8,128]{3,2,1,0:T(8,128)S(1)} %get-tuple-element.18), channel_id=1, source_target_pairs={{0,192},{192,384},{384,576},{1,193},{193,385},{385,577},{2,194},{1... | collective-permute-start | bytes 405512 | tf_op jit(solution)/shard_map/ppermute | solution.py:407
  19.2 5.9 %collective-permute-start.3 = (f32[3,11,8,128]{3,2,1,0:T(8,128)S(1)}, f32[3,11,8,128]{3,2,1,0:T(8,128)S(1)}, u32[]{:S(2)}, u32[]{:S(2)}) collective-permute-start(f32[3,11,8,128]{3,2,1,0:T(8,128)S(1)} %get-tuple-element.19), channel_id=1, source_target_pairs={{192,0},{384,192},{576,384},{193,1},{385,193},{577,385},{194,2},{3... | collective-permute-start | bytes 405512 | tf_op jit(solution)/shard_map/ppermute | solution.py:407
  25.1 0.0 collective-permute-done.2.below
  25.1 1.0 %collective-permute-done.3.above = f32[3,11,8,128]{3,2,1,0:T(8,128)S(1)} collective-permute-done((f32[3,11,8,128]{3,2,1,0:T(8,128)S(1)}, f32[3,11,8,128]{3,2,1,0:T(8,128)S(1)}, u32[]{:S(2)}, u32[]{:S(2)}) %collective-permute-start.3) | collective-permute-done | bytes 135200 | tf_op jit(solution)/shard_map/ppermute | solution.py:407
  26.1 1.3 %pack_z.1 = (f32[3,16,24,128]{3,2,1,0:T(8,128)S(1)}, f32[3,24,128]{2,1,0:T(8,128)S(1)}, f32[3,24,128]{2,1,0:T(8,128)S(1)}) custom-call(f32[3,8,16,128]{3,2,1,0:T(8,128)} %copy-done.1, f32[3,4,8,128]{3,2,1,0:T(8,128)S(1)} %collective-permute-done.low, f32[3,4,8,128]{3,2,1,0:T(8,128)S(1)} %collective-permute-done.1.high, ...), custom_call_target="tpu_custom_call" | custom-call | tf_op jit(solution)/shard_map/pack_z/pallas_call | solution.py:388
  27.3 0.0 copy-start.2
  27.3 0.8 copy-done.2
  28.2 3.5 %collective-permute-start.4 = (f32[3,24,128]{2,1,0:T(8,128)S(1)}, f32[3,24,128]{2,1,0:T(8,128)S(1)}, u32[]{:S(2)}, u32[]{:S(2)}) collective-permute-start(f32[3,24,128]{2,1,0:T(8,128)S(1)} %get-tuple-element.22), channel_id=1, source_target_pairs={{0,1},{1,2},{2,3},{3,4},{4,5},{5,6},{6,7},{7,8},{8,9},{9,10},{10,1... | collective-permute-start | bytes 110600 | tf_op jit(solution)/shard_map/ppermute | solution.py:407
  31.7 1.3 %collective-permute-start.5 = (f32[3,24,128]{2,1,0:T(8,128)S(1)}, f32[3,24,128]{2,1,0:T(8,128)S(1)}, u32[]{:S(2)}, u32[]{:S(2)}) collective-permute-start(f32[3,24,128]{2,1,0:T(8,128)S(1)} %get-tuple-element.23), channel_id=1, source_target_pairs={{1,0},{2,1},{3,2},{4,3},{5,4},{6,5},{7,6},{8,7},{9,8},{10,9},{11,1... | collective-permute-start | bytes 110600 | tf_op jit(solution)/shard_map/ppermute | solution.py:407
  33.0 0.1 stack.29
  33.2 0.1 broadcast_in_dim.4.flags
  33.2 2.4 %inner_lanes.1 = (f32[4,3,8,16,128]{4,3,2,1,0:T(8,128)S(1)}, f32[3,6,2,8,128]{4,3,2,1,0:T(8,128)S(1)}, f32[3,4,24,128]{3,2,1,0:T(8,128)S(1)}) custom-call(f32[8,128]{1,0:T(8,128)S(1)} %broadcast_in_dim.4.flags, f32[3,16,24,128]{3,2,1,0:T(8,128)} %copy-done.2), custom_call_target="tpu_custom_call" | custom-call | tf_op jit(solution)/shard_map/inner_lanes/pallas_call | solution.py:388
  35.7 0.0 copy-start
  35.7 0.9 %copy-done = f32[4,3,8,16,128]{4,3,2,1,0:T(8,128)} copy-done((f32[4,3,8,16,128]{4,3,2,1,0:T(8,128)}, f32[4,3,8,16,128]{4,3,2,1,0:T(8,128)S(1)}, u32[]{:S(2)}) %copy-start) | copy-done | bytes 786456
  36.6 0.0 copy-start.4
  36.6 0.7 copy-done.4
  37.2 0.0 copy-start.5
  37.2 0.7 copy-done.5
  37.9 0.0 collective-permute-done.4.low
  37.9 0.0 collective-permute-done.5.high
  37.9 2.1 %edge_lanes.1 = (f32[4,3,4,16,128]{4,3,2,1,0:T(8,128)S(1)}, f32[64,128]{1,0:T(8,128)S(1)}) custom-call(f32[8,128]{1,0:T(8,128)S(1)} %broadcast_in_dim.4.flags, f32[3,4,24,128]{3,2,1,0:T(8,128)} %copy-done.5, f32[3,24,128]{2,1,0:T(8,128)S(1)} %collective-permute-done.4.low, f32[3,24,128]{2,1,0:T(8,128)S(1)} %collective-permute-done.5.high, ...), custom_call_target="tpu_custom_call" | custom-call | tf_op jit(solution)/shard_map/edge_lanes/pallas_call | solution.py:388
  40.0 0.0 copy-start.3
  40.0 0.8 copy-done.3
  40.8 17.8 %all_to_all.22 = f32[64,1,128]{2,1,0:T(1,128)S(1)} all-to-all(f32[64,1,128]{2,1,0:T(1,128)S(1)} %bitcast.17), channel_id=1, replica_groups=mesh['gx_0'=2,'gx_1'=2,'gy_0'=4,'gy_1'=4,'gz'=12] {'gx_0','gx_1','gy_0',..., dimensions={0} | all-to-all | bytes 65536 | tf_op jit(solution)/shard_map/all_to_all | solution.py:411
  58.6 0.2 fold.1
  58.7 0.6 copy.5
  59.3 0.0 copy-start.6
  59.3 15.0 %all-to-all-start.1 = ((f32[12,1,128]{2,1,0:T(1,128)}), f32[12,1,128]{2,1,0:T(1,128)S(1)}, u32[]{:S(2)}, u32[]{:S(2)}) async-start(f32[12,1,128]{2,1,0:T(1,128)} %copy.5), calls=%async_computation.1 | async-start | bytes 12288 | tf_op jit(solution)/shard_map/all_to_all | solution.py:411
  74.4 0.0 copy-done.6
  74.4 8.8 %all-to-all-done.1 = f32[12,1,128]{2,1,0:T(1,128)S(1)} async-done(((f32[12,1,128]{2,1,0:T(1,128)}), f32[12,1,128]{2,1,0:T(1,128)S(1)}, u32[]{:S(2)}, u32[]{:S(2)}) %all-to-all-start.1) | async-done | bytes 6176 | tf_op jit(solution)/shard_map/all_to_all | solution.py:411
  83.2 2.5 %combine.1 = (f32[3,8,16,128]{3,2,1,0:T(8,128)}, f32[3,8,16,128]{3,2,1,0:T(8,128)}) custom-call(f32[12,128]{1,0:T(8,128)S(1)} %bitcast.15, f32[8,128]{1,0:T(8,128)S(1)} %broadcast_in_dim.5.scale, f32[4,3,8,16,128]{4,3,2,1,0:T(8,128)} %copy-done, f32[4,3,4,16,128]{4,3,2,1,0:T(8,128)} %copy-done.3), custom_call_target="tpu_custom_call" | custom-call | tf_op jit(solution)/shard_map/combine/pallas_call | solution.py:388
  (5 shorter events, 0.0 us)
Async XLA Ops:
  1.6 0.7 copy-start.1
  2.3 6.3 %collective-permute-start = (f32[3,4,8,128]{3,2,1,0:T(8,128)S(1)}, f32[3,4,8,128]{3,2,1,0:T(8,128)S(1)}, u32[]{:S(2)}, u32[]{:S(2)}) collective-permute-start(f32[3,4,8,128]{3,2,1,0:T(8,128)S(1)} %get-tuple-element.16), channel_id=1, source_target_pairs={{0,12},{12,24},{24,36},{36,48},{48,60},{60,72},{72,84},{84,96},{96... | collective-permute-start | bytes 147464 | tf_op jit(solution)/shard_map/ppermute | solution.py:407
  7.3 7.4 %collective-permute-start.1 = (f32[3,4,8,128]{3,2,1,0:T(8,128)S(1)}, f32[3,4,8,128]{3,2,1,0:T(8,128)S(1)}, u32[]{:S(2)}, u32[]{:S(2)}) collective-permute-start(f32[3,4,8,128]{3,2,1,0:T(8,128)S(1)} %get-tuple-element.17), channel_id=1, source_target_pairs={{12,0},{24,12},{36,24},{48,36},{60,48},{72,60},{84,72},{96,84},{10... | collective-permute-start | bytes 147464 | tf_op jit(solution)/shard_map/ppermute | solution.py:407
  15.7 9.4 %collective-permute-start.2 = (f32[3,11,8,128]{3,2,1,0:T(8,128)S(1)}, f32[3,11,8,128]{3,2,1,0:T(8,128)S(1)}, u32[]{:S(2)}, u32[]{:S(2)}) collective-permute-start(f32[3,11,8,128]{3,2,1,0:T(8,128)S(1)} %get-tuple-element.18), channel_id=1, source_target_pairs={{0,192},{192,384},{384,576},{1,193},{193,385},{385,577},{2,194},{1... | collective-permute-start | bytes 405512 | tf_op jit(solution)/shard_map/ppermute | solution.py:407
  19.2 6.9 %collective-permute-start.3 = (f32[3,11,8,128]{3,2,1,0:T(8,128)S(1)}, f32[3,11,8,128]{3,2,1,0:T(8,128)S(1)}, u32[]{:S(2)}, u32[]{:S(2)}) collective-permute-start(f32[3,11,8,128]{3,2,1,0:T(8,128)S(1)} %get-tuple-element.19), channel_id=1, source_target_pairs={{192,0},{384,192},{576,384},{193,1},{385,193},{577,385},{194,2},{3... | collective-permute-start | bytes 405512 | tf_op jit(solution)/shard_map/ppermute | solution.py:407
  27.3 0.8 copy-start.2
  28.2 9.7 %collective-permute-start.4 = (f32[3,24,128]{2,1,0:T(8,128)S(1)}, f32[3,24,128]{2,1,0:T(8,128)S(1)}, u32[]{:S(2)}, u32[]{:S(2)}) collective-permute-start(f32[3,24,128]{2,1,0:T(8,128)S(1)} %get-tuple-element.22), channel_id=1, source_target_pairs={{0,1},{1,2},{2,3},{3,4},{4,5},{5,6},{6,7},{7,8},{8,9},{9,10},{10,1... | collective-permute-start | bytes 110600 | tf_op jit(solution)/shard_map/ppermute | solution.py:407
  31.7 6.2 %collective-permute-start.5 = (f32[3,24,128]{2,1,0:T(8,128)S(1)}, f32[3,24,128]{2,1,0:T(8,128)S(1)}, u32[]{:S(2)}, u32[]{:S(2)}) collective-permute-start(f32[3,24,128]{2,1,0:T(8,128)S(1)} %get-tuple-element.23), channel_id=1, source_target_pairs={{1,0},{2,1},{3,2},{4,3},{5,4},{6,5},{7,6},{8,7},{9,8},{10,9},{11,1... | collective-permute-start | bytes 110600 | tf_op jit(solution)/shard_map/ppermute | solution.py:407
  35.7 0.9 %copy-start = (f32[4,3,8,16,128]{4,3,2,1,0:T(8,128)}, f32[4,3,8,16,128]{4,3,2,1,0:T(8,128)S(1)}, u32[]{:S(2)}) copy-start(f32[4,3,8,16,128]{4,3,2,1,0:T(8,128)S(1)} %get-tuple-element.26.powers) | copy-start | bytes 2359300
  36.6 0.7 copy-start.4
  37.2 0.7 copy-start.5
  40.0 0.8 copy-start.3
  59.3 15.0 %copy-start.6 = (f32[3]{0:T(128)S(1)}, f32[3]{0:T(128)}, u32[]{:S(2)}) copy-start(f32[3]{0:T(128)} %param.3) | copy-start | bytes 40
  59.3 23.9 %all-to-all-start.1 = ((f32[12,1,128]{2,1,0:T(1,128)}), f32[12,1,128]{2,1,0:T(1,128)S(1)}, u32[]{:S(2)}, u32[]{:S(2)}) async-start(f32[12,1,128]{2,1,0:T(1,128)} %copy.5), calls=%async_computation.1 | async-start | bytes 12288 | tf_op jit(solution)/shard_map/all_to_all | solution.py:411

commit v4 on v3

--- a/solution.py
+++ b/solution.py
@@ -380,11 +380,13 @@
                         out[c, x, part, :] = value
 
 
-def kernel(body, outs, scratch=(), whole_array=False):
+def kernel(body, outs, scratch=(), first=False, last=False):
     vmem = pl.BlockSpec(memory_space=pltpu.VMEM)
-    shape = jax.ShapeDtypeStruct if whole_array else pltpu.VMEM
+    shape = jax.ShapeDtypeStruct if last else pltpu.VMEM
 
     def call(*args):
+        if not first:
+            args = [pltpu.with_memory_space_constraint(a, pltpu.VMEM) for a in args]
         return pl.pallas_call(
             body,
             in_specs=[vmem] * len(args),
@@ -397,10 +399,6 @@
     return call
 
 
-def held(value):
-    return pltpu.with_memory_space_constraint(value, pltpu.VMEM)
-
-
 def exchanged(up, down, axis):
     size = lax.axis_size(axis)
     steps = [(i, i + 1) for i in range(size - 1)]
@@ -416,13 +414,12 @@
     flags = jnp.broadcast_to(jnp.stack(ends + ends[:2]).astype(jnp.float32)[:, None], (8, NZ))
     scale = jnp.broadcast_to(jnp.pad(6.0 * diffusion, (0, NZ - 3))[None], (8, NZ))
     block, wide, tiles = (3, NX, NY, NZ), (3, EX, EY, NZ), (3, GROUPS, EY, NZ)
-    flags, scale = held(flags), held(scale)
-    own, up, down = kernel(pack_y, [block] + [(3, 4, 8, NZ)] * 2)(velocity)
-    low, high = map(held, exchanged(up, down, GY))
+    own, up, down = kernel(pack_y, [block] + [(3, 4, 8, NZ)] * 2, first=True)(velocity)
+    low, high = exchanged(up, down, GY)
     up, down = kernel(pack_x, [(3, 11, 8, NZ)] * 2)(own, low, high)
-    below, above = map(held, exchanged(up, down, GX))
+    below, above = exchanged(up, down, GX)
     whole, up, down = kernel(pack_z, [wide, (3, EY, NZ), (3, EY, NZ)])(own, low, high, below, above)
-    low, high = map(held, exchanged(up, down, GZ))
+    low, high = exchanged(up, down, GZ)
     powers, sums, edge = kernel(
         inner_lanes, [(ITERS + 1,) + block, (3, MOMENTS, 2, 8, NZ), tiles], [wide] * ITERS
     )(flags, whole)
@@ -430,8 +427,8 @@
     edges, row = kernel(
         edge_lanes, [(ITERS + 1, 3, GROUPS, NY, NZ), (planes, NZ)], [tiles] * (ITERS + 1)
     )(flags, edge, low, high, sums)
-    (row,) = kernel(fold, [(stack, NZ)])(held(gathered(row, GX + GY)))
-    return kernel(combine, [block] * 2, whole_array=True)(held(gathered(row, GZ)), scale, powers, edges)
+    (row,) = kernel(fold, [(stack, NZ)])(gathered(row, GX + GY))
+    return kernel(combine, [block] * 2, last=True)(gathered(row, GZ), scale, powers, edges)
 
 
 def solution(mesh):

time: 86.2 us -> 79.5 us (0.922)
  Pallas kernels: 10.4 us -> 5.36 us
  local copies, waits for them, and re-layouts: 5.24 us -> 0.79 us
  waiting for transfers between devices: 15.9 us -> 18.3 us
    pallas_call x7, Pallas kernels: 10.4 us -> 5.36 us  [call(): pl.pallas_call(body, in_specs=[vmem] * len(args), out_specs=[vmem] * len(...]
    unnamed x15 -> x3, local copies, waits for them, and re-layouts: 4.45 us -> 0.01 us
    ppermute x3, waiting for transfers between devices: 7.08 us -> 9.48 us  [exchanged(): lax.ppermute(down, axis, [(b, a) for a, b in steps])]
  transfers between devices with their start and end apart: 7 -> 7, of which waited for: 3 -> 4; matrix products, arithmetic and copies ran while one was open for 0% -> 0% of each run, Pallas kernels for 3% -> 2%
where the time goes in v4:
time: 79.5 us; the launch traced here: 79.1 us
  starting transfers between devices  35.5 us (45%)
  waiting for transfers between devices  18.3 us (23%)
  blocking collectives  18.3 us (23%)
  Pallas kernels  5.36 us (7%)
    all_to_all x1, blocking collectives, gathered(): return lax.all_to_all(row, axes, 0, 0, tiled=True)  18.3 us
    all_to_all x1, starting transfers between devices, gathered(): return lax.all_to_all(row, axes, 0, 0, tiled=True)  15 us
    ppermute x3, starting transfers between devices, exchanged(): lax.ppermute(up, axis, steps)  12.1 us
    ppermute x3, waiting for transfers between devices, exchanged(): lax.ppermute(down, axis, [(b, a) for a, b in steps])  9.48 us
    all_to_all x1, waiting for transfers between devices, gathered(): return lax.all_to_all(row, axes, 0, 0, tiled=True)  8.84 us
    ppermute x3, starting transfers between devices, exchanged(): lax.ppermute(down, axis, [(b, a) for a, b in steps])  8.48 us
    pallas_call x7, Pallas kernels, call(): pl.pallas_call(body, in_specs=[vmem] * len(args), out_specs=[vmem] * len(...  5.36 us
  transfers between devices with their start and end apart: 7, of which 4 were waited for; matrix products, arithmetic and copies ran while one was open for 0% of the time, Pallas kernels for 2%

profile of v4, /device:TPU:1, one launch (start us, length us, event | category | flops | bytes accessed | tf_op | source)
XLA Modules:
  0.0 79.1 jit_solution(15263629760724516193)
XLA Ops:
  0.6 1.0 %pack_y.1 = (f32[3,8,16,128]{3,2,1,0:T(8,128)S(1)}, f32[3,4,8,128]{3,2,1,0:T(8,128)S(1)}, f32[3,4,8,128]{3,2,1,0:T(8,128)S(1)}) custom-call(f32[3,8,16,128]{3,2,1,0:T(8,128)} %block.1), custom_call_target="tpu_custom_call" | custom-call | tf_op jit(solution)/shard_map/pack_y/pallas_call | solution.py:390
  1.6 5.0 %collective-permute-start = (f32[3,4,8,128]{3,2,1,0:T(8,128)S(1)}, f32[3,4,8,128]{3,2,1,0:T(8,128)S(1)}, u32[]{:S(2)}, u32[]{:S(2)}) collective-permute-start(f32[3,4,8,128]{3,2,1,0:T(8,128)S(1)} %get-tuple-element.16), channel_id=1, source_target_pairs={{0,12},{12,24},{24,36},{36,48},{48,60},{60,72},{72,84},{84,96},{96... | collective-permute-start | bytes 147464 | tf_op jit(solution)/shard_map/ppermute | solution.py:405
  6.6 1.3 %collective-permute-start.1 = (f32[3,4,8,128]{3,2,1,0:T(8,128)S(1)}, f32[3,4,8,128]{3,2,1,0:T(8,128)S(1)}, u32[]{:S(2)}, u32[]{:S(2)}) collective-permute-start(f32[3,4,8,128]{3,2,1,0:T(8,128)S(1)} %get-tuple-element.17), channel_id=1, source_target_pairs={{12,0},{24,12},{36,24},{48,36},{60,48},{72,60},{84,72},{96,84},{10... | collective-permute-start | bytes 147464 | tf_op jit(solution)/shard_map/ppermute | solution.py:405
  7.9 0.0 collective-permute-done.low
  7.9 6.1 %collective-permute-done.1.high = f32[3,4,8,128]{3,2,1,0:T(8,128)S(1)} collective-permute-done((f32[3,4,8,128]{3,2,1,0:T(8,128)S(1)}, f32[3,4,8,128]{3,2,1,0:T(8,128)S(1)}, u32[]{:S(2)}, u32[]{:S(2)}) %collective-permute-start.1) | collective-permute-done | bytes 49184 | tf_op jit(solution)/shard_map/ppermute | solution.py:405
  14.1 3.5 %collective-permute-start.2 = (f32[3,11,8,128]{3,2,1,0:T(8,128)S(1)}, f32[3,11,8,128]{3,2,1,0:T(8,128)S(1)}, u32[]{:S(2)}, u32[]{:S(2)}) collective-permute-start(f32[3,11,8,128]{3,2,1,0:T(8,128)S(1)} %get-tuple-element.18), channel_id=1, source_target_pairs={{0,192},{192,384},{384,576},{1,193},{193,385},{385,577},{2,194},{1... | collective-permute-start | bytes 405512 | tf_op jit(solution)/shard_map/ppermute | solution.py:405
  17.6 5.9 %collective-permute-start.3 = (f32[3,11,8,128]{3,2,1,0:T(8,128)S(1)}, f32[3,11,8,128]{3,2,1,0:T(8,128)S(1)}, u32[]{:S(2)}, u32[]{:S(2)}) collective-permute-start(f32[3,11,8,128]{3,2,1,0:T(8,128)S(1)} %get-tuple-element.19), channel_id=1, source_target_pairs={{192,0},{384,192},{576,384},{193,1},{385,193},{577,385},{194,2},{3... | collective-permute-start | bytes 405512 | tf_op jit(solution)/shard_map/ppermute | solution.py:405
  23.5 0.0 collective-permute-done.2.below
  23.5 1.0 %collective-permute-done.3.above = f32[3,11,8,128]{3,2,1,0:T(8,128)S(1)} collective-permute-done((f32[3,11,8,128]{3,2,1,0:T(8,128)S(1)}, f32[3,11,8,128]{3,2,1,0:T(8,128)S(1)}, u32[]{:S(2)}, u32[]{:S(2)}) %collective-permute-start.3) | collective-permute-done | bytes 135200 | tf_op jit(solution)/shard_map/ppermute | solution.py:405
  24.5 0.4 pack_z.1
  24.8 3.6 %collective-permute-start.4 = (f32[3,24,128]{2,1,0:T(8,128)S(1)}, f32[3,24,128]{2,1,0:T(8,128)S(1)}, u32[]{:S(2)}, u32[]{:S(2)}) collective-permute-start(f32[3,24,128]{2,1,0:T(8,128)S(1)} %get-tuple-element.22), channel_id=1, source_target_pairs={{0,1},{1,2},{2,3},{3,4},{4,5},{5,6},{6,7},{7,8},{8,9},{9,10},{10,1... | collective-permute-start | bytes 110600 | tf_op jit(solution)/shard_map/ppermute | solution.py:405
  28.4 1.3 %collective-permute-start.5 = (f32[3,24,128]{2,1,0:T(8,128)S(1)}, f32[3,24,128]{2,1,0:T(8,128)S(1)}, u32[]{:S(2)}, u32[]{:S(2)}) collective-permute-start(f32[3,24,128]{2,1,0:T(8,128)S(1)} %get-tuple-element.23), channel_id=1, source_target_pairs={{1,0},{2,1},{3,2},{4,3},{5,4},{6,5},{7,6},{8,7},{9,8},{10,9},{11,1... | collective-permute-start | bytes 110600 | tf_op jit(solution)/shard_map/ppermute | solution.py:405
  29.7 0.1 stack.29
  29.8 0.1 broadcast_in_dim.4.flags
  29.9 1.4 %inner_lanes.1 = (f32[4,3,8,16,128]{4,3,2,1,0:T(8,128)S(1)}, f32[3,6,2,8,128]{4,3,2,1,0:T(8,128)S(1)}, f32[3,4,24,128]{3,2,1,0:T(8,128)S(1)}) custom-call(f32[8,128]{1,0:T(8,128)S(1)} %broadcast_in_dim.4.flags, f32[3,16,24,128]{3,2,1,0:T(8,128)S(1)} %get-tuple-element.20.whole), custom_call_target="tpu_custom_call" | custom-call | tf_op jit(solution)/shard_map/inner_lanes/pallas_call | solution.py:390
  31.3 0.0 collective-permute-done.4.low
  31.3 2.4 %collective-permute-done.5.high = f32[3,24,128]{2,1,0:T(8,128)S(1)} collective-permute-done((f32[3,24,128]{2,1,0:T(8,128)S(1)}, f32[3,24,128]{2,1,0:T(8,128)S(1)}, u32[]{:S(2)}, u32[]{:S(2)}) %collective-permute-start.5) | collective-permute-done | bytes 36896 | tf_op jit(solution)/shard_map/ppermute | solution.py:405
  33.7 1.1 %edge_lanes.1 = (f32[4,3,4,16,128]{4,3,2,1,0:T(8,128)S(1)}, f32[64,128]{1,0:T(8,128)S(1)}) custom-call(f32[8,128]{1,0:T(8,128)S(1)} %broadcast_in_dim.4.flags, f32[3,4,24,128]{3,2,1,0:T(8,128)S(1)} %get-tuple-element.21.edge, f32[3,24,128]{2,1,0:T(8,128)S(1)} %collective-permute-done.4.low, f32[3,24,128]{2,1,0:T(8,128)S(1)} %collective-permute-done.5.high, ...), custom_call_target="tpu_custom_call" | custom-call | tf_op jit(solution)/shard_map/edge_lanes/pallas_call | solution.py:390
  34.9 18.3 %all_to_all.22 = f32[64,1,128]{2,1,0:T(1,128)S(1)} all-to-all(f32[64,1,128]{2,1,0:T(1,128)S(1)} %bitcast.17), channel_id=1, replica_groups=mesh['gx_0'=2,'gx_1'=2,'gy_0'=4,'gy_1'=4,'gz'=12] {'gx_0','gx_1','gy_0',..., dimensions={0} | all-to-all | bytes 65536 | tf_op jit(solution)/shard_map/all_to_all | solution.py:409
  53.2 0.2 fold.1
  53.4 0.6 copy.5
  54.0 0.0 copy-start
  54.0 15.0 %all-to-all-start.1 = ((f32[12,1,128]{2,1,0:T(1,128)}), f32[12,1,128]{2,1,0:T(1,128)S(1)}, u32[]{:S(2)}, u32[]{:S(2)}) async-start(f32[12,1,128]{2,1,0:T(1,128)} %copy.5), calls=%async_computation.1 | async-start | bytes 12288 | tf_op jit(solution)/shard_map/all_to_all | solution.py:409
  68.9 0.0 copy-done
  69.0 8.8 %all-to-all-done.1 = f32[12,1,128]{2,1,0:T(1,128)S(1)} async-done(((f32[12,1,128]{2,1,0:T(1,128)}), f32[12,1,128]{2,1,0:T(1,128)S(1)}, u32[]{:S(2)}, u32[]{:S(2)}) %all-to-all-start.1) | async-done | bytes 6176 | tf_op jit(solution)/shard_map/all_to_all | solution.py:409
  77.8 1.3 %combine.1 = (f32[3,8,16,128]{3,2,1,0:T(8,128)}, f32[3,8,16,128]{3,2,1,0:T(8,128)}) custom-call(f32[12,128]{1,0:T(8,128)S(1)} %bitcast.15, f32[8,128]{1,0:T(8,128)S(1)} %broadcast_in_dim.5.scale, f32[4,3,8,16,128]{4,3,2,1,0:T(8,128)S(1)} %get-tuple-element.26.powers, f32[4,3,4,16,128]{4,3,2,1,0:T(8,128)S(1)} %get-tuple-element.27.edges), custom_call_target="tpu_custom_call" | custom-call | tf_op jit(solution)/shard_map/combine/pallas_call | solution.py:390
  (6 shorter events, 0.0 us)
Async XLA Ops:
  1.6 6.3 %collective-permute-start = (f32[3,4,8,128]{3,2,1,0:T(8,128)S(1)}, f32[3,4,8,128]{3,2,1,0:T(8,128)S(1)}, u32[]{:S(2)}, u32[]{:S(2)}) collective-permute-start(f32[3,4,8,128]{3,2,1,0:T(8,128)S(1)} %get-tuple-element.16), channel_id=1, source_target_pairs={{0,12},{12,24},{24,36},{36,48},{48,60},{60,72},{72,84},{84,96},{96... | collective-permute-start | bytes 147464 | tf_op jit(solution)/shard_map/ppermute | solution.py:405
  6.6 7.4 %collective-permute-start.1 = (f32[3,4,8,128]{3,2,1,0:T(8,128)S(1)}, f32[3,4,8,128]{3,2,1,0:T(8,128)S(1)}, u32[]{:S(2)}, u32[]{:S(2)}) collective-permute-start(f32[3,4,8,128]{3,2,1,0:T(8,128)S(1)} %get-tuple-element.17), channel_id=1, source_target_pairs={{12,0},{24,12},{36,24},{48,36},{60,48},{72,60},{84,72},{96,84},{10... | collective-permute-start | bytes 147464 | tf_op jit(solution)/shard_map/ppermute | solution.py:405
  14.1 9.4 %collective-permute-start.2 = (f32[3,11,8,128]{3,2,1,0:T(8,128)S(1)}, f32[3,11,8,128]{3,2,1,0:T(8,128)S(1)}, u32[]{:S(2)}, u32[]{:S(2)}) collective-permute-start(f32[3,11,8,128]{3,2,1,0:T(8,128)S(1)} %get-tuple-element.18), channel_id=1, source_target_pairs={{0,192},{192,384},{384,576},{1,193},{193,385},{385,577},{2,194},{1... | collective-permute-start | bytes 405512 | tf_op jit(solution)/shard_map/ppermute | solution.py:405
  17.6 6.9 %collective-permute-start.3 = (f32[3,11,8,128]{3,2,1,0:T(8,128)S(1)}, f32[3,11,8,128]{3,2,1,0:T(8,128)S(1)}, u32[]{:S(2)}, u32[]{:S(2)}) collective-permute-start(f32[3,11,8,128]{3,2,1,0:T(8,128)S(1)} %get-tuple-element.19), channel_id=1, source_target_pairs={{192,0},{384,192},{576,384},{193,1},{385,193},{577,385},{194,2},{3... | collective-permute-start | bytes 405512 | tf_op jit(solution)/shard_map/ppermute | solution.py:405
  24.8 6.5 %collective-permute-start.4 = (f32[3,24,128]{2,1,0:T(8,128)S(1)}, f32[3,24,128]{2,1,0:T(8,128)S(1)}, u32[]{:S(2)}, u32[]{:S(2)}) collective-permute-start(f32[3,24,128]{2,1,0:T(8,128)S(1)} %get-tuple-element.22), channel_id=1, source_target_pairs={{0,1},{1,2},{2,3},{3,4},{4,5},{5,6},{6,7},{7,8},{8,9},{9,10},{10,1... | collective-permute-start | bytes 110600 | tf_op jit(solution)/shard_map/ppermute | solution.py:405
  28.4 5.3 %collective-permute-start.5 = (f32[3,24,128]{2,1,0:T(8,128)S(1)}, f32[3,24,128]{2,1,0:T(8,128)S(1)}, u32[]{:S(2)}, u32[]{:S(2)}) collective-permute-start(f32[3,24,128]{2,1,0:T(8,128)S(1)} %get-tuple-element.23), channel_id=1, source_target_pairs={{1,0},{2,1},{3,2},{4,3},{5,4},{6,5},{7,6},{8,7},{9,8},{10,9},{11,1... | collective-permute-start | bytes 110600 | tf_op jit(solution)/shard_map/ppermute | solution.py:405
  54.0 15.0 %copy-start = (f32[3]{0:T(128)S(1)}, f32[3]{0:T(128)}, u32[]{:S(2)}) copy-start(f32[3]{0:T(128)} %param.3) | copy-start | bytes 40
  54.0 23.8 %all-to-all-start.1 = ((f32[12,1,128]{2,1,0:T(1,128)}), f32[12,1,128]{2,1,0:T(1,128)S(1)}, u32[]{:S(2)}, u32[]{:S(2)}) async-start(f32[12,1,128]{2,1,0:T(1,128)} %copy.5), calls=%async_computation.1 | async-start | bytes 12288 | tf_op jit(solution)/shard_map/all_to_all | solution.py:409

commit v5 on v4

--- a/solution.py
+++ b/solution.py
@@ -44,46 +44,71 @@
     return pltpu.roll(value, shift, value.ndim - 1) if shift else value
 
 
-def pack_y(block, own, up, down):
+def is_odd(axes):
+    return lax.axis_index(axes) % 2 == 1
+
+
+def pack_y(block, own, first, second):
+    odd = is_odd(GY)
+    sub = rows((8, NZ))
     own[...] = block[...]
     for c in range(3):
         for q in range(4):
-            up[c, q, 4:8, :] = block[c, q, NY - HALO : NY, :]
-            up[c, q, 0:4, :] = block[c, q + 4, NY - HALO : NY, :]
-            down[c, q, 0:4, :] = block[c, q, 0:HALO, :]
-            down[c, q, 4:8, :] = block[c, q + 4, 0:HALO, :]
-
-
-def beside_y(low, high, c, x):
+            up = jnp.where(sub >= 4, block[c, q, 8:16, :], pltpu.roll(block[c, q + 4, 8:16, :], 4, 0))
+            down = jnp.where(sub < 4, block[c, q, 0:8, :], pltpu.roll(block[c, q + 4, 0:8, :], 4, 0))
+            first[c, q] = jnp.where(odd, up, down)
+            second[c, q] = jnp.where(odd, down, up)
+
+
+def beside_y(odd, first, second, c, x):
+    low = jnp.where(odd, second[c, x % 4], first[c, x % 4])
+    high = jnp.where(odd, first[c, x % 4], second[c, x % 4])
     sub = rows((8, NZ))
     if x < 4:
-        return jnp.where(sub < 4, high[c, x], low[c, x])
-    return pltpu.roll(jnp.where(sub < 4, low[c, x - 4], high[c, x - 4]), 4, 0)
-
-
-def pack_x(own, low, high, up, down):
+        return jnp.where(sub < 4, high, low)
+    return pltpu.roll(jnp.where(sub < 4, low, high), 4, 0)
+
+
+def pack_x(own, low, high, first, second):
+    odd_y, odd = is_odd(GY), is_odd(GX)
+
+    def put(c, n, up, down):
+        first[c, n] = jnp.where(odd, up, down)
+        second[c, n] = jnp.where(odd, down, up)
+
     for c in range(3):
         for n in range(HALO):
             for t in range(2):
-                up[c, 2 * n + t] = own[c, NX - HALO + n, 8 * t : 8 * t + 8, :]
-                down[c, 2 * n + t] = own[c, n, 8 * t : 8 * t + 8, :]
+                part = slice(8 * t, 8 * t + 8)
+                put(c, 2 * n + t, own[c, NX - HALO + n, part, :], own[c, n, part, :])
         for n in range(HALO - 1):
-            up[c, 8 + n] = beside_y(low, high, c, NX - HALO + 1 + n)
-            down[c, 8 + n] = beside_y(low, high, c, n)
-
-
-def pack_z(own, low, high, below, above, whole, up, down):
+            put(
+                c,
+                8 + n,
+                beside_y(odd_y, low, high, c, NX - HALO + 1 + n),
+                beside_y(odd_y, low, high, c, n),
+            )
+
+
+def pack_z(own, first_y, second_y, first_x, second_x, whole, up, down):
+    odd_y, odd = is_odd(GY), is_odd(GX)
     lane = lanes((8, NZ))
     zero = jnp.zeros((8, NZ), jnp.float32)
 
     def tile_of(c, i, t):
         if i < NX:
-            return own[c, i, 8 * t : 8 * t + 8, :] if t < 2 else beside_y(low, high, c, i)
+            return own[c, i, 8 * t : 8 * t + 8, :] if t < 2 else beside_y(odd_y, first_y, second_y, c, i)
         n = i - NX
         if n < HALO:
-            return above[c, 2 * n + t] if t < 2 else (above[c, 8 + n] if n < HALO - 1 else zero)
+            if t == 2 and n == HALO - 1:
+                return zero
+            k = 2 * n + t if t < 2 else 8 + n
+            return jnp.where(odd, first_x[c, k], second_x[c, k])
         n -= HALO
-        return below[c, 2 * n + t] if t < 2 else (below[c, 7 + n] if n > 0 else zero)
+        if t == 2 and n == 0:
+            return zero
+        k = 2 * n + t if t < 2 else 7 + n
+        return jnp.where(odd, second_x[c, k], first_x[c, k])
 
     for c in range(3):
         for t in range(3):
@@ -353,7 +378,7 @@
     return in_powers_of_l(total), in_powers_of_l(residual)
 
 
-def combine(parts, scale, powers, edges, total, rest):
+def combine(parts, flags, powers, edges, total, rest):
     lane = lanes((8, NZ))
     high, low = folded(lambda first, size: parts[first : first + size, :], parts.shape[0])
     moments = [(turned(high, -3 * k), turned(low, -3 * k)) for k in range(MOMENTS)]
@@ -361,7 +386,7 @@
     def spread(value, c):
         return jnp.broadcast_to(jnp.sum(jnp.where(lane == c, value, 0.0), axis=1, keepdims=True), (8, NZ))
 
-    for out, weights in zip((total, rest), weights_of(moments, jnp.broadcast_to(scale[0:1, :], (8, NZ)))):
+    for out, weights in zip((total, rest), weights_of(moments, jnp.broadcast_to(flags[6:7, :], (8, NZ)))):
         for c in range(3):
             factors = [spread(w, c) for w in weights]
 
@@ -405,19 +430,29 @@
     return lax.ppermute(up, axis, steps), lax.ppermute(down, axis, [(b, a) for a, b in steps])
 
 
+def swapped(first, second, axis):
+    size = lax.axis_size(axis)
+
+    def pairs_from(start):
+        up = [(i, i + 1) for i in range(start, size - 1, 2)]
+        return up + [(b, a) for a, b in up]
+
+    return lax.ppermute(first, axis, pairs_from(1)), lax.ppermute(second, axis, pairs_from(0))
+
+
 def gathered(row, axes):
     return lax.all_to_all(row, axes, 0, 0, tiled=True)
 
 
 def body(velocity, diffusion):
     ends = [f for a in (GX, GY, GZ) for f in (lax.axis_index(a) > 0, lax.axis_index(a) + 1 < lax.axis_size(a))]
-    flags = jnp.broadcast_to(jnp.stack(ends + ends[:2]).astype(jnp.float32)[:, None], (8, NZ))
-    scale = jnp.broadcast_to(jnp.pad(6.0 * diffusion, (0, NZ - 3))[None], (8, NZ))
+    flags = jnp.broadcast_to(jnp.stack(ends).astype(jnp.float32)[:, None], (6, NZ))
+    flags = jnp.concatenate([flags, jnp.broadcast_to(jnp.pad(6.0 * diffusion, (0, NZ - 3))[None], (2, NZ))])
     block, wide, tiles = (3, NX, NY, NZ), (3, EX, EY, NZ), (3, GROUPS, EY, NZ)
     own, up, down = kernel(pack_y, [block] + [(3, 4, 8, NZ)] * 2, first=True)(velocity)
-    low, high = exchanged(up, down, GY)
+    low, high = swapped(up, down, GY)
     up, down = kernel(pack_x, [(3, 11, 8, NZ)] * 2)(own, low, high)
-    below, above = exchanged(up, down, GX)
+    below, above = swapped(up, down, GX)
     whole, up, down = kernel(pack_z, [wide, (3, EY, NZ), (3, EY, NZ)])(own, low, high, below, above)
     low, high = exchanged(up, down, GZ)
     powers, sums, edge = kernel(
@@ -428,7 +463,7 @@
         edge_lanes, [(ITERS + 1, 3, GROUPS, NY, NZ), (planes, NZ)], [tiles] * (ITERS + 1)
     )(flags, edge, low, high, sums)
     (row,) = kernel(fold, [(stack, NZ)])(gathered(row, GX + GY))
-    return kernel(combine, [block] * 2, last=True)(gathered(row, GZ), scale, powers, edges)
+    return kernel(combine, [block] * 2, last=True)(gathered(row, GZ), flags, powers, edges)
 
 
 def solution(mesh):

time: 79.5 us -> 75.6 us (0.951)
  blocking collectives: 18.3 us -> 42 us
  starting transfers between devices: 35.5 us -> 21.6 us
  waiting for transfers between devices: 18.3 us -> 5.31 us
    all_to_all x1 -> x2, blocking collectives: 18.3 us -> 42 us  [gathered(): return lax.all_to_all(row, axes, 0, 0, tiled=True)]
    ppermute x0 -> x4, starting transfers between devices: none -> 18.6 us  [the longest x2 14.4 us: swapped(): lax.ppermute(second, axis, pairs_from(0))]
    all_to_all x1 -> x0, starting transfers between devices: 15 us -> none  [gathered(): return lax.all_to_all(row, axes, 0, 0, tiled=True)]
    ppermute x3 -> x1, starting transfers between devices: 12.1 us -> 1.72 us  [exchanged(): lax.ppermute(up, axis, steps)]
    all_to_all x1 -> x0, waiting for transfers between devices: 8.84 us -> none  [gathered(): return lax.all_to_all(row, axes, 0, 0, tiled=True)]
    ppermute x3 -> x1, starting transfers between devices: 8.48 us -> 1.29 us  [exchanged(): lax.ppermute(down, axis, [(b, a) for a, b in steps])]
    ppermute x3 -> x1, waiting for transfers between devices: 9.48 us -> 2.54 us  [exchanged(): lax.ppermute(down, axis, [(b, a) for a, b in steps])]
    ppermute x0 -> x4, waiting for transfers between devices: none -> 2.77 us  [the longest x2 2.76 us: swapped(): lax.ppermute(second, axis, pairs_from(0))]
  transfers between devices with their start and end apart: 7 -> 6, of which waited for: 4 -> 3; matrix products, arithmetic and copies ran while one was open for 0% -> 0% of each run, Pallas kernels for 2% -> 2%
where the time goes in v5:
time: 75.6 us; the launch traced here: 75.3 us
  blocking collectives  42 us (56%)
  starting transfers between devices  21.6 us (29%)
  Pallas kernels  5.37 us (7%)
  waiting for transfers between devices  5.31 us (7%)
  between operations  0.79 us (1%)
    all_to_all x2, blocking collectives, gathered(): return lax.all_to_all(row, axes, 0, 0, tiled=True)  42 us
    ppermute x2, starting transfers between devices, swapped(): lax.ppermute(second, axis, pairs_from(0))  14.4 us
    pallas_call x7, Pallas kernels, call(): pl.pallas_call(body, in_specs=[vmem] * len(args), out_specs=[vmem] * len(...  5.37 us
    ppermute x2, starting transfers between devices, swapped(): lax.ppermute(first, axis, pairs_from(1))  4.15 us
    ppermute x2, waiting for transfers between devices, swapped(): lax.ppermute(second, axis, pairs_from(0))  2.76 us
    ppermute x1, waiting for transfers between devices, exchanged(): lax.ppermute(down, axis, [(b, a) for a, b in steps])  2.54 us
    ppermute x1, starting transfers between devices, exchanged(): lax.ppermute(up, axis, steps)  1.72 us
  transfers between devices with their start and end apart: 6, of which 3 were waited for; matrix products, arithmetic and copies ran while one was open for 0% of the time, Pallas kernels for 2%

profile of v5, /device:TPU:1, one launch (start us, length us, event | category | flops | bytes accessed | tf_op | source)
XLA Modules:
  0.0 75.3 jit_solution(5288433424831062473)
XLA Ops:
  0.6 1.0 %pack_y.1 = (f32[3,8,16,128]{3,2,1,0:T(8,128)S(1)}, f32[3,4,8,128]{3,2,1,0:T(8,128)S(1)}, f32[3,4,8,128]{3,2,1,0:T(8,128)S(1)}) custom-call(f32[3,8,16,128]{3,2,1,0:T(8,128)} %block.1), custom_call_target="tpu_custom_call" | custom-call | tf_op jit(solution)/shard_map/pack_y/pallas_call | solution.py:415
  1.6 0.7 collective-permute-start
  2.3 9.8 %collective-permute-start.1 = (f32[3,4,8,128]{3,2,1,0:T(8,128)S(1)}, f32[3,4,8,128]{3,2,1,0:T(8,128)S(1)}, u32[]{:S(2)}, u32[]{:S(2)}) collective-permute-start(f32[3,4,8,128]{3,2,1,0:T(8,128)S(1)} %get-tuple-element.17), channel_id=1, source_target_pairs={{0,12},{24,36},{48,60},{72,84},{96,108},{120,132},{144,156},{168,1... | collective-permute-start | bytes 147464 | tf_op jit(solution)/shard_map/ppermute | solution.py:440
  12.1 0.1 stack.27
  12.2 0.0 collective-permute-done.low.first_y
  12.2 1.8 %collective-permute-done.1.high.second_y = f32[3,4,8,128]{3,2,1,0:T(8,128)S(1)} collective-permute-done((f32[3,4,8,128]{3,2,1,0:T(8,128)S(1)}, f32[3,4,8,128]{3,2,1,0:T(8,128)S(1)}, u32[]{:S(2)}, u32[]{:S(2)}) %collective-permute-start.1) | collective-permute-done | bytes 49184 | tf_op jit(solution)/shard_map/ppermute | solution.py:440
  14.1 0.0 copy-start
  14.1 3.5 %collective-permute-start.2 = (f32[3,11,8,128]{3,2,1,0:T(8,128)S(1)}, f32[3,11,8,128]{3,2,1,0:T(8,128)S(1)}, u32[]{:S(2)}, u32[]{:S(2)}) collective-permute-start(f32[3,11,8,128]{3,2,1,0:T(8,128)S(1)} %get-tuple-element.18), channel_id=1, source_target_pairs={{192,384},{384,192},{193,385},{385,193},{194,386},{386,194},{195,3... | collective-permute-start | bytes 405512 | tf_op jit(solution)/shard_map/ppermute | solution.py:440
  17.6 4.6 %collective-permute-start.3 = (f32[3,11,8,128]{3,2,1,0:T(8,128)S(1)}, f32[3,11,8,128]{3,2,1,0:T(8,128)S(1)}, u32[]{:S(2)}, u32[]{:S(2)}) collective-permute-start(f32[3,11,8,128]{3,2,1,0:T(8,128)S(1)} %get-tuple-element.19), channel_id=1, source_target_pairs={{0,192},{384,576},{192,0},{576,384},{1,193},{385,577},{193,1},{577... | collective-permute-start | bytes 405512 | tf_op jit(solution)/shard_map/ppermute | solution.py:440
  22.3 0.0 copy-done
  22.3 0.0 collective-permute-done.2.first_x
  22.3 0.9 %collective-permute-done.3.second_x = f32[3,11,8,128]{3,2,1,0:T(8,128)S(1)} collective-permute-done((f32[3,11,8,128]{3,2,1,0:T(8,128)S(1)}, f32[3,11,8,128]{3,2,1,0:T(8,128)S(1)}, u32[]{:S(2)}, u32[]{:S(2)}) %collective-permute-start.3) | collective-permute-done | bytes 135200 | tf_op jit(solution)/shard_map/ppermute | solution.py:440
  23.2 0.4 pack_z.1
  23.6 1.7 %collective-permute-start.4 = (f32[3,24,128]{2,1,0:T(8,128)S(1)}, f32[3,24,128]{2,1,0:T(8,128)S(1)}, u32[]{:S(2)}, u32[]{:S(2)}) collective-permute-start(f32[3,24,128]{2,1,0:T(8,128)S(1)} %get-tuple-element.22), channel_id=1, source_target_pairs={{0,1},{1,2},{2,3},{3,4},{4,5},{5,6},{6,7},{7,8},{8,9},{9,10},{10,1... | collective-permute-start | bytes 110600 | tf_op jit(solution)/shard_map/ppermute | solution.py:430
  25.3 1.3 %collective-permute-start.5 = (f32[3,24,128]{2,1,0:T(8,128)S(1)}, f32[3,24,128]{2,1,0:T(8,128)S(1)}, u32[]{:S(2)}, u32[]{:S(2)}) collective-permute-start(f32[3,24,128]{2,1,0:T(8,128)S(1)} %get-tuple-element.23), channel_id=1, source_target_pairs={{1,0},{2,1},{3,2},{4,3},{5,4},{6,5},{7,6},{8,7},{9,8},{10,9},{11,1... | collective-permute-start | bytes 110600 | tf_op jit(solution)/shard_map/ppermute | solution.py:430
  26.6 0.1 pad_maximum_fusion.flags
  26.7 1.4 %inner_lanes.1 = (f32[4,3,8,16,128]{4,3,2,1,0:T(8,128)S(1)}, f32[3,6,2,8,128]{4,3,2,1,0:T(8,128)S(1)}, f32[3,4,24,128]{3,2,1,0:T(8,128)S(1)}) custom-call(f32[8,128]{1,0:T(8,128)S(1)} %pad_maximum_fusion.flags, f32[3,16,24,128]{3,2,1,0:T(8,128)S(1)} %get-tuple-element.20.whole), custom_call_target="tpu_custom_call" | custom-call | tf_op jit(solution)/shard_map/inner_lanes/pallas_call | solution.py:415
  28.1 0.0 collective-permute-done.4.low
  28.1 2.5 %collective-permute-done.5.high = f32[3,24,128]{2,1,0:T(8,128)S(1)} collective-permute-done((f32[3,24,128]{2,1,0:T(8,128)S(1)}, f32[3,24,128]{2,1,0:T(8,128)S(1)}, u32[]{:S(2)}, u32[]{:S(2)}) %collective-permute-start.5) | collective-permute-done | bytes 36896 | tf_op jit(solution)/shard_map/ppermute | solution.py:430
  30.7 1.1 %edge_lanes.1 = (f32[4,3,4,16,128]{4,3,2,1,0:T(8,128)S(1)}, f32[64,128]{1,0:T(8,128)S(1)}) custom-call(f32[8,128]{1,0:T(8,128)S(1)} %pad_maximum_fusion.flags, f32[3,4,24,128]{3,2,1,0:T(8,128)S(1)} %get-tuple-element.21.edge, f32[3,24,128]{2,1,0:T(8,128)S(1)} %collective-permute-done.4.low, f32[3,24,128]{2,1,0:T(8,128)S(1)} %collective-permute-done.5.high, ...), custom_call_target="tpu_custom_call" | custom-call | tf_op jit(solution)/shard_map/edge_lanes/pallas_call | solution.py:415
  31.8 18.4 %all_to_all.22 = f32[64,1,128]{2,1,0:T(1,128)S(1)} all-to-all(f32[64,1,128]{2,1,0:T(1,128)S(1)} %bitcast.17), channel_id=1, replica_groups=mesh['gx_0'=2,'gx_1'=2,'gy_0'=4,'gy_1'=4,'gz'=12] {'gx_0','gx_1','gy_0',..., dimensions={0} | all-to-all | bytes 65536 | tf_op jit(solution)/shard_map/all_to_all | solution.py:444
  50.2 0.2 fold.1
  50.4 23.6 %all_to_all.23 = f32[12,1,128]{2,1,0:T(1,128)S(1)} all-to-all(f32[12,1,128]{2,1,0:T(1,128)S(1)} %copy.5), channel_id=1, replica_groups=mesh['gx_0'=2,'gx_1'=2,'gy_0'=4,'gy_1'=4,'gz'=12] {'gz'}, dimensions={0} | all-to-all | bytes 12288 | tf_op jit(solution)/shard_map/all_to_all | solution.py:444
  74.0 1.3 %combine.1 = (f32[3,8,16,128]{3,2,1,0:T(8,128)}, f32[3,8,16,128]{3,2,1,0:T(8,128)}) custom-call(f32[12,128]{1,0:T(8,128)S(1)} %bitcast.15, f32[8,128]{1,0:T(8,128)S(1)} %pad_maximum_fusion.flags, f32[4,3,8,16,128]{4,3,2,1,0:T(8,128)S(1)} %get-tuple-element.26.powers, f32[4,3,4,16,128]{4,3,2,1,0:T(8,128)S(1)} %get-tuple-element.27.edges), custom_call_target="tpu_custom_call" | custom-call | tf_op jit(solution)/shard_map/combine/pallas_call | solution.py:415
  (8 shorter events, 0.1 us)
Async XLA Ops:
  1.6 10.6 %collective-permute-start = (f32[3,4,8,128]{3,2,1,0:T(8,128)S(1)}, f32[3,4,8,128]{3,2,1,0:T(8,128)S(1)}, u32[]{:S(2)}, u32[]{:S(2)}) collective-permute-start(f32[3,4,8,128]{3,2,1,0:T(8,128)S(1)} %get-tuple-element.16), channel_id=1, source_target_pairs={{12,24},{36,48},{60,72},{84,96},{108,120},{132,144},{156,168},{24,... | collective-permute-start | bytes 147464 | tf_op jit(solution)/shard_map/ppermute | solution.py:440
  2.3 11.8 %collective-permute-start.1 = (f32[3,4,8,128]{3,2,1,0:T(8,128)S(1)}, f32[3,4,8,128]{3,2,1,0:T(8,128)S(1)}, u32[]{:S(2)}, u32[]{:S(2)}) collective-permute-start(f32[3,4,8,128]{3,2,1,0:T(8,128)S(1)} %get-tuple-element.17), channel_id=1, source_target_pairs={{0,12},{24,36},{48,60},{72,84},{96,108},{120,132},{144,156},{168,1... | collective-permute-start | bytes 147464 | tf_op jit(solution)/shard_map/ppermute | solution.py:440
  14.1 8.2 %copy-start = (f32[3]{0:T(128)S(1)}, f32[3]{0:T(128)}, u32[]{:S(2)}) copy-start(f32[3]{0:T(128)} %param.3) | copy-start | bytes 40
  14.1 8.2 %collective-permute-start.2 = (f32[3,11,8,128]{3,2,1,0:T(8,128)S(1)}, f32[3,11,8,128]{3,2,1,0:T(8,128)S(1)}, u32[]{:S(2)}, u32[]{:S(2)}) collective-permute-start(f32[3,11,8,128]{3,2,1,0:T(8,128)S(1)} %get-tuple-element.18), channel_id=1, source_target_pairs={{192,384},{384,192},{193,385},{385,193},{194,386},{386,194},{195,3... | collective-permute-start | bytes 405512 | tf_op jit(solution)/shard_map/ppermute | solution.py:440
  17.6 5.6 %collective-permute-start.3 = (f32[3,11,8,128]{3,2,1,0:T(8,128)S(1)}, f32[3,11,8,128]{3,2,1,0:T(8,128)S(1)}, u32[]{:S(2)}, u32[]{:S(2)}) collective-permute-start(f32[3,11,8,128]{3,2,1,0:T(8,128)S(1)} %get-tuple-element.19), channel_id=1, source_target_pairs={{0,192},{384,576},{192,0},{576,384},{1,193},{385,577},{193,1},{577... | collective-permute-start | bytes 405512 | tf_op jit(solution)/shard_map/ppermute | solution.py:440
  23.6 4.5 %collective-permute-start.4 = (f32[3,24,128]{2,1,0:T(8,128)S(1)}, f32[3,24,128]{2,1,0:T(8,128)S(1)}, u32[]{:S(2)}, u32[]{:S(2)}) collective-permute-start(f32[3,24,128]{2,1,0:T(8,128)S(1)} %get-tuple-element.22), channel_id=1, source_target_pairs={{0,1},{1,2},{2,3},{3,4},{4,5},{5,6},{6,7},{7,8},{8,9},{9,10},{10,1... | collective-permute-start | bytes 110600 | tf_op jit(solution)/shard_map/ppermute | solution.py:430
  25.3 5.3 %collective-permute-start.5 = (f32[3,24,128]{2,1,0:T(8,128)S(1)}, f32[3,24,128]{2,1,0:T(8,128)S(1)}, u32[]{:S(2)}, u32[]{:S(2)}) collective-permute-start(f32[3,24,128]{2,1,0:T(8,128)S(1)} %get-tuple-element.23), channel_id=1, source_target_pairs={{1,0},{2,1},{3,2},{4,3},{5,4},{6,5},{7,6},{8,7},{9,8},{10,9},{11,1... | collective-permute-start | bytes 110600 | tf_op jit(solution)/shard_map/ppermute | solution.py:430

commit v6 on v5

--- a/solution.py
+++ b/solution.py
@@ -441,6 +441,8 @@
 
 
 def gathered(row, axes):
+    if row.shape[0] == 1:
+        return lax.all_gather(row, axes, axis=0, tiled=True)
     return lax.all_to_all(row, axes, 0, 0, tiled=True)
 
 
@@ -458,11 +460,11 @@
     powers, sums, edge = kernel(
         inner_lanes, [(ITERS + 1,) + block, (3, MOMENTS, 2, 8, NZ), tiles], [wide] * ITERS
     )(flags, whole)
-    planes, stack = lax.axis_size(GX + GY), lax.axis_size(GZ)
+    planes = lax.axis_size(GX + GY)
     edges, row = kernel(
         edge_lanes, [(ITERS + 1, 3, GROUPS, NY, NZ), (planes, NZ)], [tiles] * (ITERS + 1)
     )(flags, edge, low, high, sums)
-    (row,) = kernel(fold, [(stack, NZ)])(gathered(row, GX + GY))
+    (row,) = kernel(fold, [(1, NZ)])(gathered(row, GX + GY))
     return kernel(combine, [block] * 2, last=True)(gathered(row, GZ), flags, powers, edges)
 
 

time: 75.6 us -> 79.5 us (1.052)
  the two profiles are of different devices: /device:TPU:1 before, /device:TPU:8 now
where the time goes in v6:
time: 79.5 us; the launch traced here: 79.2 us
  blocking collectives  46.3 us (58%)
  starting transfers between devices  19 us (24%)
  waiting for transfers between devices  7.61 us (10%)
  Pallas kernels  5.37 us (7%)
    all_gather x1, blocking collectives, gathered(): return lax.all_gather(row, axes, axis=0, tiled=True)  29.3 us
    all_to_all x1, blocking collectives, gathered(): return lax.all_to_all(row, axes, 0, 0, tiled=True)  17 us
    ppermute x2, starting transfers between devices, swapped(): lax.ppermute(second, axis, pairs_from(0))  10.6 us
    pallas_call x7, Pallas kernels, call(): pl.pallas_call(body, in_specs=[vmem] * len(args), out_specs=[vmem] * len(...  5.37 us
    ppermute x1, starting transfers between devices, exchanged(): lax.ppermute(up, axis, steps)  4.38 us
    ppermute x1, waiting for transfers between devices, exchanged(): lax.ppermute(down, axis, [(b, a) for a, b in steps])  3.41 us
    ppermute x2, starting transfers between devices, swapped(): lax.ppermute(first, axis, pairs_from(1))  2.74 us
    ppermute x2, waiting for transfers between devices, swapped(): lax.ppermute(first, axis, pairs_from(1))  2.29 us
  transfers between devices with their start and end apart: 6, of which 3 were waited for; matrix products, arithmetic and copies ran while one was open for 0% of the time, Pallas kernels for 2%

profile of v6, /device:TPU:8, one launch (start us, length us, event | category | flops | bytes accessed | tf_op | source)
XLA Modules:
  0.0 79.2 jit_solution(4957329411426916923)
XLA Ops:
  0.6 1.0 %pack_y.1 = (f32[3,8,16,128]{3,2,1,0:T(8,128)S(1)}, f32[3,4,8,128]{3,2,1,0:T(8,128)S(1)}, f32[3,4,8,128]{3,2,1,0:T(8,128)S(1)}) custom-call(f32[3,8,16,128]{3,2,1,0:T(8,128)} %block.1), custom_call_target="tpu_custom_call" | custom-call | tf_op jit(solution)/shard_map/pack_y/pallas_call | solution.py:415
  1.6 0.7 collective-permute-start
  2.3 8.6 %collective-permute-start.1 = (f32[3,4,8,128]{3,2,1,0:T(8,128)S(1)}, f32[3,4,8,128]{3,2,1,0:T(8,128)S(1)}, u32[]{:S(2)}, u32[]{:S(2)}) collective-permute-start(f32[3,4,8,128]{3,2,1,0:T(8,128)S(1)} %get-tuple-element.17), channel_id=1, source_target_pairs={{0,12},{24,36},{48,60},{72,84},{96,108},{120,132},{144,156},{168,1... | collective-permute-start | bytes 147464 | tf_op jit(solution)/shard_map/ppermute | solution.py:440
  10.9 0.1 stack.27
  11.1 0.0 collective-permute-done.low.first_y
  11.1 1.9 %collective-permute-done.1.high.second_y = f32[3,4,8,128]{3,2,1,0:T(8,128)S(1)} collective-permute-done((f32[3,4,8,128]{3,2,1,0:T(8,128)S(1)}, f32[3,4,8,128]{3,2,1,0:T(8,128)S(1)}, u32[]{:S(2)}, u32[]{:S(2)}) %collective-permute-start.1) | collective-permute-done | bytes 49184 | tf_op jit(solution)/shard_map/ppermute | solution.py:440
  13.0 0.0 copy-start
  13.0 2.1 %collective-permute-start.2 = (f32[3,11,8,128]{3,2,1,0:T(8,128)S(1)}, f32[3,11,8,128]{3,2,1,0:T(8,128)S(1)}, u32[]{:S(2)}, u32[]{:S(2)}) collective-permute-start(f32[3,11,8,128]{3,2,1,0:T(8,128)S(1)} %get-tuple-element.18), channel_id=1, source_target_pairs={{192,384},{384,192},{193,385},{385,193},{194,386},{386,194},{195,3... | collective-permute-start | bytes 405512 | tf_op jit(solution)/shard_map/ppermute | solution.py:440
  15.1 1.9 %collective-permute-start.3 = (f32[3,11,8,128]{3,2,1,0:T(8,128)S(1)}, f32[3,11,8,128]{3,2,1,0:T(8,128)S(1)}, u32[]{:S(2)}, u32[]{:S(2)}) collective-permute-start(f32[3,11,8,128]{3,2,1,0:T(8,128)S(1)} %get-tuple-element.19), channel_id=1, source_target_pairs={{0,192},{384,576},{192,0},{576,384},{1,193},{385,577},{193,1},{577... | collective-permute-start | bytes 405512 | tf_op jit(solution)/shard_map/ppermute | solution.py:440
  17.0 0.0 copy-done
  17.1 2.3 %collective-permute-done.2.first_x = f32[3,11,8,128]{3,2,1,0:T(8,128)S(1)} collective-permute-done((f32[3,11,8,128]{3,2,1,0:T(8,128)S(1)}, f32[3,11,8,128]{3,2,1,0:T(8,128)S(1)}, u32[]{:S(2)}, u32[]{:S(2)}) %collective-permute-start.2) | collective-permute-done | bytes 135200 | tf_op jit(solution)/shard_map/ppermute | solution.py:440
  19.4 0.0 collective-permute-done.3.second_x
  19.4 0.4 pack_z.1
  19.7 4.4 %collective-permute-start.4 = (f32[3,24,128]{2,1,0:T(8,128)S(1)}, f32[3,24,128]{2,1,0:T(8,128)S(1)}, u32[]{:S(2)}, u32[]{:S(2)}) collective-permute-start(f32[3,24,128]{2,1,0:T(8,128)S(1)} %get-tuple-element.22), channel_id=1, source_target_pairs={{0,1},{1,2},{2,3},{3,4},{4,5},{5,6},{6,7},{7,8},{8,9},{9,10},{10,1... | collective-permute-start | bytes 110600 | tf_op jit(solution)/shard_map/ppermute | solution.py:430
  24.1 1.3 %collective-permute-start.5 = (f32[3,24,128]{2,1,0:T(8,128)S(1)}, f32[3,24,128]{2,1,0:T(8,128)S(1)}, u32[]{:S(2)}, u32[]{:S(2)}) collective-permute-start(f32[3,24,128]{2,1,0:T(8,128)S(1)} %get-tuple-element.23), channel_id=1, source_target_pairs={{1,0},{2,1},{3,2},{4,3},{5,4},{6,5},{7,6},{8,7},{9,8},{10,9},{11,1... | collective-permute-start | bytes 110600 | tf_op jit(solution)/shard_map/ppermute | solution.py:430
  25.4 0.1 pad_maximum_fusion.flags
  25.5 1.4 %inner_lanes.1 = (f32[4,3,8,16,128]{4,3,2,1,0:T(8,128)S(1)}, f32[3,6,2,8,128]{4,3,2,1,0:T(8,128)S(1)}, f32[3,4,24,128]{3,2,1,0:T(8,128)S(1)}) custom-call(f32[8,128]{1,0:T(8,128)S(1)} %pad_maximum_fusion.flags, f32[3,16,24,128]{3,2,1,0:T(8,128)S(1)} %get-tuple-element.20.whole), custom_call_target="tpu_custom_call" | custom-call | tf_op jit(solution)/shard_map/inner_lanes/pallas_call | solution.py:415
  26.9 0.0 collective-permute-done.4.low
  26.9 3.4 %collective-permute-done.5.high = f32[3,24,128]{2,1,0:T(8,128)S(1)} collective-permute-done((f32[3,24,128]{2,1,0:T(8,128)S(1)}, f32[3,24,128]{2,1,0:T(8,128)S(1)}, u32[]{:S(2)}, u32[]{:S(2)}) %collective-permute-start.5) | collective-permute-done | bytes 36896 | tf_op jit(solution)/shard_map/ppermute | solution.py:430
  30.3 1.1 %edge_lanes.1 = (f32[4,3,4,16,128]{4,3,2,1,0:T(8,128)S(1)}, f32[64,128]{1,0:T(8,128)S(1)}) custom-call(f32[8,128]{1,0:T(8,128)S(1)} %pad_maximum_fusion.flags, f32[3,4,24,128]{3,2,1,0:T(8,128)S(1)} %get-tuple-element.21.edge, f32[3,24,128]{2,1,0:T(8,128)S(1)} %collective-permute-done.4.low, f32[3,24,128]{2,1,0:T(8,128)S(1)} %collective-permute-done.5.high, ...), custom_call_target="tpu_custom_call" | custom-call | tf_op jit(solution)/shard_map/edge_lanes/pallas_call | solution.py:415
  31.5 17.0 %all_to_all.11 = f32[64,1,128]{2,1,0:T(1,128)S(1)} all-to-all(f32[64,1,128]{2,1,0:T(1,128)S(1)} %bitcast.16), channel_id=1, replica_groups=mesh['gx_0'=2,'gx_1'=2,'gy_0'=4,'gy_1'=4,'gz'=12] {'gx_0','gx_1','gy_0',..., dimensions={0} | all-to-all | bytes 65536 | tf_op jit(solution)/shard_map/all_to_all | solution.py:446
  48.5 0.2 fold.1
  48.7 29.3 %all-gather = f32[12,1,128]{2,1,0:T(1,128)S(1)} all-gather(f32[1,1,128]{2,1,0:T(1,128)S(1)} %bitcast.17), channel_id=1, replica_groups=mesh['gx_0'=2,'gx_1'=2,'gy_0'=4,'gy_1'=4,'gz'=12] {'gz'}, dimensions={0}, use_global_device_ids=true | all-gather | bytes 6656 | tf_op jit(solution)/shard_map/all_gather | solution.py:445
  77.9 1.3 %combine.1 = (f32[3,8,16,128]{3,2,1,0:T(8,128)}, f32[3,8,16,128]{3,2,1,0:T(8,128)}) custom-call(f32[12,128]{1,0:T(8,128)S(1)} %bitcast.15, f32[8,128]{1,0:T(8,128)S(1)} %pad_maximum_fusion.flags, f32[4,3,8,16,128]{4,3,2,1,0:T(8,128)S(1)} %get-tuple-element.26.powers, f32[4,3,4,16,128]{4,3,2,1,0:T(8,128)S(1)} %get-tuple-element.27.edges), custom_call_target="tpu_custom_call" | custom-call | tf_op jit(solution)/shard_map/combine/pallas_call | solution.py:415
  (7 shorter events, 0.1 us)
Async XLA Ops:
  1.6 9.5 %collective-permute-start = (f32[3,4,8,128]{3,2,1,0:T(8,128)S(1)}, f32[3,4,8,128]{3,2,1,0:T(8,128)S(1)}, u32[]{:S(2)}, u32[]{:S(2)}) collective-permute-start(f32[3,4,8,128]{3,2,1,0:T(8,128)S(1)} %get-tuple-element.16), channel_id=1, source_target_pairs={{12,24},{36,48},{60,72},{84,96},{108,120},{132,144},{156,168},{24,... | collective-permute-start | bytes 147464 | tf_op jit(solution)/shard_map/ppermute | solution.py:440
  2.3 10.7 %collective-permute-start.1 = (f32[3,4,8,128]{3,2,1,0:T(8,128)S(1)}, f32[3,4,8,128]{3,2,1,0:T(8,128)S(1)}, u32[]{:S(2)}, u32[]{:S(2)}) collective-permute-start(f32[3,4,8,128]{3,2,1,0:T(8,128)S(1)} %get-tuple-element.17), channel_id=1, source_target_pairs={{0,12},{24,36},{48,60},{72,84},{96,108},{120,132},{144,156},{168,1... | collective-permute-start | bytes 147464 | tf_op jit(solution)/shard_map/ppermute | solution.py:440
  13.0 4.0 %copy-start = (f32[3]{0:T(128)S(1)}, f32[3]{0:T(128)}, u32[]{:S(2)}) copy-start(f32[3]{0:T(128)} %param.3) | copy-start | bytes 40
  13.0 6.3 %collective-permute-start.2 = (f32[3,11,8,128]{3,2,1,0:T(8,128)S(1)}, f32[3,11,8,128]{3,2,1,0:T(8,128)S(1)}, u32[]{:S(2)}, u32[]{:S(2)}) collective-permute-start(f32[3,11,8,128]{3,2,1,0:T(8,128)S(1)} %get-tuple-element.18), channel_id=1, source_target_pairs={{192,384},{384,192},{193,385},{385,193},{194,386},{386,194},{195,3... | collective-permute-start | bytes 405512 | tf_op jit(solution)/shard_map/ppermute | solution.py:440
  15.1 4.3 %collective-permute-start.3 = (f32[3,11,8,128]{3,2,1,0:T(8,128)S(1)}, f32[3,11,8,128]{3,2,1,0:T(8,128)S(1)}, u32[]{:S(2)}, u32[]{:S(2)}) collective-permute-start(f32[3,11,8,128]{3,2,1,0:T(8,128)S(1)} %get-tuple-element.19), channel_id=1, source_target_pairs={{0,192},{384,576},{192,0},{576,384},{1,193},{385,577},{193,1},{577... | collective-permute-start | bytes 405512 | tf_op jit(solution)/shard_map/ppermute | solution.py:440
  19.7 7.2 %collective-permute-start.4 = (f32[3,24,128]{2,1,0:T(8,128)S(1)}, f32[3,24,128]{2,1,0:T(8,128)S(1)}, u32[]{:S(2)}, u32[]{:S(2)}) collective-permute-start(f32[3,24,128]{2,1,0:T(8,128)S(1)} %get-tuple-element.22), channel_id=1, source_target_pairs={{0,1},{1,2},{2,3},{3,4},{4,5},{5,6},{6,7},{7,8},{8,9},{9,10},{10,1... | collective-permute-start | bytes 110600 | tf_op jit(solution)/shard_map/ppermute | solution.py:430
  24.1 6.2 %collective-permute-start.5 = (f32[3,24,128]{2,1,0:T(8,128)S(1)}, f32[3,24,128]{2,1,0:T(8,128)S(1)}, u32[]{:S(2)}, u32[]{:S(2)}) collective-permute-start(f32[3,24,128]{2,1,0:T(8,128)S(1)} %get-tuple-element.23), channel_id=1, source_target_pairs={{1,0},{2,1},{3,2},{4,3},{5,4},{6,5},{7,6},{8,7},{9,8},{10,9},{11,1... | collective-permute-start | bytes 110600 | tf_op jit(solution)/shard_map/ppermute | solution.py:430

commit v7 on v5

--- a/solution.py
+++ b/solution.py
@@ -21,6 +21,7 @@
 GROUPS = 4
 STEP = NZ // GROUPS
 MOMENTS = 2 * ITERS
+Z_TILES = 5
 
 
 def lanes(shape):
@@ -69,7 +70,7 @@
     return pltpu.roll(jnp.where(sub < 4, low, high), 4, 0)
 
 
-def pack_x(own, low, high, first, second):
+def pack_x(own, first_y, second_y, first, second):
     odd_y, odd = is_odd(GY), is_odd(GX)
 
     def put(c, n, up, down):
@@ -85,13 +86,13 @@
             put(
                 c,
                 8 + n,
-                beside_y(odd_y, low, high, c, NX - HALO + 1 + n),
-                beside_y(odd_y, low, high, c, n),
+                beside_y(odd_y, first_y, second_y, c, NX - HALO + 1 + n),
+                beside_y(odd_y, first_y, second_y, c, n),
             )
 
 
-def pack_z(own, first_y, second_y, first_x, second_x, whole, up, down):
-    odd_y, odd = is_odd(GY), is_odd(GX)
+def pack_z(own, first_y, second_y, first_x, second_x, whole, first, second):
+    odd_y, odd, odd_z = is_odd(GY), is_odd(GX), is_odd(GZ)
     lane = lanes((8, NZ))
     zero = jnp.zeros((8, NZ), jnp.float32)
 
@@ -110,18 +111,19 @@
         k = 2 * n + t if t < 2 else 7 + n
         return jnp.where(odd, second_x[c, k], first_x[c, k])
 
-    for c in range(3):
-        for t in range(3):
-            ups, downs = zero, zero
-            for i in range(EX):
+    for k in range(Z_TILES):
+        ups, downs = zero, zero
+        for half in range(2):
+            c, t = divmod(2 * k + half, 3)
+            for i in range(EX if c < 3 else 0):
                 tile = tile_of(c, i, t)
                 whole[c, i, 8 * t : 8 * t + 8, :] = tile
-                place = STEP * (i // 4) + 4 * (i % 4)
+                place = STEP * (i // 4) + 16 * half + 4 * (i % 4)
                 here = (lane >= place) & (lane < place + 4)
                 ups = jnp.where(here, turned(tile, place - (NZ - HALO)), ups)
                 downs = jnp.where(here, turned(tile, place), downs)
-            up[c, 8 * t : 8 * t + 8, :] = ups
-            down[c, 8 * t : 8 * t + 8, :] = downs
+        first[k] = jnp.where(odd_z, ups, downs)
+        second[k] = jnp.where(odd_z, downs, ups)
 
 
 def two_sum(a, b):
@@ -283,17 +285,25 @@
                 sums[c, k, part] = jnp.where(valid, total[k][part], 0.0)
 
 
-def edge_lanes(flags, edge, low, high, sums, powers, moments, whole, *work):
+def edge_lanes(flags, edge, first, second, sums, powers, moments, whole, *work):
     row = rows((EY, NZ))
     lane = lanes((EY, NZ))
     group, offset = lane // STEP, lane % STEP
     inside = jnp.where(row >= NY + HALO, flags[2:3, :], jnp.where(row >= NY, flags[3:4, :], 1.0))
     inside *= jnp.where(group == 3, flags[0:1, :], jnp.where(group == 2, flags[1:2, :], 1.0))
     inside *= jnp.where(offset < 4, flags[4:5, :], jnp.where(offset >= 24, flags[5:6, :], 1.0))
-    for c in range(3):
-        for p in range(GROUPS):
-            value = jnp.where(offset < 4, turned(low[c], -4 * p), edge[c, p])
-            whole[c, p] = jnp.where((offset >= 24) & (offset < 28), turned(high[c], 24 - 4 * p), value)
+    odd = is_odd(GZ)
+    lowest = lanes((8, NZ)) % STEP < 4
+    highest = (lanes((8, NZ)) % STEP >= 24) & (lanes((8, NZ)) % STEP < 28)
+    for k in range(Z_TILES):
+        low = jnp.where(odd, second[k], first[k])
+        high = jnp.where(odd, first[k], second[k])
+        for half in range(2):
+            c, t = divmod(2 * k + half, 3)
+            part = slice(8 * t, 8 * t + 8)
+            for p in range(GROUPS if c < 3 else 0):
+                value = jnp.where(lowest, turned(low, -16 * half - 4 * p), edge[c, p, part, :])
+                whole[c, p, part, :] = jnp.where(highest, turned(high, 24 - 16 * half - 4 * p), value)
 
     def beyond(read, p):
         return turned(read(0), -STEP) if p == GROUPS - 1 else read(p + 1)
@@ -424,12 +434,6 @@
     return call
 
 
-def exchanged(up, down, axis):
-    size = lax.axis_size(axis)
-    steps = [(i, i + 1) for i in range(size - 1)]
-    return lax.ppermute(up, axis, steps), lax.ppermute(down, axis, [(b, a) for a, b in steps])
-
-
 def swapped(first, second, axis):
     size = lax.axis_size(axis)
 
@@ -449,19 +453,19 @@
     flags = jnp.broadcast_to(jnp.stack(ends).astype(jnp.float32)[:, None], (6, NZ))
     flags = jnp.concatenate([flags, jnp.broadcast_to(jnp.pad(6.0 * diffusion, (0, NZ - 3))[None], (2, NZ))])
     block, wide, tiles = (3, NX, NY, NZ), (3, EX, EY, NZ), (3, GROUPS, EY, NZ)
-    own, up, down = kernel(pack_y, [block] + [(3, 4, 8, NZ)] * 2, first=True)(velocity)
-    low, high = swapped(up, down, GY)
-    up, down = kernel(pack_x, [(3, 11, 8, NZ)] * 2)(own, low, high)
-    below, above = swapped(up, down, GX)
-    whole, up, down = kernel(pack_z, [wide, (3, EY, NZ), (3, EY, NZ)])(own, low, high, below, above)
-    low, high = exchanged(up, down, GZ)
+    own, first, second = kernel(pack_y, [block] + [(3, 4, 8, NZ)] * 2, first=True)(velocity)
+    beside = swapped(first, second, GY)
+    first, second = kernel(pack_x, [(3, 11, 8, NZ)] * 2)(own, *beside)
+    beside += swapped(first, second, GX)
+    whole, first, second = kernel(pack_z, [wide] + [(Z_TILES, 8, NZ)] * 2)(own, *beside)
+    first, second = swapped(first, second, GZ)
     powers, sums, edge = kernel(
         inner_lanes, [(ITERS + 1,) + block, (3, MOMENTS, 2, 8, NZ), tiles], [wide] * ITERS
     )(flags, whole)
     planes, stack = lax.axis_size(GX + GY), lax.axis_size(GZ)
     edges, row = kernel(
         edge_lanes, [(ITERS + 1, 3, GROUPS, NY, NZ), (planes, NZ)], [tiles] * (ITERS + 1)
-    )(flags, edge, low, high, sums)
+    )(flags, edge, first, second, sums)
     (row,) = kernel(fold, [(stack, NZ)])(gathered(row, GX + GY))
     return kernel(combine, [block] * 2, last=True)(gathered(row, GZ), flags, powers, edges)
 

time: 75.6 us -> 74.3 us (0.983)
  starting transfers between devices: 21.6 us -> 24.3 us
  waiting for transfers between devices: 5.31 us -> 2.77 us
  blocking collectives: 42 us -> 40.4 us
    ppermute x2 -> x3, starting transfers between devices: 14.4 us -> 19.5 us  [swapped(): lax.ppermute(second, axis, pairs_from(0))]
    ppermute x2 -> x0, starting transfers between devices: 3.01 us -> none  [the longest x1 1.72 us: exchanged(): lax.ppermute(up, axis, steps)]
    ppermute x2 -> x0, waiting for transfers between devices: 2.55 us -> none  [the longest x1 2.54 us: exchanged(): lax.ppermute(down, axis, [(b, a) for a, b in steps])]
    all_to_all x2, blocking collectives: 42 us -> 40.4 us  [gathered(): return lax.all_to_all(row, axes, 0, 0, tiled=True)]
    ppermute x2 -> x3, starting transfers between devices: 4.15 us -> 4.82 us  [swapped(): lax.ppermute(first, axis, pairs_from(1))]
    ppermute x2 -> x3, waiting for transfers between devices: 2.76 us -> 2.77 us  [swapped(): lax.ppermute(second, axis, pairs_from(0))]
  transfers between devices with their start and end apart: 6 -> 6, of which waited for: 3 -> 2; matrix products, arithmetic and copies ran while one was open for 0% -> 0% of each run, Pallas kernels for 2% -> 2%
where the time goes in v7:
time: 74.3 us; the launch traced here: 73.9 us
  blocking collectives  40.4 us (54%)
  starting transfers between devices  24.3 us (33%)
  Pallas kernels  5.39 us (7%)
  waiting for transfers between devices  2.77 us (4%)
  between operations  0.8 us (1%)
    all_to_all x2, blocking collectives, gathered(): return lax.all_to_all(row, axes, 0, 0, tiled=True)  40.4 us
    ppermute x3, starting transfers between devices, swapped(): lax.ppermute(second, axis, pairs_from(0))  19.5 us
    pallas_call x7, Pallas kernels, call(): pl.pallas_call(body, in_specs=[vmem] * len(args), out_specs=[vmem] * len(...  5.39 us
    ppermute x3, starting transfers between devices, swapped(): lax.ppermute(first, axis, pairs_from(1))  4.82 us
    ppermute x3, waiting for transfers between devices, swapped(): lax.ppermute(second, axis, pairs_from(0))  2.77 us
  transfers between devices with their start and end apart: 6, of which 2 were waited for; matrix products, arithmetic and copies ran while one was open for 0% of the time, Pallas kernels for 2%

profile of v7, /device:TPU:1, one launch (start us, length us, event | category | flops | bytes accessed | tf_op | source)
XLA Modules:
  0.0 73.9 jit_solution(6882857217606412877)
XLA Ops:
  0.6 1.0 %pack_y.1 = (f32[3,8,16,128]{3,2,1,0:T(8,128)S(1)}, f32[3,4,8,128]{3,2,1,0:T(8,128)S(1)}, f32[3,4,8,128]{3,2,1,0:T(8,128)S(1)}) custom-call(f32[3,8,16,128]{3,2,1,0:T(8,128)} %block.1), custom_call_target="tpu_custom_call" | custom-call | tf_op jit(solution)/shard_map/pack_y/pallas_call | solution.py:425
  1.6 0.7 collective-permute-start
  2.3 9.8 %collective-permute-start.1 = (f32[3,4,8,128]{3,2,1,0:T(8,128)S(1)}, f32[3,4,8,128]{3,2,1,0:T(8,128)S(1)}, u32[]{:S(2)}, u32[]{:S(2)}) collective-permute-start(f32[3,4,8,128]{3,2,1,0:T(8,128)S(1)} %get-tuple-element.17), channel_id=1, source_target_pairs={{0,12},{24,36},{48,60},{72,84},{96,108},{120,132},{144,156},{168,1... | collective-permute-start | bytes 147464 | tf_op jit(solution)/shard_map/ppermute | solution.py:444
  12.1 0.1 stack.27
  12.2 0.0 collective-permute-done.first_y
  12.2 1.8 %collective-permute-done.1.second_y = f32[3,4,8,128]{3,2,1,0:T(8,128)S(1)} collective-permute-done((f32[3,4,8,128]{3,2,1,0:T(8,128)S(1)}, f32[3,4,8,128]{3,2,1,0:T(8,128)S(1)}, u32[]{:S(2)}, u32[]{:S(2)}) %collective-permute-start.1) | collective-permute-done | bytes 49184 | tf_op jit(solution)/shard_map/ppermute | solution.py:444
  14.1 0.0 copy-start
  14.1 3.5 %collective-permute-start.2 = (f32[3,11,8,128]{3,2,1,0:T(8,128)S(1)}, f32[3,11,8,128]{3,2,1,0:T(8,128)S(1)}, u32[]{:S(2)}, u32[]{:S(2)}) collective-permute-start(f32[3,11,8,128]{3,2,1,0:T(8,128)S(1)} %get-tuple-element.18), channel_id=1, source_target_pairs={{192,384},{384,192},{193,385},{385,193},{194,386},{386,194},{195,3... | collective-permute-start | bytes 405512 | tf_op jit(solution)/shard_map/ppermute | solution.py:444
  17.6 4.6 %collective-permute-start.3 = (f32[3,11,8,128]{3,2,1,0:T(8,128)S(1)}, f32[3,11,8,128]{3,2,1,0:T(8,128)S(1)}, u32[]{:S(2)}, u32[]{:S(2)}) collective-permute-start(f32[3,11,8,128]{3,2,1,0:T(8,128)S(1)} %get-tuple-element.19), channel_id=1, source_target_pairs={{0,192},{384,576},{192,0},{576,384},{1,193},{385,577},{193,1},{577... | collective-permute-start | bytes 405512 | tf_op jit(solution)/shard_map/ppermute | solution.py:444
  22.3 0.0 copy-done
  22.3 0.0 collective-permute-done.2.first_x
  22.3 0.9 %collective-permute-done.3.second_x = f32[3,11,8,128]{3,2,1,0:T(8,128)S(1)} collective-permute-done((f32[3,11,8,128]{3,2,1,0:T(8,128)S(1)}, f32[3,11,8,128]{3,2,1,0:T(8,128)S(1)}, u32[]{:S(2)}, u32[]{:S(2)}) %collective-permute-start.3) | collective-permute-done | bytes 135200 | tf_op jit(solution)/shard_map/ppermute | solution.py:444
  23.2 0.4 pack_z.1
  23.6 0.7 collective-permute-start.4
  24.3 5.1 %collective-permute-start.5 = (f32[5,8,128]{2,1,0:T(8,128)S(1)}, f32[5,8,128]{2,1,0:T(8,128)S(1)}, u32[]{:S(2)}, u32[]{:S(2)}) collective-permute-start(f32[5,8,128]{2,1,0:T(8,128)S(1)} %get-tuple-element.23), channel_id=1, source_target_pairs={{0,1},{2,3},{4,5},{6,7},{8,9},{10,11},{1,0},{3,2},{5,4},{7,6},{9,8... | collective-permute-start | bytes 61448 | tf_op jit(solution)/shard_map/ppermute | solution.py:444
  29.4 0.1 pad_maximum_fusion.flags
  29.4 1.4 %inner_lanes.1 = (f32[4,3,8,16,128]{4,3,2,1,0:T(8,128)S(1)}, f32[3,6,2,8,128]{4,3,2,1,0:T(8,128)S(1)}, f32[3,4,24,128]{3,2,1,0:T(8,128)S(1)}) custom-call(f32[8,128]{1,0:T(8,128)S(1)} %pad_maximum_fusion.flags, f32[3,16,24,128]{3,2,1,0:T(8,128)S(1)} %get-tuple-element.20.whole), custom_call_target="tpu_custom_call" | custom-call | tf_op jit(solution)/shard_map/inner_lanes/pallas_call | solution.py:425
  30.8 0.0 collective-permute-done.4.first
  30.8 0.0 collective-permute-done.5.second
  30.9 1.2 %edge_lanes.1 = (f32[4,3,4,16,128]{4,3,2,1,0:T(8,128)S(1)}, f32[64,128]{1,0:T(8,128)S(1)}) custom-call(f32[8,128]{1,0:T(8,128)S(1)} %pad_maximum_fusion.flags, f32[3,4,24,128]{3,2,1,0:T(8,128)S(1)} %get-tuple-element.21.edge, f32[5,8,128]{2,1,0:T(8,128)S(1)} %collective-permute-done.4.first, f32[5,8,128]{2,1,0:T(8,128)S(1)} %collective-permute-done.5.second, ...), custom_call_target="tpu_custom_call" | custom-call | tf_op jit(solution)/shard_map/edge_lanes/pallas_call | solution.py:425
  32.0 18.1 %all_to_all.22 = f32[64,1,128]{2,1,0:T(1,128)S(1)} all-to-all(f32[64,1,128]{2,1,0:T(1,128)S(1)} %bitcast.17), channel_id=1, replica_groups=mesh['gx_0'=2,'gx_1'=2,'gy_0'=4,'gy_1'=4,'gz'=12] {'gx_0','gx_1','gy_0',..., dimensions={0} | all-to-all | bytes 65536 | tf_op jit(solution)/shard_map/all_to_all | solution.py:448
  50.1 0.2 fold.1
  50.3 22.4 %all_to_all.23 = f32[12,1,128]{2,1,0:T(1,128)S(1)} all-to-all(f32[12,1,128]{2,1,0:T(1,128)S(1)} %copy.5), channel_id=1, replica_groups=mesh['gx_0'=2,'gx_1'=2,'gy_0'=4,'gy_1'=4,'gz'=12] {'gz'}, dimensions={0} | all-to-all | bytes 12288 | tf_op jit(solution)/shard_map/all_to_all | solution.py:448
  72.6 1.3 %combine.1 = (f32[3,8,16,128]{3,2,1,0:T(8,128)}, f32[3,8,16,128]{3,2,1,0:T(8,128)}) custom-call(f32[12,128]{1,0:T(8,128)S(1)} %bitcast.15, f32[8,128]{1,0:T(8,128)S(1)} %pad_maximum_fusion.flags, f32[4,3,8,16,128]{4,3,2,1,0:T(8,128)S(1)} %get-tuple-element.26.powers, f32[4,3,4,16,128]{4,3,2,1,0:T(8,128)S(1)} %get-tuple-element.27.edges), custom_call_target="tpu_custom_call" | custom-call | tf_op jit(solution)/shard_map/combine/pallas_call | solution.py:425
  (8 shorter events, 0.1 us)
Async XLA Ops:
  1.6 10.6 %collective-permute-start = (f32[3,4,8,128]{3,2,1,0:T(8,128)S(1)}, f32[3,4,8,128]{3,2,1,0:T(8,128)S(1)}, u32[]{:S(2)}, u32[]{:S(2)}) collective-permute-start(f32[3,4,8,128]{3,2,1,0:T(8,128)S(1)} %get-tuple-element.16), channel_id=1, source_target_pairs={{12,24},{36,48},{60,72},{84,96},{108,120},{132,144},{156,168},{24,... | collective-permute-start | bytes 147464 | tf_op jit(solution)/shard_map/ppermute | solution.py:444
  2.3 11.8 %collective-permute-start.1 = (f32[3,4,8,128]{3,2,1,0:T(8,128)S(1)}, f32[3,4,8,128]{3,2,1,0:T(8,128)S(1)}, u32[]{:S(2)}, u32[]{:S(2)}) collective-permute-start(f32[3,4,8,128]{3,2,1,0:T(8,128)S(1)} %get-tuple-element.17), channel_id=1, source_target_pairs={{0,12},{24,36},{48,60},{72,84},{96,108},{120,132},{144,156},{168,1... | collective-permute-start | bytes 147464 | tf_op jit(solution)/shard_map/ppermute | solution.py:444
  14.1 8.2 %copy-start = (f32[3]{0:T(128)S(1)}, f32[3]{0:T(128)}, u32[]{:S(2)}) copy-start(f32[3]{0:T(128)} %param.3) | copy-start | bytes 40
  14.1 8.2 %collective-permute-start.2 = (f32[3,11,8,128]{3,2,1,0:T(8,128)S(1)}, f32[3,11,8,128]{3,2,1,0:T(8,128)S(1)}, u32[]{:S(2)}, u32[]{:S(2)}) collective-permute-start(f32[3,11,8,128]{3,2,1,0:T(8,128)S(1)} %get-tuple-element.18), channel_id=1, source_target_pairs={{192,384},{384,192},{193,385},{385,193},{194,386},{386,194},{195,3... | collective-permute-start | bytes 405512 | tf_op jit(solution)/shard_map/ppermute | solution.py:444
  17.6 5.6 %collective-permute-start.3 = (f32[3,11,8,128]{3,2,1,0:T(8,128)S(1)}, f32[3,11,8,128]{3,2,1,0:T(8,128)S(1)}, u32[]{:S(2)}, u32[]{:S(2)}) collective-permute-start(f32[3,11,8,128]{3,2,1,0:T(8,128)S(1)} %get-tuple-element.19), channel_id=1, source_target_pairs={{0,192},{384,576},{192,0},{576,384},{1,193},{385,577},{193,1},{577... | collective-permute-start | bytes 405512 | tf_op jit(solution)/shard_map/ppermute | solution.py:444
  23.6 7.2 %collective-permute-start.4 = (f32[5,8,128]{2,1,0:T(8,128)S(1)}, f32[5,8,128]{2,1,0:T(8,128)S(1)}, u32[]{:S(2)}, u32[]{:S(2)}) collective-permute-start(f32[5,8,128]{2,1,0:T(8,128)S(1)} %get-tuple-element.22), channel_id=1, source_target_pairs={{1,2},{3,4},{5,6},{7,8},{9,10},{2,1},{4,3},{6,5},{8,7},{10,9},{13,... | collective-permute-start | bytes 61448 | tf_op jit(solution)/shard_map/ppermute | solution.py:444
  24.3 6.6 %collective-permute-start.5 = (f32[5,8,128]{2,1,0:T(8,128)S(1)}, f32[5,8,128]{2,1,0:T(8,128)S(1)}, u32[]{:S(2)}, u32[]{:S(2)}) collective-permute-start(f32[5,8,128]{2,1,0:T(8,128)S(1)} %get-tuple-element.23), channel_id=1, source_target_pairs={{0,1},{2,3},{4,5},{6,7},{8,9},{10,11},{1,0},{3,2},{5,4},{7,6},{9,8... | collective-permute-start | bytes 61448 | tf_op jit(solution)/shard_map/ppermute | solution.py:444

commit v8 on v7

--- a/solution.py
+++ b/solution.py
@@ -49,14 +49,17 @@
     return lax.axis_index(axes) % 2 == 1
 
 
-def pack_y(block, own, first, second):
+def pack_y(block, own, first, second, arrived):
     odd = is_odd(GY)
     sub = rows((8, NZ))
-    own[...] = block[...]
+    copies = [pltpu.make_async_copy(block.at[c], own.at[c], arrived.at[c]) for c in range(3)]
+    for copy in copies:
+        copy.start()
     for c in range(3):
+        copies[c].wait()
         for q in range(4):
-            up = jnp.where(sub >= 4, block[c, q, 8:16, :], pltpu.roll(block[c, q + 4, 8:16, :], 4, 0))
-            down = jnp.where(sub < 4, block[c, q, 0:8, :], pltpu.roll(block[c, q + 4, 0:8, :], 4, 0))
+            up = jnp.where(sub >= 4, own[c, q, 8:16, :], pltpu.roll(own[c, q + 4, 8:16, :], 4, 0))
+            down = jnp.where(sub < 4, own[c, q, 0:8, :], pltpu.roll(own[c, q + 4, 0:8, :], 4, 0))
             first[c, q] = jnp.where(odd, up, down)
             second[c, q] = jnp.where(odd, down, up)
 
@@ -388,7 +391,8 @@
     return in_powers_of_l(total), in_powers_of_l(residual)
 
 
-def combine(parts, flags, powers, edges, total, rest):
+def combine(parts, flags, powers, edges, total, rest, total_here, rest_here, left):
+    copies = []
     lane = lanes((8, NZ))
     high, low = folded(lambda first, size: parts[first : first + size, :], parts.shape[0])
     moments = [(turned(high, -3 * k), turned(low, -3 * k)) for k in range(MOMENTS)]
@@ -396,7 +400,7 @@
     def spread(value, c):
         return jnp.broadcast_to(jnp.sum(jnp.where(lane == c, value, 0.0), axis=1, keepdims=True), (8, NZ))
 
-    for out, weights in zip((total, rest), weights_of(moments, jnp.broadcast_to(flags[6:7, :], (8, NZ)))):
+    for (target, out), weights in zip(((total, total_here), (rest, rest_here)), weights_of(moments, jnp.broadcast_to(flags[6:7, :], (8, NZ)))):
         for c in range(3):
             factors = [spread(w, c) for w in weights]
 
@@ -413,21 +417,26 @@
                         value = jnp.where(lane < HALO, turned(side, -(STEP * g + 4)), value)
                         value = jnp.where(lane >= NZ - HALO, turned(side, 104 - STEP * g), value)
                         out[c, x, part, :] = value
+            copies.append(pltpu.make_async_copy(out.at[c], target.at[c], left.at[len(copies)]))
+            copies[-1].start()
+    for copy in copies:
+        copy.wait()
 
 
 def kernel(body, outs, scratch=(), first=False, last=False):
-    vmem = pl.BlockSpec(memory_space=pltpu.VMEM)
+    vmem, hbm = (pl.BlockSpec(memory_space=m) for m in (pltpu.VMEM, pl.ANY))
     shape = jax.ShapeDtypeStruct if last else pltpu.VMEM
 
     def call(*args):
         if not first:
             args = [pltpu.with_memory_space_constraint(a, pltpu.VMEM) for a in args]
+        semaphores = [pltpu.SemaphoreType.DMA((2 * 3 if last else 3,))] if first or last else []
         return pl.pallas_call(
             body,
-            in_specs=[vmem] * len(args),
-            out_specs=[vmem] * len(outs),
+            in_specs=[hbm if first else vmem] * len(args),
+            out_specs=[hbm if last else vmem] * len(outs),
             out_shape=[shape(s, jnp.float32) for s in outs],
-            scratch_shapes=[pltpu.VMEM(s, jnp.float32) for s in scratch],
+            scratch_shapes=[pltpu.VMEM(s, jnp.float32) for s in scratch] + semaphores,
             name=body.__name__,
         )(*args)
 
@@ -462,12 +471,13 @@
     powers, sums, edge = kernel(
         inner_lanes, [(ITERS + 1,) + block, (3, MOMENTS, 2, 8, NZ), tiles], [wide] * ITERS
     )(flags, whole)
-    planes, stack = lax.axis_size(GX + GY), lax.axis_size(GZ)
+    near, far = GX[:1] + GY, GX[1:] + GZ
+    planes, stack = lax.axis_size(near), lax.axis_size(far)
     edges, row = kernel(
         edge_lanes, [(ITERS + 1, 3, GROUPS, NY, NZ), (planes, NZ)], [tiles] * (ITERS + 1)
     )(flags, edge, first, second, sums)
-    (row,) = kernel(fold, [(stack, NZ)])(gathered(row, GX + GY))
-    return kernel(combine, [block] * 2, last=True)(gathered(row, GZ), flags, powers, edges)
+    (row,) = kernel(fold, [(stack, NZ)])(gathered(row, near))
+    return kernel(combine, [block] * 2, [block] * 2, last=True)(gathered(row, far), flags, powers, edges)
 
 
 def solution(mesh):

time: 74.3 us -> 75.2 us (1.012)
  blocking collectives: 40.4 us -> 41.4 us
    all_to_all x2, blocking collectives: 40.4 us -> 41.4 us  [gathered(): return lax.all_to_all(row, axes, 0, 0, tiled=True)]
where the time goes in v8:
time: 75.2 us; the launch traced here: 74.9 us
  blocking collectives  41.4 us (55%)
  starting transfers between devices  24.3 us (32%)
  Pallas kernels  5.39 us (7%)
  waiting for transfers between devices  2.77 us (4%)
  between operations  0.8 us (1%)
    all_to_all x2, blocking collectives, gathered(): return lax.all_to_all(row, axes, 0, 0, tiled=True)  41.4 us
    ppermute x3, starting transfers between devices, swapped(): lax.ppermute(second, axis, pairs_from(0))  19.5 us
    pallas_call x7, Pallas kernels, call(): pl.pallas_call(body, in_specs=[hbm if first else vmem] * len(args), out_s...  5.39 us
    ppermute x3, starting transfers between devices, swapped(): lax.ppermute(first, axis, pairs_from(1))  4.82 us
    ppermute x3, waiting for transfers between devices, swapped(): lax.ppermute(second, axis, pairs_from(0))  2.77 us
  transfers between devices with their start and end apart: 6, of which 2 were waited for; matrix products, arithmetic and copies ran while one was open for 0% of the time, Pallas kernels for 2%

profile of v8, /device:TPU:1, one launch (start us, length us, event | category | flops | bytes accessed | tf_op | source)
XLA Modules:
  0.0 74.9 jit_solution(11212549548339598894)
XLA Ops:
  0.6 0.9 %pack_y.1 = (f32[3,8,16,128]{3,2,1,0:T(8,128)S(1)}, f32[3,4,8,128]{3,2,1,0:T(8,128)S(1)}, f32[3,4,8,128]{3,2,1,0:T(8,128)S(1)}) custom-call(f32[3,8,16,128]{3,2,1,0:T(8,128)} %block.1), custom_call_target="tpu_custom_call" | custom-call | tf_op jit(solution)/shard_map/pack_y/pallas_call | solution.py:434
  1.6 0.7 collective-permute-start
  2.2 9.8 %collective-permute-start.1 = (f32[3,4,8,128]{3,2,1,0:T(8,128)S(1)}, f32[3,4,8,128]{3,2,1,0:T(8,128)S(1)}, u32[]{:S(2)}, u32[]{:S(2)}) collective-permute-start(f32[3,4,8,128]{3,2,1,0:T(8,128)S(1)} %get-tuple-element.17), channel_id=1, source_target_pairs={{0,12},{24,36},{48,60},{72,84},{96,108},{120,132},{144,156},{168,1... | collective-permute-start | bytes 147464 | tf_op jit(solution)/shard_map/ppermute | solution.py:453
  12.1 0.1 stack.27
  12.2 0.0 collective-permute-done.first_y
  12.2 1.8 %collective-permute-done.1.second_y = f32[3,4,8,128]{3,2,1,0:T(8,128)S(1)} collective-permute-done((f32[3,4,8,128]{3,2,1,0:T(8,128)S(1)}, f32[3,4,8,128]{3,2,1,0:T(8,128)S(1)}, u32[]{:S(2)}, u32[]{:S(2)}) %collective-permute-start.1) | collective-permute-done | bytes 49184 | tf_op jit(solution)/shard_map/ppermute | solution.py:453
  14.1 0.0 copy-start
  14.1 3.5 %collective-permute-start.2 = (f32[3,11,8,128]{3,2,1,0:T(8,128)S(1)}, f32[3,11,8,128]{3,2,1,0:T(8,128)S(1)}, u32[]{:S(2)}, u32[]{:S(2)}) collective-permute-start(f32[3,11,8,128]{3,2,1,0:T(8,128)S(1)} %get-tuple-element.18), channel_id=1, source_target_pairs={{192,384},{384,192},{193,385},{385,193},{194,386},{386,194},{195,3... | collective-permute-start | bytes 405512 | tf_op jit(solution)/shard_map/ppermute | solution.py:453
  17.6 4.6 %collective-permute-start.3 = (f32[3,11,8,128]{3,2,1,0:T(8,128)S(1)}, f32[3,11,8,128]{3,2,1,0:T(8,128)S(1)}, u32[]{:S(2)}, u32[]{:S(2)}) collective-permute-start(f32[3,11,8,128]{3,2,1,0:T(8,128)S(1)} %get-tuple-element.19), channel_id=1, source_target_pairs={{0,192},{384,576},{192,0},{576,384},{1,193},{385,577},{193,1},{577... | collective-permute-start | bytes 405512 | tf_op jit(solution)/shard_map/ppermute | solution.py:453
  22.3 0.0 copy-done
  22.3 0.0 collective-permute-done.2.first_x
  22.3 0.9 %collective-permute-done.3.second_x = f32[3,11,8,128]{3,2,1,0:T(8,128)S(1)} collective-permute-done((f32[3,11,8,128]{3,2,1,0:T(8,128)S(1)}, f32[3,11,8,128]{3,2,1,0:T(8,128)S(1)}, u32[]{:S(2)}, u32[]{:S(2)}) %collective-permute-start.3) | collective-permute-done | bytes 135200 | tf_op jit(solution)/shard_map/ppermute | solution.py:453
  23.2 0.4 pack_z.1
  23.6 0.7 collective-permute-start.4
  24.3 5.1 %collective-permute-start.5 = (f32[5,8,128]{2,1,0:T(8,128)S(1)}, f32[5,8,128]{2,1,0:T(8,128)S(1)}, u32[]{:S(2)}, u32[]{:S(2)}) collective-permute-start(f32[5,8,128]{2,1,0:T(8,128)S(1)} %get-tuple-element.23), channel_id=1, source_target_pairs={{0,1},{2,3},{4,5},{6,7},{8,9},{10,11},{1,0},{3,2},{5,4},{7,6},{9,8... | collective-permute-start | bytes 61448 | tf_op jit(solution)/shard_map/ppermute | solution.py:453
  29.3 0.1 pad_maximum_fusion.flags
  29.4 1.4 %inner_lanes.1 = (f32[4,3,8,16,128]{4,3,2,1,0:T(8,128)S(1)}, f32[3,6,2,8,128]{4,3,2,1,0:T(8,128)S(1)}, f32[3,4,24,128]{3,2,1,0:T(8,128)S(1)}) custom-call(f32[8,128]{1,0:T(8,128)S(1)} %pad_maximum_fusion.flags, f32[3,16,24,128]{3,2,1,0:T(8,128)S(1)} %get-tuple-element.20.whole), custom_call_target="tpu_custom_call" | custom-call | tf_op jit(solution)/shard_map/inner_lanes/pallas_call | solution.py:434
  30.8 0.0 collective-permute-done.4.first
  30.8 0.0 collective-permute-done.5.second
  30.8 1.2 %edge_lanes.1 = (f32[4,3,4,16,128]{4,3,2,1,0:T(8,128)S(1)}, f32[32,128]{1,0:T(8,128)S(1)}) custom-call(f32[8,128]{1,0:T(8,128)S(1)} %pad_maximum_fusion.flags, f32[3,4,24,128]{3,2,1,0:T(8,128)S(1)} %get-tuple-element.21.edge, f32[5,8,128]{2,1,0:T(8,128)S(1)} %collective-permute-done.4.first, f32[5,8,128]{2,1,0:T(8,128)S(1)} %collective-permute-done.5.second, ...), custom_call_target="tpu_custom_call" | custom-call | tf_op jit(solution)/shard_map/edge_lanes/pallas_call | solution.py:434
  32.0 15.7 %all_to_all.22 = f32[32,1,128]{2,1,0:T(1,128)S(1)} all-to-all(f32[32,1,128]{2,1,0:T(1,128)S(1)} %bitcast.17), channel_id=1, replica_groups=mesh['gx_0'=2,'gx_1'=2,'gy_0'=4,'gy_1'=4,'gz'=12] {'gx_0','gy_0','gy_1'}, dimensions={0} | all-to-all | bytes 32768 | tf_op jit(solution)/shard_map/all_to_all | solution.py:457
  47.7 0.2 fold.1
  47.9 25.6 %all_to_all.23 = f32[24,1,128]{2,1,0:T(1,128)S(1)} all-to-all(f32[24,1,128]{2,1,0:T(1,128)S(1)} %bitcast.16), channel_id=1, replica_groups=mesh['gx_0'=2,'gx_1'=2,'gy_0'=4,'gy_1'=4,'gz'=12] {'gx_1','gz'}, dimensions={0} | all-to-all | bytes 24576 | tf_op jit(solution)/shard_map/all_to_all | solution.py:457
  73.5 1.3 %combine.1 = (f32[3,8,16,128]{3,2,1,0:T(8,128)}, f32[3,8,16,128]{3,2,1,0:T(8,128)}) custom-call(f32[24,128]{1,0:T(8,128)S(1)} %bitcast.15, f32[8,128]{1,0:T(8,128)S(1)} %pad_maximum_fusion.flags, f32[4,3,8,16,128]{4,3,2,1,0:T(8,128)S(1)} %get-tuple-element.26.powers, f32[4,3,4,16,128]{4,3,2,1,0:T(8,128)S(1)} %get-tuple-element.27.edges), custom_call_target="tpu_custom_call" | custom-call | tf_op jit(solution)/shard_map/combine/pallas_call | solution.py:434
  (6 shorter events, 0.1 us)
Async XLA Ops:
  1.6 10.6 %collective-permute-start = (f32[3,4,8,128]{3,2,1,0:T(8,128)S(1)}, f32[3,4,8,128]{3,2,1,0:T(8,128)S(1)}, u32[]{:S(2)}, u32[]{:S(2)}) collective-permute-start(f32[3,4,8,128]{3,2,1,0:T(8,128)S(1)} %get-tuple-element.16), channel_id=1, source_target_pairs={{12,24},{36,48},{60,72},{84,96},{108,120},{132,144},{156,168},{24,... | collective-permute-start | bytes 147464 | tf_op jit(solution)/shard_map/ppermute | solution.py:453
  2.2 11.8 %collective-permute-start.1 = (f32[3,4,8,128]{3,2,1,0:T(8,128)S(1)}, f32[3,4,8,128]{3,2,1,0:T(8,128)S(1)}, u32[]{:S(2)}, u32[]{:S(2)}) collective-permute-start(f32[3,4,8,128]{3,2,1,0:T(8,128)S(1)} %get-tuple-element.17), channel_id=1, source_target_pairs={{0,12},{24,36},{48,60},{72,84},{96,108},{120,132},{144,156},{168,1... | collective-permute-start | bytes 147464 | tf_op jit(solution)/shard_map/ppermute | solution.py:453
  14.1 8.2 %copy-start = (f32[3]{0:T(128)S(1)}, f32[3]{0:T(128)}, u32[]{:S(2)}) copy-start(f32[3]{0:T(128)} %param.3) | copy-start | bytes 40
  14.1 8.2 %collective-permute-start.2 = (f32[3,11,8,128]{3,2,1,0:T(8,128)S(1)}, f32[3,11,8,128]{3,2,1,0:T(8,128)S(1)}, u32[]{:S(2)}, u32[]{:S(2)}) collective-permute-start(f32[3,11,8,128]{3,2,1,0:T(8,128)S(1)} %get-tuple-element.18), channel_id=1, source_target_pairs={{192,384},{384,192},{193,385},{385,193},{194,386},{386,194},{195,3... | collective-permute-start | bytes 405512 | tf_op jit(solution)/shard_map/ppermute | solution.py:453
  17.6 5.6 %collective-permute-start.3 = (f32[3,11,8,128]{3,2,1,0:T(8,128)S(1)}, f32[3,11,8,128]{3,2,1,0:T(8,128)S(1)}, u32[]{:S(2)}, u32[]{:S(2)}) collective-permute-start(f32[3,11,8,128]{3,2,1,0:T(8,128)S(1)} %get-tuple-element.19), channel_id=1, source_target_pairs={{0,192},{384,576},{192,0},{576,384},{1,193},{385,577},{193,1},{577... | collective-permute-start | bytes 405512 | tf_op jit(solution)/shard_map/ppermute | solution.py:453
  23.6 7.2 %collective-permute-start.4 = (f32[5,8,128]{2,1,0:T(8,128)S(1)}, f32[5,8,128]{2,1,0:T(8,128)S(1)}, u32[]{:S(2)}, u32[]{:S(2)}) collective-permute-start(f32[5,8,128]{2,1,0:T(8,128)S(1)} %get-tuple-element.22), channel_id=1, source_target_pairs={{1,2},{3,4},{5,6},{7,8},{9,10},{2,1},{4,3},{6,5},{8,7},{10,9},{13,... | collective-permute-start | bytes 61448 | tf_op jit(solution)/shard_map/ppermute | solution.py:453
  24.3 6.6 %collective-permute-start.5 = (f32[5,8,128]{2,1,0:T(8,128)S(1)}, f32[5,8,128]{2,1,0:T(8,128)S(1)}, u32[]{:S(2)}, u32[]{:S(2)}) collective-permute-start(f32[5,8,128]{2,1,0:T(8,128)S(1)} %get-tuple-element.23), channel_id=1, source_target_pairs={{0,1},{2,3},{4,5},{6,7},{8,9},{10,11},{1,0},{3,2},{5,4},{7,6},{9,8... | collective-permute-start | bytes 61448 | tf_op jit(solution)/shard_map/ppermute | solution.py:453

commit v9 on v7

--- a/solution.py
+++ b/solution.py
@@ -111,19 +111,25 @@
         k = 2 * n + t if t < 2 else 7 + n
         return jnp.where(odd, second_x[c, k], first_x[c, k])
 
+    def faces(c, t, i, count):
+        if count == 1:
+            tile = tile_of(c, i, t)
+            whole[c, i, 8 * t : 8 * t + 8, :] = tile
+            return turned(tile, 8 * i + HALO)
+        count //= 2
+        early, late = faces(c, t, i, count), faces(c, t, i + count, count)
+        return jnp.where(lane // 8 // count % 2 == 1, late, early)
+
+    both = [faces(c, t, 0, EX) for c in range(3) for t in range(3)] + [zero]
     for k in range(Z_TILES):
-        ups, downs = zero, zero
-        for half in range(2):
-            c, t = divmod(2 * k + half, 3)
-            for i in range(EX if c < 3 else 0):
-                tile = tile_of(c, i, t)
-                whole[c, i, 8 * t : 8 * t + 8, :] = tile
-                place = STEP * (i // 4) + 16 * half + 4 * (i % 4)
-                here = (lane >= place) & (lane < place + 4)
-                ups = jnp.where(here, turned(tile, place - (NZ - HALO)), ups)
-                downs = jnp.where(here, turned(tile, place), downs)
-        first[k] = jnp.where(odd_z, ups, downs)
-        second[k] = jnp.where(odd_z, downs, ups)
+        early, late = both[2 * k : 2 * k + 2]
+        if k == Z_TILES - 1:
+            up, down = early, turned(early, -HALO)
+        else:
+            up = jnp.where(lane % 8 < HALO, early, turned(late, HALO))
+            down = jnp.where(lane % 8 < HALO, turned(early, -HALO), late)
+        first[k] = jnp.where(odd_z, up, down)
+        second[k] = jnp.where(odd_z, down, up)
 
 
 def two_sum(a, b):
@@ -147,6 +153,11 @@
 def added(first, second):
     total, rest = two_sum(first[0], second[0])
     return total, (first[1] + second[1]) + rest
+
+
+def more(total, value):
+    high, rest = two_sum(total[0], value)
+    return high, total[1] + rest
 
 
 def rolled(value, shift, axis):
@@ -279,7 +290,7 @@
         for x in range(NX):
             for t in range(2):
                 v = [powers[k, c, x, 8 * t : 8 * t + 8, :] for k in range(ITERS + 1)]
-                total = [added(s, (v[a] * v[b], zero)) for s, (a, b) in zip(total, pairs())]
+                total = [more(s, v[a] * v[b]) for s, (a, b) in zip(total, pairs())]
         for k in range(MOMENTS):
             for part in range(2):
                 sums[c, k, part] = jnp.where(valid, total[k][part], 0.0)
@@ -302,8 +313,8 @@
             c, t = divmod(2 * k + half, 3)
             part = slice(8 * t, 8 * t + 8)
             for p in range(GROUPS if c < 3 else 0):
-                value = jnp.where(lowest, turned(low, -16 * half - 4 * p), edge[c, p, part, :])
-                whole[c, p, part, :] = jnp.where(highest, turned(high, 24 - 16 * half - 4 * p), value)
+                value = jnp.where(lowest, turned(low, -4 * half - 8 * p), edge[c, p, part, :])
+                whole[c, p, part, :] = jnp.where(highest, turned(high, 24 - 4 * half - 8 * p), value)
 
     def beyond(read, p):
         return turned(read(0), -STEP) if p == GROUPS - 1 else read(p + 1)
@@ -332,18 +343,13 @@
     lane = lanes((8, NZ))
     group, offset = lane // STEP, lane % STEP
     valid = (group < 2) & (((offset >= 4) & (offset < 8)) | ((offset >= 20) & (offset < 24)))
-    zero = jnp.zeros((8, NZ), jnp.float32)
     totals = []
     for k in range(MOMENTS):
         a, b = pairs()[k]
         for c in range(3):
-            total = (sums[c, k, 0], sums[c, k, 1])
-            for p in range(GROUPS):
-                for t in range(2):
-                    part = slice(8 * t, 8 * t + 8)
-                    value = powers[a, c, p, part, :] * powers[b, c, p, part, :]
-                    total = added(total, (jnp.where(valid, value, 0.0), zero))
-            totals.append(total)
+            parts = [(p, slice(8 * t, 8 * t + 8)) for p in range(GROUPS) for t in range(2)]
+            value = sum(powers[a, c, p, part, :] * powers[b, c, p, part, :] for p, part in parts)
+            totals.append(more((sums[c, k, 0], sums[c, k, 1]), jnp.where(valid, value, 0.0)))
     moments[...] = jnp.broadcast_to(lane_totals(totals), moments.shape)
 
 

time: 74.3 us -> 74.1 us (level)
  no operation moved by 1% of the time
where the time goes in v9:
time: 74.1 us; the launch traced here: 73.8 us
  blocking collectives  40.4 us (55%)
  starting transfers between devices  24.3 us (33%)
  Pallas kernels  5.24 us (7%)
  waiting for transfers between devices  2.77 us (4%)
  between operations  0.79 us (1%)
    all_to_all x2, blocking collectives, gathered(): return lax.all_to_all(row, axes, 0, 0, tiled=True)  40.4 us
    ppermute x3, starting transfers between devices, swapped(): lax.ppermute(second, axis, pairs_from(0))  19.5 us
    pallas_call x7, Pallas kernels, call(): pl.pallas_call(body, in_specs=[vmem] * len(args), out_specs=[vmem] * len(...  5.24 us
    ppermute x3, starting transfers between devices, swapped(): lax.ppermute(first, axis, pairs_from(1))  4.81 us
    ppermute x3, waiting for transfers between devices, swapped(): lax.ppermute(second, axis, pairs_from(0))  2.77 us
  transfers between devices with their start and end apart: 6, of which 2 were waited for; matrix products, arithmetic and copies ran while one was open for 0% of the time, Pallas kernels for 2%

profile of v9, /device:TPU:1, one launch (start us, length us, event | category | flops | bytes accessed | tf_op | source)
XLA Modules:
  0.0 73.8 jit_solution(13387429435685449364)
XLA Ops:
  0.6 1.0 %pack_y.1 = (f32[3,8,16,128]{3,2,1,0:T(8,128)S(1)}, f32[3,4,8,128]{3,2,1,0:T(8,128)S(1)}, f32[3,4,8,128]{3,2,1,0:T(8,128)S(1)}) custom-call(f32[3,8,16,128]{3,2,1,0:T(8,128)} %block.1), custom_call_target="tpu_custom_call" | custom-call | tf_op jit(solution)/shard_map/pack_y/pallas_call | solution.py:431
  1.6 0.7 collective-permute-start
  2.3 9.8 %collective-permute-start.1 = (f32[3,4,8,128]{3,2,1,0:T(8,128)S(1)}, f32[3,4,8,128]{3,2,1,0:T(8,128)S(1)}, u32[]{:S(2)}, u32[]{:S(2)}) collective-permute-start(f32[3,4,8,128]{3,2,1,0:T(8,128)S(1)} %get-tuple-element.17), channel_id=1, source_target_pairs={{0,12},{24,36},{48,60},{72,84},{96,108},{120,132},{144,156},{168,1... | collective-permute-start | bytes 147464 | tf_op jit(solution)/shard_map/ppermute | solution.py:450
  12.1 0.1 stack.27
  12.2 0.0 collective-permute-done.first_y
  12.2 1.8 %collective-permute-done.1.second_y = f32[3,4,8,128]{3,2,1,0:T(8,128)S(1)} collective-permute-done((f32[3,4,8,128]{3,2,1,0:T(8,128)S(1)}, f32[3,4,8,128]{3,2,1,0:T(8,128)S(1)}, u32[]{:S(2)}, u32[]{:S(2)}) %collective-permute-start.1) | collective-permute-done | bytes 49184 | tf_op jit(solution)/shard_map/ppermute | solution.py:450
  14.1 0.0 copy-start
  14.1 3.5 %collective-permute-start.2 = (f32[3,11,8,128]{3,2,1,0:T(8,128)S(1)}, f32[3,11,8,128]{3,2,1,0:T(8,128)S(1)}, u32[]{:S(2)}, u32[]{:S(2)}) collective-permute-start(f32[3,11,8,128]{3,2,1,0:T(8,128)S(1)} %get-tuple-element.18), channel_id=1, source_target_pairs={{192,384},{384,192},{193,385},{385,193},{194,386},{386,194},{195,3... | collective-permute-start | bytes 405512 | tf_op jit(solution)/shard_map/ppermute | solution.py:450
  17.6 4.6 %collective-permute-start.3 = (f32[3,11,8,128]{3,2,1,0:T(8,128)S(1)}, f32[3,11,8,128]{3,2,1,0:T(8,128)S(1)}, u32[]{:S(2)}, u32[]{:S(2)}) collective-permute-start(f32[3,11,8,128]{3,2,1,0:T(8,128)S(1)} %get-tuple-element.19), channel_id=1, source_target_pairs={{0,192},{384,576},{192,0},{576,384},{1,193},{385,577},{193,1},{577... | collective-permute-start | bytes 405512 | tf_op jit(solution)/shard_map/ppermute | solution.py:450
  22.3 0.0 copy-done
  22.3 0.0 collective-permute-done.2.first_x
  22.3 0.9 %collective-permute-done.3.second_x = f32[3,11,8,128]{3,2,1,0:T(8,128)S(1)} collective-permute-done((f32[3,11,8,128]{3,2,1,0:T(8,128)S(1)}, f32[3,11,8,128]{3,2,1,0:T(8,128)S(1)}, u32[]{:S(2)}, u32[]{:S(2)}) %collective-permute-start.3) | collective-permute-done | bytes 135200 | tf_op jit(solution)/shard_map/ppermute | solution.py:450
  23.2 0.3 pack_z.1
  23.5 0.7 collective-permute-start.4
  24.2 5.1 %collective-permute-start.5 = (f32[5,8,128]{2,1,0:T(8,128)S(1)}, f32[5,8,128]{2,1,0:T(8,128)S(1)}, u32[]{:S(2)}, u32[]{:S(2)}) collective-permute-start(f32[5,8,128]{2,1,0:T(8,128)S(1)} %get-tuple-element.23), channel_id=1, source_target_pairs={{0,1},{2,3},{4,5},{6,7},{8,9},{10,11},{1,0},{3,2},{5,4},{7,6},{9,8... | collective-permute-start | bytes 61448 | tf_op jit(solution)/shard_map/ppermute | solution.py:450
  29.3 0.1 pad_maximum_fusion.flags
  29.3 1.4 %inner_lanes.1 = (f32[4,3,8,16,128]{4,3,2,1,0:T(8,128)S(1)}, f32[3,6,2,8,128]{4,3,2,1,0:T(8,128)S(1)}, f32[3,4,24,128]{3,2,1,0:T(8,128)S(1)}) custom-call(f32[8,128]{1,0:T(8,128)S(1)} %pad_maximum_fusion.flags, f32[3,16,24,128]{3,2,1,0:T(8,128)S(1)} %get-tuple-element.20.whole), custom_call_target="tpu_custom_call" | custom-call | tf_op jit(solution)/shard_map/inner_lanes/pallas_call | solution.py:431
  30.8 0.0 collective-permute-done.4.first
  30.8 0.0 collective-permute-done.5.second
  30.8 1.1 %edge_lanes.1 = (f32[4,3,4,16,128]{4,3,2,1,0:T(8,128)S(1)}, f32[64,128]{1,0:T(8,128)S(1)}) custom-call(f32[8,128]{1,0:T(8,128)S(1)} %pad_maximum_fusion.flags, f32[3,4,24,128]{3,2,1,0:T(8,128)S(1)} %get-tuple-element.21.edge, f32[5,8,128]{2,1,0:T(8,128)S(1)} %collective-permute-done.4.first, f32[5,8,128]{2,1,0:T(8,128)S(1)} %collective-permute-done.5.second, ...), custom_call_target="tpu_custom_call" | custom-call | tf_op jit(solution)/shard_map/edge_lanes/pallas_call | solution.py:431
  31.9 18.1 %all_to_all.22 = f32[64,1,128]{2,1,0:T(1,128)S(1)} all-to-all(f32[64,1,128]{2,1,0:T(1,128)S(1)} %bitcast.17), channel_id=1, replica_groups=mesh['gx_0'=2,'gx_1'=2,'gy_0'=4,'gy_1'=4,'gz'=12] {'gx_0','gx_1','gy_0',..., dimensions={0} | all-to-all | bytes 65536 | tf_op jit(solution)/shard_map/all_to_all | solution.py:454
  49.9 0.2 fold.1
  50.1 22.4 %all_to_all.23 = f32[12,1,128]{2,1,0:T(1,128)S(1)} all-to-all(f32[12,1,128]{2,1,0:T(1,128)S(1)} %copy.5), channel_id=1, replica_groups=mesh['gx_0'=2,'gx_1'=2,'gy_0'=4,'gy_1'=4,'gz'=12] {'gz'}, dimensions={0} | all-to-all | bytes 12288 | tf_op jit(solution)/shard_map/all_to_all | solution.py:454
  72.5 1.3 %combine.1 = (f32[3,8,16,128]{3,2,1,0:T(8,128)}, f32[3,8,16,128]{3,2,1,0:T(8,128)}) custom-call(f32[12,128]{1,0:T(8,128)S(1)} %bitcast.15, f32[8,128]{1,0:T(8,128)S(1)} %pad_maximum_fusion.flags, f32[4,3,8,16,128]{4,3,2,1,0:T(8,128)S(1)} %get-tuple-element.26.powers, f32[4,3,4,16,128]{4,3,2,1,0:T(8,128)S(1)} %get-tuple-element.27.edges), custom_call_target="tpu_custom_call" | custom-call | tf_op jit(solution)/shard_map/combine/pallas_call | solution.py:431
  (8 shorter events, 0.1 us)
Async XLA Ops:
  1.6 10.6 %collective-permute-start = (f32[3,4,8,128]{3,2,1,0:T(8,128)S(1)}, f32[3,4,8,128]{3,2,1,0:T(8,128)S(1)}, u32[]{:S(2)}, u32[]{:S(2)}) collective-permute-start(f32[3,4,8,128]{3,2,1,0:T(8,128)S(1)} %get-tuple-element.16), channel_id=1, source_target_pairs={{12,24},{36,48},{60,72},{84,96},{108,120},{132,144},{156,168},{24,... | collective-permute-start | bytes 147464 | tf_op jit(solution)/shard_map/ppermute | solution.py:450
  2.3 11.8 %collective-permute-start.1 = (f32[3,4,8,128]{3,2,1,0:T(8,128)S(1)}, f32[3,4,8,128]{3,2,1,0:T(8,128)S(1)}, u32[]{:S(2)}, u32[]{:S(2)}) collective-permute-start(f32[3,4,8,128]{3,2,1,0:T(8,128)S(1)} %get-tuple-element.17), channel_id=1, source_target_pairs={{0,12},{24,36},{48,60},{72,84},{96,108},{120,132},{144,156},{168,1... | collective-permute-start | bytes 147464 | tf_op jit(solution)/shard_map/ppermute | solution.py:450
  14.1 8.2 %copy-start = (f32[3]{0:T(128)S(1)}, f32[3]{0:T(128)}, u32[]{:S(2)}) copy-start(f32[3]{0:T(128)} %param.3) | copy-start | bytes 40
  14.1 8.2 %collective-permute-start.2 = (f32[3,11,8,128]{3,2,1,0:T(8,128)S(1)}, f32[3,11,8,128]{3,2,1,0:T(8,128)S(1)}, u32[]{:S(2)}, u32[]{:S(2)}) collective-permute-start(f32[3,11,8,128]{3,2,1,0:T(8,128)S(1)} %get-tuple-element.18), channel_id=1, source_target_pairs={{192,384},{384,192},{193,385},{385,193},{194,386},{386,194},{195,3... | collective-permute-start | bytes 405512 | tf_op jit(solution)/shard_map/ppermute | solution.py:450
  17.6 5.6 %collective-permute-start.3 = (f32[3,11,8,128]{3,2,1,0:T(8,128)S(1)}, f32[3,11,8,128]{3,2,1,0:T(8,128)S(1)}, u32[]{:S(2)}, u32[]{:S(2)}) collective-permute-start(f32[3,11,8,128]{3,2,1,0:T(8,128)S(1)} %get-tuple-element.19), channel_id=1, source_target_pairs={{0,192},{384,576},{192,0},{576,384},{1,193},{385,577},{193,1},{577... | collective-permute-start | bytes 405512 | tf_op jit(solution)/shard_map/ppermute | solution.py:450
  23.5 7.2 %collective-permute-start.4 = (f32[5,8,128]{2,1,0:T(8,128)S(1)}, f32[5,8,128]{2,1,0:T(8,128)S(1)}, u32[]{:S(2)}, u32[]{:S(2)}) collective-permute-start(f32[5,8,128]{2,1,0:T(8,128)S(1)} %get-tuple-element.22), channel_id=1, source_target_pairs={{1,2},{3,4},{5,6},{7,8},{9,10},{2,1},{4,3},{6,5},{8,7},{10,9},{13,... | collective-permute-start | bytes 61448 | tf_op jit(solution)/shard_map/ppermute | solution.py:450
  24.2 6.6 %collective-permute-start.5 = (f32[5,8,128]{2,1,0:T(8,128)S(1)}, f32[5,8,128]{2,1,0:T(8,128)S(1)}, u32[]{:S(2)}, u32[]{:S(2)}) collective-permute-start(f32[5,8,128]{2,1,0:T(8,128)S(1)} %get-tuple-element.23), channel_id=1, source_target_pairs={{0,1},{2,3},{4,5},{6,7},{8,9},{10,11},{1,0},{3,2},{5,4},{7,6},{9,8... | collective-permute-start | bytes 61448 | tf_op jit(solution)/shard_map/ppermute | solution.py:450

commit v10 on v9

--- a/solution.py
+++ b/solution.py
@@ -472,7 +472,7 @@
     edges, row = kernel(
         edge_lanes, [(ITERS + 1, 3, GROUPS, NY, NZ), (planes, NZ)], [tiles] * (ITERS + 1)
     )(flags, edge, first, second, sums)
-    (row,) = kernel(fold, [(stack, NZ)])(gathered(row, GX + GY))
+    (row,) = kernel(fold, [(stack, NZ)])(gathered(row, GY + GX))
     return kernel(combine, [block] * 2, last=True)(gathered(row, GZ), flags, powers, edges)
 
 

time: 74.1 us -> 74 us (level)
  no operation moved by 1% of the time
where the time goes in v10:
time: 74 us; the launch traced here: 73.7 us
  blocking collectives  40.4 us (55%)
  starting transfers between devices  24.3 us (33%)
  Pallas kernels  5.24 us (7%)
  waiting for transfers between devices  2.77 us (4%)
  between operations  0.79 us (1%)
    all_to_all x2, blocking collectives, gathered(): return lax.all_to_all(row, axes, 0, 0, tiled=True)  40.4 us
    ppermute x3, starting transfers between devices, swapped(): lax.ppermute(second, axis, pairs_from(0))  19.5 us
    pallas_call x7, Pallas kernels, call(): pl.pallas_call(body, in_specs=[vmem] * len(args), out_specs=[vmem] * len(...  5.24 us
    ppermute x3, starting transfers between devices, swapped(): lax.ppermute(first, axis, pairs_from(1))  4.81 us
    ppermute x3, waiting for transfers between devices, swapped(): lax.ppermute(second, axis, pairs_from(0))  2.77 us
  transfers between devices with their start and end apart: 6, of which 2 were waited for; matrix products, arithmetic and copies ran while one was open for 0% of the time, Pallas kernels for 2%

profile of v10, /device:TPU:1, one launch (start us, length us, event | category | flops | bytes accessed | tf_op | source)
XLA Modules:
  0.0 73.7 jit_solution(15311649387444427602)
XLA Ops:
  0.6 1.0 %pack_y.1 = (f32[3,8,16,128]{3,2,1,0:T(8,128)S(1)}, f32[3,4,8,128]{3,2,1,0:T(8,128)S(1)}, f32[3,4,8,128]{3,2,1,0:T(8,128)S(1)}) custom-call(f32[3,8,16,128]{3,2,1,0:T(8,128)} %block.1), custom_call_target="tpu_custom_call" | custom-call | tf_op jit(solution)/shard_map/pack_y/pallas_call | solution.py:431
  1.6 0.7 collective-permute-start
  2.3 9.8 %collective-permute-start.1 = (f32[3,4,8,128]{3,2,1,0:T(8,128)S(1)}, f32[3,4,8,128]{3,2,1,0:T(8,128)S(1)}, u32[]{:S(2)}, u32[]{:S(2)}) collective-permute-start(f32[3,4,8,128]{3,2,1,0:T(8,128)S(1)} %get-tuple-element.17), channel_id=1, source_target_pairs={{0,12},{24,36},{48,60},{72,84},{96,108},{120,132},{144,156},{168,1... | collective-permute-start | bytes 147464 | tf_op jit(solution)/shard_map/ppermute | solution.py:450
  12.1 0.1 stack.27
  12.2 0.0 collective-permute-done.first_y
  12.2 1.8 %collective-permute-done.1.second_y = f32[3,4,8,128]{3,2,1,0:T(8,128)S(1)} collective-permute-done((f32[3,4,8,128]{3,2,1,0:T(8,128)S(1)}, f32[3,4,8,128]{3,2,1,0:T(8,128)S(1)}, u32[]{:S(2)}, u32[]{:S(2)}) %collective-permute-start.1) | collective-permute-done | bytes 49184 | tf_op jit(solution)/shard_map/ppermute | solution.py:450
  14.1 0.0 copy-start
  14.1 3.5 %collective-permute-start.2 = (f32[3,11,8,128]{3,2,1,0:T(8,128)S(1)}, f32[3,11,8,128]{3,2,1,0:T(8,128)S(1)}, u32[]{:S(2)}, u32[]{:S(2)}) collective-permute-start(f32[3,11,8,128]{3,2,1,0:T(8,128)S(1)} %get-tuple-element.18), channel_id=1, source_target_pairs={{192,384},{384,192},{193,385},{385,193},{194,386},{386,194},{195,3... | collective-permute-start | bytes 405512 | tf_op jit(solution)/shard_map/ppermute | solution.py:450
  17.6 4.6 %collective-permute-start.3 = (f32[3,11,8,128]{3,2,1,0:T(8,128)S(1)}, f32[3,11,8,128]{3,2,1,0:T(8,128)S(1)}, u32[]{:S(2)}, u32[]{:S(2)}) collective-permute-start(f32[3,11,8,128]{3,2,1,0:T(8,128)S(1)} %get-tuple-element.19), channel_id=1, source_target_pairs={{0,192},{384,576},{192,0},{576,384},{1,193},{385,577},{193,1},{577... | collective-permute-start | bytes 405512 | tf_op jit(solution)/shard_map/ppermute | solution.py:450
  22.3 0.0 copy-done
  22.3 0.0 collective-permute-done.2.first_x
  22.3 0.9 %collective-permute-done.3.second_x = f32[3,11,8,128]{3,2,1,0:T(8,128)S(1)} collective-permute-done((f32[3,11,8,128]{3,2,1,0:T(8,128)S(1)}, f32[3,11,8,128]{3,2,1,0:T(8,128)S(1)}, u32[]{:S(2)}, u32[]{:S(2)}) %collective-permute-start.3) | collective-permute-done | bytes 135200 | tf_op jit(solution)/shard_map/ppermute | solution.py:450
  23.2 0.3 pack_z.1
  23.5 0.7 collective-permute-start.4
  24.2 5.1 %collective-permute-start.5 = (f32[5,8,128]{2,1,0:T(8,128)S(1)}, f32[5,8,128]{2,1,0:T(8,128)S(1)}, u32[]{:S(2)}, u32[]{:S(2)}) collective-permute-start(f32[5,8,128]{2,1,0:T(8,128)S(1)} %get-tuple-element.23), channel_id=1, source_target_pairs={{0,1},{2,3},{4,5},{6,7},{8,9},{10,11},{1,0},{3,2},{5,4},{7,6},{9,8... | collective-permute-start | bytes 61448 | tf_op jit(solution)/shard_map/ppermute | solution.py:450
  29.3 0.1 pad_maximum_fusion.flags
  29.3 1.4 %inner_lanes.1 = (f32[4,3,8,16,128]{4,3,2,1,0:T(8,128)S(1)}, f32[3,6,2,8,128]{4,3,2,1,0:T(8,128)S(1)}, f32[3,4,24,128]{3,2,1,0:T(8,128)S(1)}) custom-call(f32[8,128]{1,0:T(8,128)S(1)} %pad_maximum_fusion.flags, f32[3,16,24,128]{3,2,1,0:T(8,128)S(1)} %get-tuple-element.20.whole), custom_call_target="tpu_custom_call" | custom-call | tf_op jit(solution)/shard_map/inner_lanes/pallas_call | solution.py:431
  30.8 0.0 collective-permute-done.4.first
  30.8 0.0 collective-permute-done.5.second
  30.8 1.1 %edge_lanes.1 = (f32[4,3,4,16,128]{4,3,2,1,0:T(8,128)S(1)}, f32[64,128]{1,0:T(8,128)S(1)}) custom-call(f32[8,128]{1,0:T(8,128)S(1)} %pad_maximum_fusion.flags, f32[3,4,24,128]{3,2,1,0:T(8,128)S(1)} %get-tuple-element.21.edge, f32[5,8,128]{2,1,0:T(8,128)S(1)} %collective-permute-done.4.first, f32[5,8,128]{2,1,0:T(8,128)S(1)} %collective-permute-done.5.second, ...), custom_call_target="tpu_custom_call" | custom-call | tf_op jit(solution)/shard_map/edge_lanes/pallas_call | solution.py:431
  31.9 18.0 %all_to_all.22 = f32[64,1,128]{2,1,0:T(1,128)S(1)} all-to-all(f32[64,1,128]{2,1,0:T(1,128)S(1)} %bitcast.17), channel_id=1, replica_groups=mesh['gx_0'=2,'gx_1'=2,'gy_0'=4,'gy_1'=4,'gz'=12] {'gy_0','gy_1','gx_0',..., dimensions={0} | all-to-all | bytes 65536 | tf_op jit(solution)/shard_map/all_to_all | solution.py:454
  49.9 0.2 fold.1
  50.0 22.4 %all_to_all.23 = f32[12,1,128]{2,1,0:T(1,128)S(1)} all-to-all(f32[12,1,128]{2,1,0:T(1,128)S(1)} %copy.5), channel_id=1, replica_groups=mesh['gx_0'=2,'gx_1'=2,'gy_0'=4,'gy_1'=4,'gz'=12] {'gz'}, dimensions={0} | all-to-all | bytes 12288 | tf_op jit(solution)/shard_map/all_to_all | solution.py:454
  72.4 1.3 %combine.1 = (f32[3,8,16,128]{3,2,1,0:T(8,128)}, f32[3,8,16,128]{3,2,1,0:T(8,128)}) custom-call(f32[12,128]{1,0:T(8,128)S(1)} %bitcast.15, f32[8,128]{1,0:T(8,128)S(1)} %pad_maximum_fusion.flags, f32[4,3,8,16,128]{4,3,2,1,0:T(8,128)S(1)} %get-tuple-element.26.powers, f32[4,3,4,16,128]{4,3,2,1,0:T(8,128)S(1)} %get-tuple-element.27.edges), custom_call_target="tpu_custom_call" | custom-call | tf_op jit(solution)/shard_map/combine/pallas_call | solution.py:431
  (8 shorter events, 0.1 us)
Async XLA Ops:
  1.6 10.6 %collective-permute-start = (f32[3,4,8,128]{3,2,1,0:T(8,128)S(1)}, f32[3,4,8,128]{3,2,1,0:T(8,128)S(1)}, u32[]{:S(2)}, u32[]{:S(2)}) collective-permute-start(f32[3,4,8,128]{3,2,1,0:T(8,128)S(1)} %get-tuple-element.16), channel_id=1, source_target_pairs={{12,24},{36,48},{60,72},{84,96},{108,120},{132,144},{156,168},{24,... | collective-permute-start | bytes 147464 | tf_op jit(solution)/shard_map/ppermute | solution.py:450
  2.3 11.8 %collective-permute-start.1 = (f32[3,4,8,128]{3,2,1,0:T(8,128)S(1)}, f32[3,4,8,128]{3,2,1,0:T(8,128)S(1)}, u32[]{:S(2)}, u32[]{:S(2)}) collective-permute-start(f32[3,4,8,128]{3,2,1,0:T(8,128)S(1)} %get-tuple-element.17), channel_id=1, source_target_pairs={{0,12},{24,36},{48,60},{72,84},{96,108},{120,132},{144,156},{168,1... | collective-permute-start | bytes 147464 | tf_op jit(solution)/shard_map/ppermute | solution.py:450
  14.1 8.2 %copy-start = (f32[3]{0:T(128)S(1)}, f32[3]{0:T(128)}, u32[]{:S(2)}) copy-start(f32[3]{0:T(128)} %param.3) | copy-start | bytes 40
  14.1 8.2 %collective-permute-start.2 = (f32[3,11,8,128]{3,2,1,0:T(8,128)S(1)}, f32[3,11,8,128]{3,2,1,0:T(8,128)S(1)}, u32[]{:S(2)}, u32[]{:S(2)}) collective-permute-start(f32[3,11,8,128]{3,2,1,0:T(8,128)S(1)} %get-tuple-element.18), channel_id=1, source_target_pairs={{192,384},{384,192},{193,385},{385,193},{194,386},{386,194},{195,3... | collective-permute-start | bytes 405512 | tf_op jit(solution)/shard_map/ppermute | solution.py:450
  17.6 5.6 %collective-permute-start.3 = (f32[3,11,8,128]{3,2,1,0:T(8,128)S(1)}, f32[3,11,8,128]{3,2,1,0:T(8,128)S(1)}, u32[]{:S(2)}, u32[]{:S(2)}) collective-permute-start(f32[3,11,8,128]{3,2,1,0:T(8,128)S(1)} %get-tuple-element.19), channel_id=1, source_target_pairs={{0,192},{384,576},{192,0},{576,384},{1,193},{385,577},{193,1},{577... | collective-permute-start | bytes 405512 | tf_op jit(solution)/shard_map/ppermute | solution.py:450
  23.5 7.2 %collective-permute-start.4 = (f32[5,8,128]{2,1,0:T(8,128)S(1)}, f32[5,8,128]{2,1,0:T(8,128)S(1)}, u32[]{:S(2)}, u32[]{:S(2)}) collective-permute-start(f32[5,8,128]{2,1,0:T(8,128)S(1)} %get-tuple-element.22), channel_id=1, source_target_pairs={{1,2},{3,4},{5,6},{7,8},{9,10},{2,1},{4,3},{6,5},{8,7},{10,9},{13,... | collective-permute-start | bytes 61448 | tf_op jit(solution)/shard_map/ppermute | solution.py:450
  24.2 6.6 %collective-permute-start.5 = (f32[5,8,128]{2,1,0:T(8,128)S(1)}, f32[5,8,128]{2,1,0:T(8,128)S(1)}, u32[]{:S(2)}, u32[]{:S(2)}) collective-permute-start(f32[5,8,128]{2,1,0:T(8,128)S(1)} %get-tuple-element.23), channel_id=1, source_target_pairs={{0,1},{2,3},{4,5},{6,7},{8,9},{10,11},{1,0},{3,2},{5,4},{7,6},{9,8... | collective-permute-start | bytes 61448 | tf_op jit(solution)/shard_map/ppermute | solution.py:450

commit v11 on v9

--- a/solution.py
+++ b/solution.py
@@ -92,7 +92,7 @@
 
 
 def pack_z(own, first_y, second_y, first_x, second_x, whole, first, second):
-    odd_y, odd, odd_z = is_odd(GY), is_odd(GX), is_odd(GZ)
+    odd_y, odd, even_z = is_odd(GY), is_odd(GX), ~is_odd(GZ)
     lane = lanes((8, NZ))
     zero = jnp.zeros((8, NZ), jnp.float32)
 
@@ -128,8 +128,8 @@
         else:
             up = jnp.where(lane % 8 < HALO, early, turned(late, HALO))
             down = jnp.where(lane % 8 < HALO, turned(early, -HALO), late)
-        first[k] = jnp.where(odd_z, up, down)
-        second[k] = jnp.where(odd_z, down, up)
+        first[k] = jnp.where(even_z, up, down)
+        second[k] = jnp.where(even_z, down, up)
 
 
 def two_sum(a, b):
@@ -303,12 +303,12 @@
     inside = jnp.where(row >= NY + HALO, flags[2:3, :], jnp.where(row >= NY, flags[3:4, :], 1.0))
     inside *= jnp.where(group == 3, flags[0:1, :], jnp.where(group == 2, flags[1:2, :], 1.0))
     inside *= jnp.where(offset < 4, flags[4:5, :], jnp.where(offset >= 24, flags[5:6, :], 1.0))
-    odd = is_odd(GZ)
+    even = ~is_odd(GZ)
     lowest = lanes((8, NZ)) % STEP < 4
     highest = (lanes((8, NZ)) % STEP >= 24) & (lanes((8, NZ)) % STEP < 28)
     for k in range(Z_TILES):
-        low = jnp.where(odd, second[k], first[k])
-        high = jnp.where(odd, first[k], second[k])
+        low = jnp.where(even, second[k], first[k])
+        high = jnp.where(even, first[k], second[k])
         for half in range(2):
             c, t = divmod(2 * k + half, 3)
             part = slice(8 * t, 8 * t + 8)
@@ -440,14 +440,14 @@
     return call
 
 
-def swapped(first, second, axis):
+def swapped(first, second, axis, start=1):
     size = lax.axis_size(axis)
 
     def pairs_from(start):
         up = [(i, i + 1) for i in range(start, size - 1, 2)]
         return up + [(b, a) for a, b in up]
 
-    return lax.ppermute(first, axis, pairs_from(1)), lax.ppermute(second, axis, pairs_from(0))
+    return lax.ppermute(first, axis, pairs_from(start)), lax.ppermute(second, axis, pairs_from(1 - start))
 
 
 def gathered(row, axes):
@@ -464,7 +464,7 @@
     first, second = kernel(pack_x, [(3, 11, 8, NZ)] * 2)(own, *beside)
     beside += swapped(first, second, GX)
     whole, first, second = kernel(pack_z, [wide] + [(Z_TILES, 8, NZ)] * 2)(own, *beside)
-    first, second = swapped(first, second, GZ)
+    first, second = swapped(first, second, GZ, start=0)
     powers, sums, edge = kernel(
         inner_lanes, [(ITERS + 1,) + block, (3, MOMENTS, 2, 8, NZ), tiles], [wide] * ITERS
     )(flags, whole)

time: 74.1 us -> 74.1 us (level)
  starting transfers between devices: 24.3 us -> 21.2 us
  blocking collectives: 40.4 us -> 43.2 us
    ppermute x6, starting transfers between devices: 24.3 us -> 21.2 us  [the longest x3 15.1 us: swapped(): lax.ppermute(second, axis, pairs_from(1 - start))]
    all_to_all x2, blocking collectives: 40.4 us -> 43.2 us  [gathered(): return lax.all_to_all(row, axes, 0, 0, tiled=True)]
  transfers between devices with their start and end apart: 6 -> 6, of which waited for: 2 -> 3; matrix products, arithmetic and copies ran while one was open for 0% -> 0% of each run, Pallas kernels for 2% -> 2%
where the time goes in v11:
time: 74.1 us; the launch traced here: 73.8 us
  blocking collectives  43.2 us (58%)
  starting transfers between devices  21.2 us (29%)
  Pallas kernels  5.23 us (7%)
  waiting for transfers between devices  3.21 us (4%)
  between operations  0.78 us (1%)
    all_to_all x2, blocking collectives, gathered(): return lax.all_to_all(row, axes, 0, 0, tiled=True)  43.2 us
    ppermute x3, starting transfers between devices, swapped(): lax.ppermute(second, axis, pairs_from(1 - start))  15.1 us
    ppermute x3, starting transfers between devices, swapped(): lax.ppermute(first, axis, pairs_from(start))  6.07 us
    pallas_call x7, Pallas kernels, call(): pl.pallas_call(body, in_specs=[vmem] * len(args), out_specs=[vmem] * len(...  5.23 us
    ppermute x3, waiting for transfers between devices, swapped(): lax.ppermute(second, axis, pairs_from(1 - start))  2.77 us
  transfers between devices with their start and end apart: 6, of which 3 were waited for; matrix products, arithmetic and copies ran while one was open for 0% of the time, Pallas kernels for 2%

profile of v11, /device:TPU:1, one launch (start us, length us, event | category | flops | bytes accessed | tf_op | source)
XLA Modules:
  0.0 73.8 jit_solution(11204974765183969562)
XLA Ops:
  0.6 1.0 %pack_y.1 = (f32[3,8,16,128]{3,2,1,0:T(8,128)S(1)}, f32[3,4,8,128]{3,2,1,0:T(8,128)S(1)}, f32[3,4,8,128]{3,2,1,0:T(8,128)S(1)}) custom-call(f32[3,8,16,128]{3,2,1,0:T(8,128)} %block.1), custom_call_target="tpu_custom_call" | custom-call | tf_op jit(solution)/shard_map/pack_y/pallas_call | solution.py:431
  1.6 0.7 collective-permute-start
  2.3 9.8 %collective-permute-start.1 = (f32[3,4,8,128]{3,2,1,0:T(8,128)S(1)}, f32[3,4,8,128]{3,2,1,0:T(8,128)S(1)}, u32[]{:S(2)}, u32[]{:S(2)}) collective-permute-start(f32[3,4,8,128]{3,2,1,0:T(8,128)S(1)} %get-tuple-element.17), channel_id=1, source_target_pairs={{0,12},{24,36},{48,60},{72,84},{96,108},{120,132},{144,156},{168,1... | collective-permute-start | bytes 147464 | tf_op jit(solution)/shard_map/ppermute | solution.py:450
  12.1 0.1 stack.27
  12.2 0.0 collective-permute-done.first_y
  12.2 1.8 %collective-permute-done.1.second_y = f32[3,4,8,128]{3,2,1,0:T(8,128)S(1)} collective-permute-done((f32[3,4,8,128]{3,2,1,0:T(8,128)S(1)}, f32[3,4,8,128]{3,2,1,0:T(8,128)S(1)}, u32[]{:S(2)}, u32[]{:S(2)}) %collective-permute-start.1) | collective-permute-done | bytes 49184 | tf_op jit(solution)/shard_map/ppermute | solution.py:450
  14.1 0.0 copy-start
  14.1 3.5 %collective-permute-start.2 = (f32[3,11,8,128]{3,2,1,0:T(8,128)S(1)}, f32[3,11,8,128]{3,2,1,0:T(8,128)S(1)}, u32[]{:S(2)}, u32[]{:S(2)}) collective-permute-start(f32[3,11,8,128]{3,2,1,0:T(8,128)S(1)} %get-tuple-element.18), channel_id=1, source_target_pairs={{192,384},{384,192},{193,385},{385,193},{194,386},{386,194},{195,3... | collective-permute-start | bytes 405512 | tf_op jit(solution)/shard_map/ppermute | solution.py:450
  17.6 4.6 %collective-permute-start.3 = (f32[3,11,8,128]{3,2,1,0:T(8,128)S(1)}, f32[3,11,8,128]{3,2,1,0:T(8,128)S(1)}, u32[]{:S(2)}, u32[]{:S(2)}) collective-permute-start(f32[3,11,8,128]{3,2,1,0:T(8,128)S(1)} %get-tuple-element.19), channel_id=1, source_target_pairs={{0,192},{384,576},{192,0},{576,384},{1,193},{385,577},{193,1},{577... | collective-permute-start | bytes 405512 | tf_op jit(solution)/shard_map/ppermute | solution.py:450
  22.3 0.0 copy-done
  22.3 0.0 collective-permute-done.2.first_x
  22.3 0.9 %collective-permute-done.3.second_x = f32[3,11,8,128]{3,2,1,0:T(8,128)S(1)} collective-permute-done((f32[3,11,8,128]{3,2,1,0:T(8,128)S(1)}, f32[3,11,8,128]{3,2,1,0:T(8,128)S(1)}, u32[]{:S(2)}, u32[]{:S(2)}) %collective-permute-start.3) | collective-permute-done | bytes 135200 | tf_op jit(solution)/shard_map/ppermute | solution.py:450
  23.2 0.3 pack_z.1
  23.5 1.9 %collective-permute-start.4 = (f32[5,8,128]{2,1,0:T(8,128)S(1)}, f32[5,8,128]{2,1,0:T(8,128)S(1)}, u32[]{:S(2)}, u32[]{:S(2)}) collective-permute-start(f32[5,8,128]{2,1,0:T(8,128)S(1)} %get-tuple-element.22), channel_id=1, source_target_pairs={{0,1},{2,3},{4,5},{6,7},{8,9},{10,11},{1,0},{3,2},{5,4},{7,6},{9,8... | collective-permute-start | bytes 61448 | tf_op jit(solution)/shard_map/ppermute | solution.py:450
  25.5 0.7 collective-permute-start.5
  26.1 0.1 pad_maximum_fusion.flags
  26.2 1.4 %inner_lanes.1 = (f32[4,3,8,16,128]{4,3,2,1,0:T(8,128)S(1)}, f32[3,6,2,8,128]{4,3,2,1,0:T(8,128)S(1)}, f32[3,4,24,128]{3,2,1,0:T(8,128)S(1)}) custom-call(f32[8,128]{1,0:T(8,128)S(1)} %pad_maximum_fusion.flags, f32[3,16,24,128]{3,2,1,0:T(8,128)S(1)} %get-tuple-element.20.whole), custom_call_target="tpu_custom_call" | custom-call | tf_op jit(solution)/shard_map/inner_lanes/pallas_call | solution.py:431
  27.6 0.4 collective-permute-done.4.first
  28.1 0.0 collective-permute-done.5.second
  28.1 1.1 %edge_lanes.1 = (f32[4,3,4,16,128]{4,3,2,1,0:T(8,128)S(1)}, f32[64,128]{1,0:T(8,128)S(1)}) custom-call(f32[8,128]{1,0:T(8,128)S(1)} %pad_maximum_fusion.flags, f32[3,4,24,128]{3,2,1,0:T(8,128)S(1)} %get-tuple-element.21.edge, f32[5,8,128]{2,1,0:T(8,128)S(1)} %collective-permute-done.4.first, f32[5,8,128]{2,1,0:T(8,128)S(1)} %collective-permute-done.5.second, ...), custom_call_target="tpu_custom_call" | custom-call | tf_op jit(solution)/shard_map/edge_lanes/pallas_call | solution.py:431
  29.1 16.9 %all_to_all.22 = f32[64,1,128]{2,1,0:T(1,128)S(1)} all-to-all(f32[64,1,128]{2,1,0:T(1,128)S(1)} %bitcast.17), channel_id=1, replica_groups=mesh['gx_0'=2,'gx_1'=2,'gy_0'=4,'gy_1'=4,'gz'=12] {'gx_0','gx_1','gy_0',..., dimensions={0} | all-to-all | bytes 65536 | tf_op jit(solution)/shard_map/all_to_all | solution.py:454
  46.1 0.2 fold.1
  46.2 26.2 %all_to_all.23 = f32[12,1,128]{2,1,0:T(1,128)S(1)} all-to-all(f32[12,1,128]{2,1,0:T(1,128)S(1)} %copy.5), channel_id=1, replica_groups=mesh['gx_0'=2,'gx_1'=2,'gy_0'=4,'gy_1'=4,'gz'=12] {'gz'}, dimensions={0} | all-to-all | bytes 12288 | tf_op jit(solution)/shard_map/all_to_all | solution.py:454
  72.5 1.3 %combine.1 = (f32[3,8,16,128]{3,2,1,0:T(8,128)}, f32[3,8,16,128]{3,2,1,0:T(8,128)}) custom-call(f32[12,128]{1,0:T(8,128)S(1)} %bitcast.15, f32[8,128]{1,0:T(8,128)S(1)} %pad_maximum_fusion.flags, f32[4,3,8,16,128]{4,3,2,1,0:T(8,128)S(1)} %get-tuple-element.26.powers, f32[4,3,4,16,128]{4,3,2,1,0:T(8,128)S(1)} %get-tuple-element.27.edges), custom_call_target="tpu_custom_call" | custom-call | tf_op jit(solution)/shard_map/combine/pallas_call | solution.py:431
  (8 shorter events, 0.1 us)
Async XLA Ops:
  1.6 10.6 %collective-permute-start = (f32[3,4,8,128]{3,2,1,0:T(8,128)S(1)}, f32[3,4,8,128]{3,2,1,0:T(8,128)S(1)}, u32[]{:S(2)}, u32[]{:S(2)}) collective-permute-start(f32[3,4,8,128]{3,2,1,0:T(8,128)S(1)} %get-tuple-element.16), channel_id=1, source_target_pairs={{12,24},{36,48},{60,72},{84,96},{108,120},{132,144},{156,168},{24,... | collective-permute-start | bytes 147464 | tf_op jit(solution)/shard_map/ppermute | solution.py:450
  2.3 11.8 %collective-permute-start.1 = (f32[3,4,8,128]{3,2,1,0:T(8,128)S(1)}, f32[3,4,8,128]{3,2,1,0:T(8,128)S(1)}, u32[]{:S(2)}, u32[]{:S(2)}) collective-permute-start(f32[3,4,8,128]{3,2,1,0:T(8,128)S(1)} %get-tuple-element.17), channel_id=1, source_target_pairs={{0,12},{24,36},{48,60},{72,84},{96,108},{120,132},{144,156},{168,1... | collective-permute-start | bytes 147464 | tf_op jit(solution)/shard_map/ppermute | solution.py:450
  14.1 8.2 %copy-start = (f32[3]{0:T(128)S(1)}, f32[3]{0:T(128)}, u32[]{:S(2)}) copy-start(f32[3]{0:T(128)} %param.3) | copy-start | bytes 40
  14.1 8.2 %collective-permute-start.2 = (f32[3,11,8,128]{3,2,1,0:T(8,128)S(1)}, f32[3,11,8,128]{3,2,1,0:T(8,128)S(1)}, u32[]{:S(2)}, u32[]{:S(2)}) collective-permute-start(f32[3,11,8,128]{3,2,1,0:T(8,128)S(1)} %get-tuple-element.18), channel_id=1, source_target_pairs={{192,384},{384,192},{193,385},{385,193},{194,386},{386,194},{195,3... | collective-permute-start | bytes 405512 | tf_op jit(solution)/shard_map/ppermute | solution.py:450
  17.6 5.6 %collective-permute-start.3 = (f32[3,11,8,128]{3,2,1,0:T(8,128)S(1)}, f32[3,11,8,128]{3,2,1,0:T(8,128)S(1)}, u32[]{:S(2)}, u32[]{:S(2)}) collective-permute-start(f32[3,11,8,128]{3,2,1,0:T(8,128)S(1)} %get-tuple-element.19), channel_id=1, source_target_pairs={{0,192},{384,576},{192,0},{576,384},{1,193},{385,577},{193,1},{577... | collective-permute-start | bytes 405512 | tf_op jit(solution)/shard_map/ppermute | solution.py:450
  23.5 4.5 %collective-permute-start.4 = (f32[5,8,128]{2,1,0:T(8,128)S(1)}, f32[5,8,128]{2,1,0:T(8,128)S(1)}, u32[]{:S(2)}, u32[]{:S(2)}) collective-permute-start(f32[5,8,128]{2,1,0:T(8,128)S(1)} %get-tuple-element.22), channel_id=1, source_target_pairs={{0,1},{2,3},{4,5},{6,7},{8,9},{10,11},{1,0},{3,2},{5,4},{7,6},{9,8... | collective-permute-start | bytes 61448 | tf_op jit(solution)/shard_map/ppermute | solution.py:450
  25.5 2.6 %collective-permute-start.5 = (f32[5,8,128]{2,1,0:T(8,128)S(1)}, f32[5,8,128]{2,1,0:T(8,128)S(1)}, u32[]{:S(2)}, u32[]{:S(2)}) collective-permute-start(f32[5,8,128]{2,1,0:T(8,128)S(1)} %get-tuple-element.23), channel_id=1, source_target_pairs={{1,2},{3,4},{5,6},{7,8},{9,10},{2,1},{4,3},{6,5},{8,7},{10,9},{13,... | collective-permute-start | bytes 61448 | tf_op jit(solution)/shard_map/ppermute | solution.py:450

commit v12 on v11

--- a/solution.py
+++ b/solution.py
@@ -50,20 +50,20 @@
 
 
 def pack_y(block, own, first, second):
-    odd = is_odd(GY)
+    even = ~is_odd(GY)
     sub = rows((8, NZ))
     own[...] = block[...]
     for c in range(3):
         for q in range(4):
             up = jnp.where(sub >= 4, block[c, q, 8:16, :], pltpu.roll(block[c, q + 4, 8:16, :], 4, 0))
             down = jnp.where(sub < 4, block[c, q, 0:8, :], pltpu.roll(block[c, q + 4, 0:8, :], 4, 0))
-            first[c, q] = jnp.where(odd, up, down)
-            second[c, q] = jnp.where(odd, down, up)
-
-
-def beside_y(odd, first, second, c, x):
-    low = jnp.where(odd, second[c, x % 4], first[c, x % 4])
-    high = jnp.where(odd, first[c, x % 4], second[c, x % 4])
+            first[c, q] = jnp.where(even, up, down)
+            second[c, q] = jnp.where(even, down, up)
+
+
+def beside_y(even, first, second, c, x):
+    low = jnp.where(even, second[c, x % 4], first[c, x % 4])
+    high = jnp.where(even, first[c, x % 4], second[c, x % 4])
     sub = rows((8, NZ))
     if x < 4:
         return jnp.where(sub < 4, high, low)
@@ -71,7 +71,7 @@
 
 
 def pack_x(own, first_y, second_y, first, second):
-    odd_y, odd = is_odd(GY), is_odd(GX)
+    even_y, odd = ~is_odd(GY), is_odd(GX)
 
     def put(c, n, up, down):
         first[c, n] = jnp.where(odd, up, down)
@@ -86,19 +86,19 @@
             put(
                 c,
                 8 + n,
-                beside_y(odd_y, first_y, second_y, c, NX - HALO + 1 + n),
-                beside_y(odd_y, first_y, second_y, c, n),
+                beside_y(even_y, first_y, second_y, c, NX - HALO + 1 + n),
+                beside_y(even_y, first_y, second_y, c, n),
             )
 
 
 def pack_z(own, first_y, second_y, first_x, second_x, whole, first, second):
-    odd_y, odd, even_z = is_odd(GY), is_odd(GX), ~is_odd(GZ)
+    even_y, odd, even_z = ~is_odd(GY), is_odd(GX), ~is_odd(GZ)
     lane = lanes((8, NZ))
     zero = jnp.zeros((8, NZ), jnp.float32)
 
     def tile_of(c, i, t):
         if i < NX:
-            return own[c, i, 8 * t : 8 * t + 8, :] if t < 2 else beside_y(odd_y, first_y, second_y, c, i)
+            return own[c, i, 8 * t : 8 * t + 8, :] if t < 2 else beside_y(even_y, first_y, second_y, c, i)
         n = i - NX
         if n < HALO:
             if t == 2 and n == HALO - 1:
@@ -460,7 +460,7 @@
     flags = jnp.concatenate([flags, jnp.broadcast_to(jnp.pad(6.0 * diffusion, (0, NZ - 3))[None], (2, NZ))])
     block, wide, tiles = (3, NX, NY, NZ), (3, EX, EY, NZ), (3, GROUPS, EY, NZ)
     own, first, second = kernel(pack_y, [block] + [(3, 4, 8, NZ)] * 2, first=True)(velocity)
-    beside = swapped(first, second, GY)
+    beside = swapped(first, second, GY, start=0)
     first, second = kernel(pack_x, [(3, 11, 8, NZ)] * 2)(own, *beside)
     beside += swapped(first, second, GX)
     whole, first, second = kernel(pack_z, [wide] + [(Z_TILES, 8, NZ)] * 2)(own, *beside)

time: 74.1 us -> 75.4 us (1.018)
  blocking collectives: 43.2 us -> 45.1 us
  waiting for transfers between devices: 3.21 us -> 2.01 us
    ppermute x3, starting transfers between devices: 6.07 us -> 11.9 us  [swapped(): lax.ppermute(first, axis, pairs_from(start))]
    ppermute x3, starting transfers between devices: 15.1 us -> 9.8 us  [swapped(): lax.ppermute(second, axis, pairs_from(1 - start))]
    all_to_all x2, blocking collectives: 43.2 us -> 45.1 us  [gathered(): return lax.all_to_all(row, axes, 0, 0, tiled=True)]
    ppermute x3, waiting for transfers between devices: 2.77 us -> 0.93 us  [swapped(): lax.ppermute(second, axis, pairs_from(1 - start))]
where the time goes in v12:
time: 75.4 us; the launch traced here: 75 us
  blocking collectives  45.1 us (60%)
  starting transfers between devices  21.7 us (29%)
  Pallas kernels  5.23 us (7%)
  waiting for transfers between devices  2.01 us (3%)
  between operations  0.78 us (1%)
    all_to_all x2, blocking collectives, gathered(): return lax.all_to_all(row, axes, 0, 0, tiled=True)  45.1 us
    ppermute x3, starting transfers between devices, swapped(): lax.ppermute(first, axis, pairs_from(start))  11.9 us
    ppermute x3, starting transfers between devices, swapped(): lax.ppermute(second, axis, pairs_from(1 - start))  9.8 us
    pallas_call x7, Pallas kernels, call(): pl.pallas_call(body, in_specs=[vmem] * len(args), out_specs=[vmem] * len(...  5.23 us
  transfers between devices with their start and end apart: 6, of which 3 were waited for; matrix products, arithmetic and copies ran while one was open for 0% of the time, Pallas kernels for 2%

profile of v12, /device:TPU:1, one launch (start us, length us, event | category | flops | bytes accessed | tf_op | source)
XLA Modules:
  0.0 75.0 jit_solution(10036110984079183256)
XLA Ops:
  0.6 1.0 %pack_y.1 = (f32[3,8,16,128]{3,2,1,0:T(8,128)S(1)}, f32[3,4,8,128]{3,2,1,0:T(8,128)S(1)}, f32[3,4,8,128]{3,2,1,0:T(8,128)S(1)}) custom-call(f32[3,8,16,128]{3,2,1,0:T(8,128)} %block.1), custom_call_target="tpu_custom_call" | custom-call | tf_op jit(solution)/shard_map/pack_y/pallas_call | solution.py:431
  1.6 5.0 %collective-permute-start = (f32[3,4,8,128]{3,2,1,0:T(8,128)S(1)}, f32[3,4,8,128]{3,2,1,0:T(8,128)S(1)}, u32[]{:S(2)}, u32[]{:S(2)}) collective-permute-start(f32[3,4,8,128]{3,2,1,0:T(8,128)S(1)} %get-tuple-element.16), channel_id=1, source_target_pairs={{0,12},{24,36},{48,60},{72,84},{96,108},{120,132},{144,156},{168,1... | collective-permute-start | bytes 147464 | tf_op jit(solution)/shard_map/ppermute | solution.py:450
  6.6 0.7 collective-permute-start.1
  7.3 0.1 stack.27
  7.5 0.6 collective-permute-done.first_y
  8.1 0.0 collective-permute-done.1.second_y
  8.1 0.0 copy-start
  8.2 5.0 %collective-permute-start.2 = (f32[3,11,8,128]{3,2,1,0:T(8,128)S(1)}, f32[3,11,8,128]{3,2,1,0:T(8,128)S(1)}, u32[]{:S(2)}, u32[]{:S(2)}) collective-permute-start(f32[3,11,8,128]{3,2,1,0:T(8,128)S(1)} %get-tuple-element.18), channel_id=1, source_target_pairs={{192,384},{384,192},{193,385},{385,193},{194,386},{386,194},{195,3... | collective-permute-start | bytes 405512 | tf_op jit(solution)/shard_map/ppermute | solution.py:450
  13.1 8.5 %collective-permute-start.3 = (f32[3,11,8,128]{3,2,1,0:T(8,128)S(1)}, f32[3,11,8,128]{3,2,1,0:T(8,128)S(1)}, u32[]{:S(2)}, u32[]{:S(2)}) collective-permute-start(f32[3,11,8,128]{3,2,1,0:T(8,128)S(1)} %get-tuple-element.19), channel_id=1, source_target_pairs={{0,192},{384,576},{192,0},{576,384},{1,193},{385,577},{193,1},{577... | collective-permute-start | bytes 405512 | tf_op jit(solution)/shard_map/ppermute | solution.py:450
  21.6 0.0 copy-done
  21.6 0.0 collective-permute-done.2.first_x
  21.6 0.9 %collective-permute-done.3.second_x = f32[3,11,8,128]{3,2,1,0:T(8,128)S(1)} collective-permute-done((f32[3,11,8,128]{3,2,1,0:T(8,128)S(1)}, f32[3,11,8,128]{3,2,1,0:T(8,128)S(1)}, u32[]{:S(2)}, u32[]{:S(2)}) %collective-permute-start.3) | collective-permute-done | bytes 135200 | tf_op jit(solution)/shard_map/ppermute | solution.py:450
  22.6 0.3 pack_z.1
  22.9 1.9 %collective-permute-start.4 = (f32[5,8,128]{2,1,0:T(8,128)S(1)}, f32[5,8,128]{2,1,0:T(8,128)S(1)}, u32[]{:S(2)}, u32[]{:S(2)}) collective-permute-start(f32[5,8,128]{2,1,0:T(8,128)S(1)} %get-tuple-element.22), channel_id=1, source_target_pairs={{0,1},{2,3},{4,5},{6,7},{8,9},{10,11},{1,0},{3,2},{5,4},{7,6},{9,8... | collective-permute-start | bytes 61448 | tf_op jit(solution)/shard_map/ppermute | solution.py:450
  24.8 0.7 collective-permute-start.5
  25.5 0.1 pad_maximum_fusion.flags
  25.5 1.4 %inner_lanes.1 = (f32[4,3,8,16,128]{4,3,2,1,0:T(8,128)S(1)}, f32[3,6,2,8,128]{4,3,2,1,0:T(8,128)S(1)}, f32[3,4,24,128]{3,2,1,0:T(8,128)S(1)}) custom-call(f32[8,128]{1,0:T(8,128)S(1)} %pad_maximum_fusion.flags, f32[3,16,24,128]{3,2,1,0:T(8,128)S(1)} %get-tuple-element.20.whole), custom_call_target="tpu_custom_call" | custom-call | tf_op jit(solution)/shard_map/inner_lanes/pallas_call | solution.py:431
  26.9 0.4 collective-permute-done.4.first
  27.4 0.0 collective-permute-done.5.second
  27.4 1.1 %edge_lanes.1 = (f32[4,3,4,16,128]{4,3,2,1,0:T(8,128)S(1)}, f32[64,128]{1,0:T(8,128)S(1)}) custom-call(f32[8,128]{1,0:T(8,128)S(1)} %pad_maximum_fusion.flags, f32[3,4,24,128]{3,2,1,0:T(8,128)S(1)} %get-tuple-element.21.edge, f32[5,8,128]{2,1,0:T(8,128)S(1)} %collective-permute-done.4.first, f32[5,8,128]{2,1,0:T(8,128)S(1)} %collective-permute-done.5.second, ...), custom_call_target="tpu_custom_call" | custom-call | tf_op jit(solution)/shard_map/edge_lanes/pallas_call | solution.py:431
  28.5 18.9 %all_to_all.22 = f32[64,1,128]{2,1,0:T(1,128)S(1)} all-to-all(f32[64,1,128]{2,1,0:T(1,128)S(1)} %bitcast.17), channel_id=1, replica_groups=mesh['gx_0'=2,'gx_1'=2,'gy_0'=4,'gy_1'=4,'gz'=12] {'gx_0','gx_1','gy_0',..., dimensions={0} | all-to-all | bytes 65536 | tf_op jit(solution)/shard_map/all_to_all | solution.py:454
  47.3 0.2 fold.1
  47.5 26.2 %all_to_all.23 = f32[12,1,128]{2,1,0:T(1,128)S(1)} all-to-all(f32[12,1,128]{2,1,0:T(1,128)S(1)} %copy.5), channel_id=1, replica_groups=mesh['gx_0'=2,'gx_1'=2,'gy_0'=4,'gy_1'=4,'gz'=12] {'gz'}, dimensions={0} | all-to-all | bytes 12288 | tf_op jit(solution)/shard_map/all_to_all | solution.py:454
  73.7 1.3 %combine.1 = (f32[3,8,16,128]{3,2,1,0:T(8,128)}, f32[3,8,16,128]{3,2,1,0:T(8,128)}) custom-call(f32[12,128]{1,0:T(8,128)S(1)} %bitcast.15, f32[8,128]{1,0:T(8,128)S(1)} %pad_maximum_fusion.flags, f32[4,3,8,16,128]{4,3,2,1,0:T(8,128)S(1)} %get-tuple-element.26.powers, f32[4,3,4,16,128]{4,3,2,1,0:T(8,128)S(1)} %get-tuple-element.27.edges), custom_call_target="tpu_custom_call" | custom-call | tf_op jit(solution)/shard_map/combine/pallas_call | solution.py:431
  (8 shorter events, 0.1 us)
Async XLA Ops:
  1.6 6.5 %collective-permute-start = (f32[3,4,8,128]{3,2,1,0:T(8,128)S(1)}, f32[3,4,8,128]{3,2,1,0:T(8,128)S(1)}, u32[]{:S(2)}, u32[]{:S(2)}) collective-permute-start(f32[3,4,8,128]{3,2,1,0:T(8,128)S(1)} %get-tuple-element.16), channel_id=1, source_target_pairs={{0,12},{24,36},{48,60},{72,84},{96,108},{120,132},{144,156},{168,1... | collective-permute-start | bytes 147464 | tf_op jit(solution)/shard_map/ppermute | solution.py:450
  6.6 1.5 %collective-permute-start.1 = (f32[3,4,8,128]{3,2,1,0:T(8,128)S(1)}, f32[3,4,8,128]{3,2,1,0:T(8,128)S(1)}, u32[]{:S(2)}, u32[]{:S(2)}) collective-permute-start(f32[3,4,8,128]{3,2,1,0:T(8,128)S(1)} %get-tuple-element.17), channel_id=1, source_target_pairs={{12,24},{36,48},{60,72},{84,96},{108,120},{132,144},{156,168},{24,... | collective-permute-start | bytes 147464 | tf_op jit(solution)/shard_map/ppermute | solution.py:450
  8.1 13.5 %copy-start = (f32[3]{0:T(128)S(1)}, f32[3]{0:T(128)}, u32[]{:S(2)}) copy-start(f32[3]{0:T(128)} %param.3) | copy-start | bytes 40
  8.2 13.5 %collective-permute-start.2 = (f32[3,11,8,128]{3,2,1,0:T(8,128)S(1)}, f32[3,11,8,128]{3,2,1,0:T(8,128)S(1)}, u32[]{:S(2)}, u32[]{:S(2)}) collective-permute-start(f32[3,11,8,128]{3,2,1,0:T(8,128)S(1)} %get-tuple-element.18), channel_id=1, source_target_pairs={{192,384},{384,192},{193,385},{385,193},{194,386},{386,194},{195,3... | collective-permute-start | bytes 405512 | tf_op jit(solution)/shard_map/ppermute | solution.py:450
  13.1 9.4 %collective-permute-start.3 = (f32[3,11,8,128]{3,2,1,0:T(8,128)S(1)}, f32[3,11,8,128]{3,2,1,0:T(8,128)S(1)}, u32[]{:S(2)}, u32[]{:S(2)}) collective-permute-start(f32[3,11,8,128]{3,2,1,0:T(8,128)S(1)} %get-tuple-element.19), channel_id=1, source_target_pairs={{0,192},{384,576},{192,0},{576,384},{1,193},{385,577},{193,1},{577... | collective-permute-start | bytes 405512 | tf_op jit(solution)/shard_map/ppermute | solution.py:450
  22.9 4.5 %collective-permute-start.4 = (f32[5,8,128]{2,1,0:T(8,128)S(1)}, f32[5,8,128]{2,1,0:T(8,128)S(1)}, u32[]{:S(2)}, u32[]{:S(2)}) collective-permute-start(f32[5,8,128]{2,1,0:T(8,128)S(1)} %get-tuple-element.22), channel_id=1, source_target_pairs={{0,1},{2,3},{4,5},{6,7},{8,9},{10,11},{1,0},{3,2},{5,4},{7,6},{9,8... | collective-permute-start | bytes 61448 | tf_op jit(solution)/shard_map/ppermute | solution.py:450
  24.8 2.6 %collective-permute-start.5 = (f32[5,8,128]{2,1,0:T(8,128)S(1)}, f32[5,8,128]{2,1,0:T(8,128)S(1)}, u32[]{:S(2)}, u32[]{:S(2)}) collective-permute-start(f32[5,8,128]{2,1,0:T(8,128)S(1)} %get-tuple-element.23), channel_id=1, source_target_pairs={{1,2},{3,4},{5,6},{7,8},{9,10},{2,1},{4,3},{6,5},{8,7},{10,9},{13,... | collective-permute-start | bytes 61448 | tf_op jit(solution)/shard_map/ppermute | solution.py:450
